TPU v7x, 32 devices: a whole 2x2x4 slice. The times are simulated.
32 devices in a mesh: dp: 8 (over y, x, core), tensor: 4 (over z).
Axes of the slice: x: 2, y: 2, z: 4, core: 2. Of those that a mesh axis runs over, the one named last changes fastest.
Arguments:
- inputs: bfloat16 [16384, 768], P(('dp', 'tensor')), may hold values from -6 to 6
- cotangent: bfloat16 [16384, 768], P(('dp', 'tensor')), may hold values from -6 to 6
- attn_w: float32 [3, 768, 768], P(None, 'dp', 'tensor'), may hold values from -2 to 2
- out_w: float32 [768, 768], P('tensor', 'dp'), may hold values from -2 to 2
- glu_w: float32 [2, 768, 3072], P(None, 'dp', 'tensor'), may hold values from -2 to 2
- down_w: float32 [3072, 768], P('tensor', 'dp'), may hold values from -2 to 2
- qv_bias: float32 [2, 768], P(None, ('tensor', 'dp')), may hold values from -3 to 3
- vectors: float32 [6, 768], P(None, 'dp'), may hold values from -2 to 2, as said below
- attn_mom: float32 [2, 3, 768, 768], P(None, None, 'dp', 'tensor'), as said below
- out_mom: float32 [2, 768, 768], P(None, 'tensor', 'dp'), as said below
- glu_mom: float32 [2, 2, 768, 3072], P(None, None, 'dp', 'tensor'), as said below
- down_mom: float32 [2, 3072, 768], P(None, 'tensor', 'dp'), as said below
- qv_mom: float32 [2, 2, 768], P(None, None, ('tensor', 'dp')), as said below
- vector_mom: float32 [2, 6, 768], P(None, None, ('dp', 'tensor')), as said below
Outputs:
- output: bfloat16 [16384, 768], P(('dp', 'tensor'))
- input_grad: float32 [16384, 768], P(('dp', 'tensor'))
- attn_grad: float32 [3, 768, 768], P(None, 'dp', 'tensor')
- out_grad: float32 [768, 768], P('tensor', 'dp')
- glu_grad: float32 [2, 768, 3072], P(None, 'dp', 'tensor')
- down_grad: float32 [3072, 768], P('tensor', 'dp')
- qv_grad: float32 [2, 768], P(None, ('tensor', 'dp'))
- vector_grad: float32 [6, 768], P(None, ('dp', 'tensor'))
- attn_mom_new: float32 [2, 3, 768, 768], P(None, None, 'dp', 'tensor')
- out_mom_new: float32 [2, 768, 768], P(None, 'tensor', 'dp')
- glu_mom_new: float32 [2, 2, 768, 3072], P(None, None, 'dp', 'tensor')
- down_mom_new: float32 [2, 3072, 768], P(None, 'tensor', 'dp')
- qv_mom_new: float32 [2, 2, 768], P(None, None, ('tensor', 'dp'))
- vector_mom_new: float32 [2, 6, 768], P(None, None, ('dp', 'tensor'))
- attn_new: float32 [3, 768, 768], P(None, 'dp', 'tensor')
- out_new: float32 [768, 768], P('tensor', 'dp')
- glu_new: float32 [2, 768, 3072], P(None, 'dp', 'tensor')
- down_new: float32 [3072, 768], P('tensor', 'dp')
- qv_new: float32 [2, 768], P(None, ('tensor', 'dp'))
- vector_new: float32 [6, 768], P(None, ('dp', 'tensor'))
- norm_values: float32 [2, 15], replicated
- ratios: float32 [15], replicated
Inputs may be any that keep to these rules, and one draw needn't show every extreme that they name: `vectors`: rows 1 and 4 (the norms' gains) lie within 0.2 to 1.8, the other rows within -2 to 2. `attn_mom`: index 0 of the leading dimension holds first moments, index 1 root mean squares of gradients, which are positive. `out_mom`: index 0 of the leading dimension holds first moments, index 1 root mean squares of gradients, which are positive. `glu_mom`: index 0 of the leading dimension holds first moments, index 1 root mean squares of gradients, which are positive. `down_mom`: index 0 of the leading dimension holds first moments, index 1 root mean squares of gradients, which are positive. `qv_mom`: index 0 of the leading dimension holds first moments, index 1 root mean squares of gradients, which are positive. `vector_mom`: index 0 of the leading dimension holds first moments, index 1 root mean squares of gradients, which are positive.
All inputs are finite; a program needn't handle non-finite values.
Results may differ from a plain program's by a relative error of at most 0.022.
The roundings to bfloat16 on the way count: a program that leaves them out, or rounds other values in their place, can miss the bound.
Values may be sent and summed in bfloat16 or wider, within the bound.
A program may use at most 128 MiB of HBM per device.

v0:
```python
import math

import jax
import jax.numpy as jnp
from jax import lax
from jax.sharding import PartitionSpec as P

HEADS = 12
HEAD = 64
BLOCK = 512


norm_eps = 1e-06
learn_rate = 0.2
decay_rate = 0.01
moment_eps = 1e-06


def alibi_table(head_total):
    power_two = 2 ** int(math.floor(math.log2(head_total)))
    first_set = [2.0 ** (-8.0 * (j + 1) / power_two) for j in range(power_two)]
    extra_set = [2.0 ** (-4.0 * (2 * j + 1) / power_two) for j in range(head_total - power_two)]
    return jnp.array(first_set + extra_set, jnp.float32)


def layer_norm(tensor_in, gain_row, shift_row):
    center = tensor_in - jnp.mean(tensor_in, axis=-1, keepdims=True)
    spread = jnp.mean(center * center, axis=-1, keepdims=True)
    return center * lax.rsqrt(spread + norm_eps) * gain_row + shift_row


def gated(gate_val, up_val):
    return jax.nn.gelu(gate_val, approximate=False) * up_val


def score_block(query_block, key_rows, slope, first_row):
    raw_scores = lax.dot_general(
        query_block, key_rows, (((1,), (1,)), ((), ())), preferred_element_type=jnp.float32
    )
    row_pos = first_row + jnp.arange(query_block.shape[0], dtype=jnp.int32)
    col_pos = jnp.arange(key_rows.shape[0], dtype=jnp.int32)
    distance = jnp.abs(row_pos[:, None] - col_pos[None, :]).astype(jnp.float32)
    return raw_scores * query_block.shape[1] ** (-0.5) - slope * distance


def head_forward(members):
    queries, key_rows, value_rows, slope = members
    length = key_rows.shape[0]
    block_rows = min(BLOCK, length)
    amount = length // block_rows

    def one_block(pieces):
        query_block, first_row = pieces
        scores = score_block(query_block, key_rows, slope, first_row)
        top_val = jnp.max(scores, axis=-1, keepdims=True)
        weights = jnp.exp(scores - top_val)
        totals = jnp.sum(weights, axis=-1, keepdims=True)
        soft_weights = (weights / totals).astype(jnp.bfloat16)
        result = jnp.dot(soft_weights, value_rows, preferred_element_type=jnp.float32)
        return (result, (top_val + jnp.log(totals))[:, 0])

    starts = jnp.arange(amount, dtype=jnp.int32) * block_rows
    outputs, log_totals = lax.map(one_block, (queries.reshape(amount, block_rows, -1), starts))
    return (outputs.reshape(length, -1), log_totals.reshape(length))


def head_backward(members):
    queries, key_rows, value_rows, grad_rows, log_totals, slope = members
    length = key_rows.shape[0]
    block_rows = min(BLOCK, length)
    amount = length // block_rows
    scale_val = queries.shape[1] ** (-0.5)

    def one_block(running, pieces):
        grad_keys, grad_values = running
        query_block, grad_block, total_block, first_row = pieces
        scores = score_block(query_block, key_rows, slope, first_row)
        soft_weights = jnp.exp(scores - total_block[:, None])
        grad_values = grad_values + lax.dot_general(
            soft_weights.astype(jnp.bfloat16),
            grad_block,
            (((0,), (0,)), ((), ())),
            preferred_element_type=jnp.float32,
        )
        grad_soft = lax.dot_general(
            grad_block, value_rows, (((1,), (1,)), ((), ())), preferred_element_type=jnp.float32
        )
        centre = jnp.sum(soft_weights * grad_soft, axis=-1, keepdims=True)
        grad_scores = (soft_weights * (grad_soft - centre)).astype(jnp.bfloat16)
        grad_query = jnp.dot(grad_scores, key_rows, preferred_element_type=jnp.float32) * scale_val
        grad_keys = (
            grad_keys
            + lax.dot_general(
                grad_scores,
                query_block,
                (((0,), (0,)), ((), ())),
                preferred_element_type=jnp.float32,
            )
            * scale_val
        )
        return ((grad_keys, grad_values), grad_query)

    starts = jnp.arange(amount, dtype=jnp.int32) * block_rows
    empty = jnp.zeros(key_rows.shape, jnp.float32)
    pieces = (
        queries.reshape(amount, block_rows, -1),
        grad_rows.reshape(amount, block_rows, -1),
        log_totals.reshape(amount, block_rows),
        starts,
    )
    (grad_keys, grad_values), grad_query = lax.scan(one_block, (empty, empty), pieces)
    return (grad_keys, grad_values, grad_query.reshape(length, -1))


def lamb_terms(weight, gradient, moments):
    first_moment = 0.5 * moments[0] + 0.5 * gradient
    root_moment = jnp.sqrt(0.5 * moments[1] * moments[1] + 0.5 * gradient * gradient)
    direction = first_moment / (root_moment + moment_eps) + decay_rate * weight
    return (jnp.stack([first_moment, root_moment]), direction)


def piece_sums(tensor_val, stacked):
    squares = tensor_val * tensor_val
    if stacked:
        return jnp.sum(squares.reshape(squares.shape[0], -1), axis=1)
    return jnp.sum(squares).reshape(1)


def local(
    inputs,
    cotangent,
    attn_w,
    out_w,
    glu_w,
    down_w,
    qv_bias,
    vectors,
    attn_mom,
    out_mom,
    glu_mom,
    down_mom,
    qv_mom,
    vector_mom,
):
    tensor_pos = lax.axis_index("tensor")
    attn_all, out_all, glu_all, down_all, qv_all, vector_all = (
        lax.all_gather(attn_w.astype(jnp.bfloat16), "dp", axis=1, tiled=True),
        lax.all_gather(out_w.astype(jnp.bfloat16), "dp", axis=1, tiled=True),
        lax.all_gather(glu_w.astype(jnp.bfloat16), "dp", axis=1, tiled=True),
        lax.all_gather(down_w.astype(jnp.bfloat16), "dp", axis=1, tiled=True),
        lax.all_gather(qv_bias.astype(jnp.bfloat16), "dp", axis=1, tiled=True),
        lax.all_gather(vectors.astype(jnp.bfloat16), "dp", axis=1, tiled=True),
    )
    vector_rows = vector_all.astype(jnp.float32)
    qv_rows = qv_all.astype(jnp.float32)
    head_cols = out_all.shape[0]
    head_count = head_cols // HEAD
    slopes_mine = lax.dynamic_slice_in_dim(alibi_table(HEADS), tensor_pos * head_count, head_count)
    inputs_local = inputs.astype(jnp.float32)
    inputs_full = lax.all_gather(inputs, "tensor", axis=0, tiled=True)
    length = inputs_full.shape[0]
    projected = jnp.einsum("td,kdc->ktc", inputs_full, attn_all, preferred_element_type=jnp.float32)
    queries = (projected[0] + qv_rows[0]).astype(jnp.bfloat16)
    key_rows = projected[1].astype(jnp.bfloat16)
    value_rows = (projected[2] + qv_rows[1]).astype(jnp.bfloat16)

    def split_heads(tensor_in):
        return tensor_in.reshape(length, head_count, HEAD).transpose(1, 0, 2)

    def join_heads(tensor_in):
        return tensor_in.transpose(1, 0, 2).reshape(length, head_cols)

    head_out, log_totals = lax.map(
        head_forward,
        (split_heads(queries), split_heads(key_rows), split_heads(value_rows), slopes_mine),
    )
    attended = join_heads(head_out).astype(jnp.bfloat16)
    branch_one = lax.psum_scatter(
        jnp.dot(attended, out_all, preferred_element_type=jnp.float32),
        "tensor",
        scatter_dimension=0,
        tiled=True,
    )
    summed_one = inputs_local + branch_one + vector_rows[0]
    normed_one, norm_one_back = jax.vjp(layer_norm, summed_one, vector_rows[1], vector_rows[2])
    normed_full = lax.all_gather(normed_one.astype(jnp.bfloat16), "tensor", axis=0, tiled=True)
    gate_up = jnp.einsum("td,kdf->ktf", normed_full, glu_all, preferred_element_type=jnp.float32)
    hidden_val, gated_back = jax.vjp(gated, gate_up[0], gate_up[1])
    hidden = hidden_val.astype(jnp.bfloat16)
    branch_two = lax.psum_scatter(
        jnp.dot(hidden, down_all, preferred_element_type=jnp.float32),
        "tensor",
        scatter_dimension=0,
        tiled=True,
    )
    summed_two = normed_one + branch_two + vector_rows[3]
    output, norm_two_back = jax.vjp(layer_norm, summed_two, vector_rows[4], vector_rows[5])
    grad_two, grad_gain_two, grad_shift_two = norm_two_back(cotangent.astype(jnp.float32))
    grad_branch = lax.all_gather(grad_two.astype(jnp.bfloat16), "tensor", axis=0, tiled=True)
    down_grad = lax.dot_general(
        hidden, grad_branch, (((0,), (0,)), ((), ())), preferred_element_type=jnp.float32
    )
    grad_hidden = lax.dot_general(
        grad_branch, down_all, (((1,), (1,)), ((), ())), preferred_element_type=jnp.float32
    )
    grad_gate, grad_up = gated_back(grad_hidden)
    grad_glu = jnp.stack([grad_gate, grad_up]).astype(jnp.bfloat16)
    glu_grad = jnp.einsum("td,ktf->kdf", normed_full, grad_glu, preferred_element_type=jnp.float32)
    piece = grad_glu
    grad_normed = grad_two + lax.psum_scatter(
        jnp.einsum("ktf,kdf->td", piece, glu_all, preferred_element_type=jnp.float32),
        "tensor",
        scatter_dimension=0,
        tiled=True,
    )
    grad_one, grad_gain_one, grad_shift_one = norm_one_back(grad_normed)
    grad_attn = lax.all_gather(grad_one.astype(jnp.bfloat16), "tensor", axis=0, tiled=True)
    out_grad = lax.dot_general(
        attended, grad_attn, (((0,), (0,)), ((), ())), preferred_element_type=jnp.float32
    )
    grad_attended = lax.dot_general(
        grad_attn, out_all, (((1,), (1,)), ((), ())), preferred_element_type=jnp.float32
    ).astype(jnp.bfloat16)
    grad_keys, grad_values, grad_query = lax.map(
        head_backward,
        (
            split_heads(queries),
            split_heads(key_rows),
            split_heads(value_rows),
            split_heads(grad_attended),
            log_totals,
            slopes_mine,
        ),
    )
    grad_qkv = jnp.stack(
        [join_heads(grad_query), join_heads(grad_keys), join_heads(grad_values)]
    ).astype(jnp.bfloat16)
    attn_grad = jnp.einsum("td,ktc->kdc", inputs_full, grad_qkv, preferred_element_type=jnp.float32)
    qv_grad = jnp.stack(
        [
            jnp.sum(grad_qkv[0].astype(jnp.float32), axis=0),
            jnp.sum(grad_qkv[2].astype(jnp.float32), axis=0),
        ]
    )
    piece = grad_qkv
    input_grad = grad_one + lax.psum_scatter(
        jnp.einsum("ktc,kdc->td", piece, attn_all, preferred_element_type=jnp.float32),
        "tensor",
        scatter_dimension=0,
        tiled=True,
    )
    attn_sum, out_sum, glu_sum, down_sum, qv_sum = (
        lax.psum_scatter(attn_grad, "dp", scatter_dimension=1, tiled=True),
        lax.psum_scatter(out_grad, "dp", scatter_dimension=1, tiled=True),
        lax.psum_scatter(glu_grad, "dp", scatter_dimension=1, tiled=True),
        lax.psum_scatter(down_grad, "dp", scatter_dimension=1, tiled=True),
        lax.psum_scatter(qv_grad, "dp", scatter_dimension=1, tiled=True),
    )
    vector_part = jnp.stack(
        [
            jnp.sum(grad_one, axis=0),
            grad_gain_one,
            grad_shift_one,
            jnp.sum(grad_two, axis=0),
            grad_gain_two,
            grad_shift_two,
        ]
    )
    vector_sum = lax.psum_scatter(vector_part, ("dp", "tensor"), scatter_dimension=1, tiled=True)
    slice_width = vector_mom.shape[2]
    vector_own = lax.dynamic_slice_in_dim(vectors, tensor_pos * slice_width, slice_width, 1)
    owned_parts = (attn_w, out_w, glu_w, down_w, qv_bias, vector_own)
    gradients = (attn_sum, out_sum, glu_sum, down_sum, qv_sum, vector_sum)
    moments = (attn_mom, out_mom, glu_mom, down_mom, qv_mom, vector_mom)
    stack_flags = (True, False, True, False, True, True)
    new_moments = []
    directions = []
    for weight, gradient, moment in zip(owned_parts, gradients, moments):
        pair, direction = lamb_terms(weight, gradient, moment)
        new_moments.append(pair)
        directions.append(direction)
    weight_sums = jnp.concatenate([piece_sums(w, f) for w, f in zip(owned_parts, stack_flags)])
    dir_sums = jnp.concatenate([piece_sums(r, f) for r, f in zip(directions, stack_flags)])
    totals = lax.psum(jnp.stack([weight_sums, dir_sums]), ("dp", "tensor"))
    norm_values = jnp.sqrt(totals + 1e-12)
    ratios = norm_values[0] / norm_values[1]
    new_weights = []
    offset = 0
    for weight, direction, stacked in zip(owned_parts, directions, stack_flags):
        amount = weight.shape[0] if stacked else 1
        factor = ratios[offset : offset + amount]
        if stacked:
            factor = factor.reshape((amount,) + (1,) * (weight.ndim - 1))
        else:
            factor = factor[0]
        new_weights.append(weight - learn_rate * factor * direction)
        offset = offset + amount
    return (
        output.astype(jnp.bfloat16),
        input_grad,
        attn_sum,
        out_sum,
        glu_sum,
        down_sum,
        qv_sum,
        vector_sum,
        new_moments[0],
        new_moments[1],
        new_moments[2],
        new_moments[3],
        new_moments[4],
        new_moments[5],
        new_weights[0],
        new_weights[1],
        new_weights[2],
        new_weights[3],
        new_weights[4],
        new_weights[5],
        norm_values,
        ratios,
    )


def solution(mesh):
    placed = (
        P(("dp", "tensor"), None),
        P(("dp", "tensor"), None),
        P(None, "dp", "tensor"),
        P("tensor", "dp"),
        P(None, "dp", "tensor"),
        P("tensor", "dp"),
        P(None, ("tensor", "dp")),
        P(None, "dp"),
        P(None, None, "dp", "tensor"),
        P(None, "tensor", "dp"),
        P(None, None, "dp", "tensor"),
        P(None, "tensor", "dp"),
        P(None, None, ("tensor", "dp")),
        P(None, None, ("dp", "tensor")),
    )
    return jax.shard_map(
        local,
        mesh=mesh,
        in_specs=placed,
        out_specs=(
            P(("dp", "tensor"), None),
            P(("dp", "tensor"), None),
            P(None, "dp", "tensor"),
            P("tensor", "dp"),
            P(None, "dp", "tensor"),
            P("tensor", "dp"),
            P(None, ("tensor", "dp")),
            P(None, ("dp", "tensor")),
            P(None, None, "dp", "tensor"),
            P(None, "tensor", "dp"),
            P(None, None, "dp", "tensor"),
            P(None, "tensor", "dp"),
            P(None, None, ("tensor", "dp")),
            P(None, None, ("dp", "tensor")),
            P(None, "dp", "tensor"),
            P("tensor", "dp"),
            P(None, "dp", "tensor"),
            P("tensor", "dp"),
            P(None, ("tensor", "dp")),
            P(None, ("dp", "tensor")),
            P(),
            P(),
        ),
        check_vma=False,
    )
```

profile of v0, /device:TPU:0, one launch (start us, length us, event | category | flops | bytes accessed | tf_op | source)
XLA Modules:
  0.0 1193.6 jit_solution(6248312872441670400)
XLA Ops:
  12.0 10.3 all-gather
  24.3 10.5 all_gather.33
  34.8 12.6 %all_gather.30 = bf16[3,768,192]{2,0,1:T(4,128)(2,1)S(1)} all-gather(bf16[3,96,192]{2,0,1:T(4,128)(2,1)S(1)} %copy.135), channel_id=1, replica_groups=mesh['dp'=8,'tensor'=4] {'dp'}, dimensions={1}, use_global_device_ids=true | all-gather | bytes 995328 | tf_op jit(solution)/shard_map/all_gather | solution.py:147
  47.4 29.2 %all-gather.9.cloned.1.call-done = bf16[2048,768]{1,0:T(8,128)(2,1)} async-done(((bf16[512,768]{1,0:T(8,128)(2,1)}), bf16[2048,768]{1,0:T(8,128)(2,1)}) %all-gather.9.cloned.1.call-update) | async-done | bytes 3145744 | tf_op jit(solution)/shard_map/all_gather | solution.py:160
  76.6 4.6 convolution_bitcast_fusion.2
  88.0 5.0 fusion.61
  94.0 125.0 %while.54 = (s32[]{:T(128)}, bf16[3,2048,64]{1,2,0:T(8,128)(2,1)}, f32[3,2048]{1,0:T(4,128)S(1)}, bf16[3,2048,64]{2,1,0:T(8,128)(2,1)}, bf16[3,2048,64]{2,1,0:T(...) while((s32[]{:T(128)}, bf16[3,2048,64]{1,2,0:T(8,128)(2,1)}, ...), condition=%wide.region_5.6_spmd, body=%wide.region_0.5_spmd.sunk | while | flops 281018368 | bytes 33874828 | solution.py:173
  96.8 37.5 %while.57 = (s32[]{:T(128)}, bf16[4,512,64]{1,2,0:T(8,128)(2,1)S(1)}, f32[4,512]{1,0:T(4,128)S(1)}, bf16[4,512,64]{2,1,0:T(8,128)(2,1)S(1)}, bf16[2048,64]{1,0:T...) while((s32[]{:T(128)}, ...), condition=%wide.region_4.4_spmd, body=%wide.region_1.3_spmd.sunk | while | flops 281018368 | bytes 30695584 | solution.py:63
  138.5 37.5 %while.57 = (s32[]{:T(128)}, bf16[4,512,64]{1,2,0:T(8,128)(2,1)S(1)}, f32[4,512]{1,0:T(4,128)S(1)}, bf16[4,512,64]{2,1,0:T(8,128)(2,1)S(1)}, bf16[2048,64]{1,0:T...) while((s32[]{:T(128)}, ...), condition=%wide.region_4.4_spmd, body=%wide.region_1.3_spmd.sunk | while | flops 281018368 | bytes 30695584 | solution.py:63
  180.2 37.5 %while.57 = (s32[]{:T(128)}, bf16[4,512,64]{1,2,0:T(8,128)(2,1)S(1)}, f32[4,512]{1,0:T(4,128)S(1)}, bf16[4,512,64]{2,1,0:T(8,128)(2,1)S(1)}, bf16[2048,64]{1,0:T...) while((s32[]{:T(128)}, ...), condition=%wide.region_4.4_spmd, body=%wide.region_1.3_spmd.sunk | while | flops 281018368 | bytes 30695584 | solution.py:63
  219.0 5.5 fusion.110
  227.1 9.1 all-gather.1
  236.3 97.9 %reduce-scatter.14.cloned.1.call-done = f32[512,768]{1,0:T(8,128)} async-done(((f32[2048,768]{1,0:T(8,128)}), f32[512,768]{1,0:T(8,128)}) %reduce-scatter.14.cloned.1.call-update) | async-done | bytes 1572880 | tf_op jit(solution)/shard_map/reduce_scatter | solution.py:178
  338.9 62.5 %all-gather.11.cloned.1.call-done = bf16[2048,768]{1,0:T(8,128)(2,1)} async-done(((bf16[512,768]{1,0:T(8,128)(2,1)}), bf16[2048,768]{1,0:T(8,128)(2,1)}) %all-gather.11.cloned.1.call-update) | async-done | bytes 3145744 | tf_op jit(solution)/shard_map/all_gather | solution.py:186
  401.4 7.8 convolution_bitcast_fusion
  409.2 4.6 copy-done.12
  413.8 14.7 %multiply_convert_fusion.2 = (bf16[2048,768]{1,0:T(8,128)(2,1)}, f32[2048,768]{1,0:T(8,128)}) fusion(f32[2,2048,768]{2,1,0:T(8,128)S(1)} %convolution_bitcast_fusion), kind=kLoop, calls=%fused_computation.69 | loop fusion | flops 103809024 | bytes 22020096 | tf_op jit(solution)/shard_map/convert_element_type | solution.py:189
  428.5 7.5 fusion.111
  436.4 109.0 %reduce-scatter.16.cloned.1.call-done = f32[512,768]{1,0:T(8,128)} async-done(((f32[2048,768]{1,0:T(8,128)}), f32[512,768]{1,0:T(8,128)}) %reduce-scatter.16.cloned.1.call-update) | async-done | bytes 1572880 | tf_op jit(solution)/shard_map/reduce_scatter | solution.py:190
  552.5 64.1 %all-gather.17.cloned.1.call-done = bf16[2048,768]{1,0:T(8,128)(2,1)} async-done(((bf16[512,768]{1,0:T(8,128)(2,1)}), bf16[2048,768]{1,0:T(8,128)(2,1)}) %all-gather.17.cloned.1.call-update) | async-done | bytes 3145744 | tf_op jit(solution)/shard_map/all_gather | solution.py:199
  616.5 10.2 fusion.53
  629.5 7.0 fusion.46
  636.5 109.5 %reduce-scatter.18.cloned.1.call-done = f32[512,768]{1,0:T(8,128)} async-done(((f32[2048,768]{1,0:T(8,128)}), f32[512,768]{1,0:T(8,128)}) %reduce-scatter.18.cloned.1.call-update) | async-done | bytes 1572880 | tf_op jit(solution)/shard_map/reduce_scatter | solution.py:210
  752.4 8.7 fusion.54
  761.1 8.3 copy.150
  769.6 7.0 fusion.112
  776.7 39.5 %all-gather.19.cloned.1.call-done = bf16[2048,768]{1,0:T(8,128)(2,1)} async-done(((bf16[512,768]{1,0:T(8,128)(2,1)}), bf16[2048,768]{1,0:T(8,128)(2,1)}) %all-gather.19.cloned.1.call-update) | async-done | bytes 3145744 | tf_op jit(solution)/shard_map/all_gather | solution.py:217
  820.9 4.1 convolution_bitcast_fusion.3
  827.0 188.2 %while.56 = (s32[]{:T(128)}, bf16[3,2048,64]{1,2,0:T(8,128)(2,1)}, bf16[3,2048,64]{1,2,0:T(8,128)(2,1)}, bf16[3,2048,64]{2,1,0:T(8,128)(2,1)}, bf16[3,2048,64]{2...) while((s32[]{:T(128)}, bf16[3,2048,64]{1,2,0:T(8,128)(2,1)}, ...), condition=%wide.region_21.22_spmd, body=%wide.region_17.21_spmd.sunk | while | flops 685408256 | bytes 80921272 | solution.py:224
  832.0 54.8 %while.58 = (s32[]{:T(128)}, f32[2048,64]{0,1:T(8,128)}, f32[2048,64]{0,1:T(8,128)S(1)}, bf16[4,512,64]{1,2,0:T(8,128)(2,1)S(1)}, bf16[4,512,64]{2,1,0:T(8,128)(...) while((s32[]{:T(128)}, f32[2048,64]{0,1:T(8,128)}, ...), condition=%wide.region_20.20_spmd.clone, body=%wide.region_18.19_spmd.clone.sunk | while | flops 685408256 | bytes 75382168 | solution.py:111
  834.0 3.2 multiply_reduce_fusion.18
  847.5 3.2 multiply_reduce_fusion.18
  861.3 3.2 multiply_reduce_fusion.18
  875.0 3.2 multiply_reduce_fusion.18
  894.9 54.8 %while.58 = (s32[]{:T(128)}, f32[2048,64]{0,1:T(8,128)}, f32[2048,64]{0,1:T(8,128)S(1)}, bf16[4,512,64]{1,2,0:T(8,128)(2,1)S(1)}, bf16[4,512,64]{2,1,0:T(8,128)(...) while((s32[]{:T(128)}, f32[2048,64]{0,1:T(8,128)}, ...), condition=%wide.region_20.20_spmd.clone, body=%wide.region_18.19_spmd.clone.sunk | while | flops 685408256 | bytes 75382168 | solution.py:111
  896.9 3.2 multiply_reduce_fusion.18
  910.4 3.2 multiply_reduce_fusion.18
  924.2 3.2 multiply_reduce_fusion.18
  957.7 54.6 %while.58 = (s32[]{:T(128)}, f32[2048,64]{0,1:T(8,128)}, f32[2048,64]{0,1:T(8,128)S(1)}, bf16[4,512,64]{1,2,0:T(8,128)(2,1)S(1)}, bf16[4,512,64]{2,1,0:T(8,128)(...) while((s32[]{:T(128)}, f32[2048,64]{0,1:T(8,128)}, ...), condition=%wide.region_20.20_spmd.clone, body=%wide.region_18.19_spmd.clone.sunk | while | flops 685408256 | bytes 75382168 | solution.py:111
  959.7 3.2 multiply_reduce_fusion.18
  973.2 3.2 multiply_reduce_fusion.18
  1000.6 3.2 multiply_reduce_fusion.18
  1017.8 5.6 fusion.63
  1029.4 7.5 convolution_bitcast_fusion.1
  1043.2 3.5 multiply_reduce_fusion.5
  1054.3 42.0 %all-reduce.2 = f32[6,768]{1,0:T(8,128)S(1)} all-reduce(f32[6,768]{1,0:T(8,128)S(1)} %stack.110), channel_id=11, replica_groups=mesh['dp'=8,'tensor'=4] {'dp','tensor'}, use_global_device_ids=true, to_apply=%region_36.37.clone | all-reduce | flops 4608 | bytes 36864
  1098.1 13.2 %all-reduce.1 = f32[2,192]{1,0:T(2,128)S(1)} all-reduce(f32[2,192]{1,0:T(2,128)S(1)} %pad_maximum_fusion.15), channel_id=10, replica_groups=mesh['dp'=8,'tensor'=4] {'dp'}, use_global_device_ids=true, to_apply=%region_29.30.clone | all-reduce | flops 384 | bytes 3072
  1123.2 48.7 %psum.7 = f32[2,15]{1,0:T(2,128)S(1)} all-reduce(f32[2,15]{1,0:T(2,128)S(1)} %pad_maximum_fusion.17), channel_id=1, replica_groups=mesh['dp'=8,'tensor'=4] {'dp','tensor'}, use_global_device_ids=true, to_apply=%region_49.50 | all-reduce | flops 30 | bytes 240 | tf_op jit(solution)/shard_map/psum | solution.py:284
  (717 shorter events, 369.5 us)
Async XLA Ops:
  8.0 68.6 %all-gather.9.cloned.1.call-start = ((), (), s32[]{:S(2)}) async-start(), calls=%async_computation.7 | async-start | bytes 3932160 | tf_op jit(solution)/shard_map/all_gather | solution.py:160
  8.8 325.4 %reduce-scatter.14.cloned.1.call-start = ((), (), s32[]{:S(2)}) async-start(), calls=%async_computation.8 | async-start | bytes 7864320 | tf_op jit(solution)/shard_map/reduce_scatter | solution.py:178
  47.4 29.2 %copy-start.25 = (bf16[3,768,192]{2,0,1:T(4,128)(2,1)}, bf16[3,768,192]{2,0,1:T(4,128)(2,1)S(1)}, u32[]{:S(2)}) copy-start(bf16[3,768,192]{2,0,1:T(4,128)(2,1)S(1)} %all_gather.30) | copy-start | bytes 2654212
  219.0 5.5 copy-start.9
  224.6 109.6 %copy-start.19 = (bf16[512,768]{1,0:T(8,128)(2,1)S(1)}, bf16[512,768]{1,0:T(8,128)(2,1)}, u32[]{:S(2)}) copy-start(bf16[512,768]{1,0:T(8,128)(2,1)} %param.23) | copy-start | bytes 2359300
  224.6 114.2 %all-gather.13.cloned.1.call-start = ((), (), s32[]{:S(2)}) async-start(), calls=%async_computation.10 | async-start | bytes 2654208 | tf_op jit(solution)/shard_map/all_gather | solution.py:149
  227.0 174.4 %all-gather.11.cloned.1.call-start = ((), (), s32[]{:S(2)}) async-start(), calls=%async_computation.9 | async-start | bytes 3932160 | tf_op jit(solution)/shard_map/all_gather | solution.py:186
  337.4 91.1 %all-gather.15.cloned.1.call-start = ((), (), s32[]{:S(2)}) async-start(), calls=%async_computation.11 | async-start | bytes 1327104 | tf_op jit(solution)/shard_map/all_gather | solution.py:150
  338.8 206.7 %reduce-scatter.16.cloned.1.call-start = ((), (), s32[]{:S(2)}) async-start(), calls=%async_computation.12 | async-start | bytes 7864320 | tf_op jit(solution)/shard_map/reduce_scatter | solution.py:190
  436.0 180.6 %all-gather.17.cloned.1.call-start = ((), (), s32[]{:S(2)}) async-start(), calls=%async_computation.13 | async-start | bytes 3932160 | tf_op jit(solution)/shard_map/all_gather | solution.py:199
  552.4 193.6 %reduce-scatter.18.cloned.1.call-start = ((), (), s32[]{:S(2)}) async-start(), calls=%async_computation.14 | async-start | bytes 7864320 | tf_op jit(solution)/shard_map/reduce_scatter | solution.py:210
  616.5 12.9 %copy-start.56 = (bf16[2,768,768]{2,1,0:T(8,128)(2,1)S(1)}, bf16[2,768,768]{2,1,0:T(8,128)(2,1)}, u32[]{:S(2)}) copy-start(bf16[2,768,768]{2,1,0:T(8,128)(2,1)} %all-gather.13.cloned.1.call-done) | copy-start | bytes 7077892
  636.5 179.8 %all-gather.19.cloned.1.call-start = ((), (), s32[]{:S(2)}) async-start(), calls=%async_computation.15 | async-start | bytes 3932160 | tf_op jit(solution)/shard_map/all_gather | solution.py:217
  752.4 290.9 %all-reduce.5.cloned.1.call-start = ((), (), s32[]{:S(2)}) async-start(), calls=%async_computation.20 | async-start | bytes 9437184
  769.4 46.9 %copy-start.16 = (bf16[192,768]{0,1:T(8,128)(2,1)S(1)}, bf16[192,768]{0,1:T(8,128)(2,1)}, u32[]{:S(2)}) copy-start(bf16[192,768]{0,1:T(8,128)(2,1)} %all_gather.33) | copy-start | bytes 884740
  769.4 281.2 %reduce-scatter.22.cloned.1.call-start = ((), (), s32[]{:S(2)}) async-start(), calls=%async_computation.17 | async-start | bytes 2654208 | tf_op jit(solution)/shard_map/reduce_scatter | solution.py:256
  776.7 336.1 %reduce-scatter.26.cloned.1.call-start = ((), (), s32[]{:S(2)}) async-start(), calls=%async_computation.19 | async-start | bytes 884736
  776.7 44.2 %copy-start.13 = (bf16[3,2048,64]{1,2,0:T(8,128)(2,1)S(1)}, bf16[3,2048,64]{1,2,0:T(8,128)(2,1)}, u32[]{:S(2)}) copy-start(bf16[3,2048,64]{1,2,0:T(8,128)(2,1)} %get-tuple-element.216) | copy-start | bytes 2359300
  825.0 293.0 %reduce-scatter.24.cloned.1.call-start = ((), (), s32[]{:S(2)}) async-start(), calls=%async_computation.18 | async-start | bytes 2211840
  832.0 5.3 copy-start.5
  845.6 5.3 copy-start.5
  894.9 5.3 copy-start.5
  908.4 5.3 copy-start.5
  971.2 5.3 copy-start.5
  998.6 5.3 copy-start.5
  1029.2 154.1 %reduce-scatter.20.cloned.1.call-start = ((), (), s32[]{:S(2)}) async-start(), calls=%async_computation.16 | async-start | bytes 7864320 | tf_op jit(solution)/shard_map/reduce_scatter | solution.py:246
  1037.0 6.2 copy-start.41
  1037.0 6.2 copy-start.40
  1037.0 6.2 copy-start.39
  1037.0 6.2 copy-start.15
  1049.4 46.9 %copy-start.36 = (f32[6,96]{1,0:T(8,128)S(1)}, f32[6,96]{1,0:T(8,128)}, u32[]{:S(2)}) copy-start(f32[6,96]{1,0:T(8,128)} %param.30) | copy-start | bytes 6916
  1049.4 48.2 %copy-start.21 = (bf16[2048,3,64]{0,2,1:T(8,128)(2,1)S(1)}, bf16[2048,3,64]{0,2,1:T(8,128)(2,1)}, u32[]{:S(2)}) copy-start(bf16[2048,3,64]{0,2,1:T(8,128)(2,1)} %copy-done.20) | copy-start | bytes 2359300
  1049.4 48.4 %copy-start.18 = (bf16[3,2048,64]{1,2,0:T(8,128)(2,1)S(1)}, bf16[3,2048,64]{1,2,0:T(8,128)(2,1)}, u32[]{:S(2)}) copy-start(bf16[3,2048,64]{1,2,0:T(8,128)(2,1)} %get-tuple-element.220) | copy-start | bytes 2359300
  1049.5 61.9 %copy-start.46 = (f32[2,24]{1,0:T(2,128)S(1)}, f32[2,24]{1,0:T(2,128)}, u32[]{:S(2)}) copy-start(f32[2,24]{1,0:T(2,128)} %param.29) | copy-start | bytes 580
  1049.5 61.9 %copy-start.47 = (f32[2,2,24]{2,1,0:T(2,128)S(1)}, f32[2,2,24]{2,1,0:T(2,128)}, u32[]{:S(2)}) copy-start(f32[2,2,24]{2,1,0:T(2,128)} %param.35) | copy-start | bytes 1156
  1050.6 63.1 %copy-start.31 = (f32[192,96]{1,0:T(8,128)S(1)}, f32[192,96]{1,0:T(8,128)}, u32[]{:S(2)}) copy-start(f32[192,96]{1,0:T(8,128)} %param.26) | copy-start | bytes 221188
  1097.0 26.2 %copy-start.43 = (f32[6,24]{1,0:T(8,128)}, f32[6,24]{1,0:T(8,128)S(1)}, u32[]{:S(2)}) copy-start(f32[6,24]{1,0:T(8,128)S(1)} %get-tuple-element.501) | copy-start | bytes 1732
  1097.9 21.5 %copy-start.28 = (f32[1,3,96,192]{2,3,1,0:T(8,128)S(1)}, f32[1,3,96,192]{2,3,1,0:T(8,128)}, u32[]{:S(2)}) copy-start(f32[1,3,96,192]{2,3,1,0:T(8,128)} %copy.180) | copy-start | bytes 663556
  1097.9 21.5 %copy-start.29 = (f32[1,3,96,192]{2,3,1,0:T(8,128)S(1)}, f32[1,3,96,192]{2,3,1,0:T(8,128)}, u32[]{:S(2)}) copy-start(f32[1,3,96,192]{2,3,1,0:T(8,128)} %copy.181) | copy-start | bytes 663556
  1097.9 22.6 %copy-start.51 = (f32[6]{0:T(128)S(1)}, f32[6]{0:T(128)}, u32[]{:S(2)}) copy-start(f32[6]{0:T(128)} %get-tuple-element.499) | copy-start | bytes 76
  1113.7 60.3 %copy-start.33 = (f32[192,96]{1,0:T(8,128)}, f32[192,96]{1,0:T(8,128)S(1)}, u32[]{:S(2)}) copy-start(f32[192,96]{1,0:T(8,128)S(1)} %copy.172) | copy-start | bytes 221188
  1174.0 6.1 copy-start.54
  1174.0 6.6 copy-start.50
  1174.0 6.6 copy-start.52
  1174.0 7.9 copy-start.34
  1174.0 8.5 copy-start.26
  1174.1 9.2 copy-start.11
  1174.1 9.2 copy-start.38
  (125 other events, 375.8 us)
Sparse Core Ops, SparseCore 0:
  10.4 66.1 all-gather.8
  224.7 109.4 reduce-scatter.13
  552.6 63.9 all-gather.16
  636.6 109.4 reduce-scatter.17
Sparse Core Ops, SparseCore 1:
  227.6 27.4 all-gather.12
  337.5 63.8 all-gather.10
  403.7 22.4 all-gather.14
  436.1 109.3 reduce-scatter.15
  752.4 63.8 all-gather.18
  819.6 84.9 all-reduce.4
  908.4 42.3 reduce-scatter.21
  953.7 34.9 reduce-scatter.25
  1029.2 38.6 reduce-scatter.23
  1070.2 112.1 reduce-scatter.19
where the time goes:
time: 1210 us; the launch traced here: 1190 us
  waiting for transfers between devices  513 us (42%)
  matrix products  262 us (22%)
  local copies, waits for them, and re-layouts  154 us (13%)
  blocking collectives  146 us (12%)
  other arithmetic  95.3 us (8%)
  between operations  19.1 us (2%)
    reduce_scatter x1, waiting for transfers between devices, local(): lax.psum_scatter(jnp.einsum('ktf,kdf->td', piece, glu_all, preferred_elem...  110 us
    reduce_scatter x1, waiting for transfers between devices, local(): lax.psum_scatter(jnp.dot(hidden, down_all, preferred_element_type=jnp.flo...  109 us
    reduce_scatter x1, waiting for transfers between devices, local(): lax.psum_scatter(jnp.dot(attended, out_all, preferred_element_type=jnp.fl...  97.9 us
    dot_general x24, matrix products, score_block(): lax.dot_general(query_block, key_rows, (((1,), (1,)), ((), ())), preferre...  65.8 us
    all_gather x1, waiting for transfers between devices, local(): lax.all_gather(grad_two.astype(jnp.bfloat16), 'tensor', axis=0, tiled=True)  64.1 us
    all_gather x1, waiting for transfers between devices, local(): lax.all_gather(normed_one.astype(jnp.bfloat16), 'tensor', axis=0, tiled=T...  62.5 us
    unnamed x2, blocking collectives  55.2 us
    psum x1, blocking collectives, local(): totals = lax.psum(jnp.stack([weight_sums, dir_sums]), ('dp', 'tensor'))  48.7 us
  transfers between devices with their start and end apart: 14, of which 7 were waited for; matrix products, arithmetic and copies ran while one was open for 24% of the time, Pallas kernels for 0%

commit v1 on v0

v1 whole, which is shorter than its diff:
```python
import functools
import math

import jax
import jax.numpy as jnp
import numpy as np
from jax import lax
from jax.experimental import pallas as pl
from jax.experimental.pallas import tpu as pltpu
from jax.sharding import PartitionSpec as P

HEADS = 12
HEAD = 64
BLOCK = 256

norm_eps = 1e-06
learn_rate = 0.2
decay_rate = 0.01
moment_eps = 1e-06

bf16 = jnp.bfloat16
f32 = jnp.float32


def dot(a, b, ca, cb):
    return lax.dot_general(a, b, (((ca,), (cb,)), ((), ())), preferred_element_type=f32)


def slope_parts(head_total):
    power_two = 2 ** int(math.floor(math.log2(head_total)))
    slopes = [2.0 ** (-8.0 * (j + 1) / power_two) for j in range(power_two)]
    slopes += [2.0 ** (-4.0 * (2 * j + 1) / power_two) for j in range(head_total - power_two)]
    rest = np.array(slopes, np.float32)
    parts = []
    for _ in range(3):
        part = rest.astype(bf16).astype(np.float32)
        parts.append(part)
        rest = rest - part
    return np.stack(parts, axis=1)


def layer_norm(tensor_in, gain_row, shift_row):
    center = tensor_in - jnp.mean(tensor_in, axis=-1, keepdims=True)
    spread = jnp.mean(center * center, axis=-1, keepdims=True)
    return center * lax.rsqrt(spread + norm_eps) * gain_row + shift_row


def gated(gate_val, up_val):
    return jax.nn.gelu(gate_val, approximate=False) * up_val


def pos_features(length, parts):
    row = lax.broadcasted_iota(jnp.int32, (length, HEAD), 0)
    lane = lax.broadcasted_iota(jnp.int32, (length, HEAD), 1)
    low = (row & 7).astype(f32)
    high = row.astype(f32) - low
    m1, m2, m3 = parts
    slope_q = jnp.where(lane < 2, m1, jnp.where(lane < 4, m2, m3))
    for_q = jnp.where(lane < 6, slope_q, jnp.where(lane < 9, high, jnp.where(lane < 12, low, 0.0)))
    turn = lane - 6
    slope_k = jnp.where(
        (turn == 0) | (turn == 3), m1, jnp.where((turn == 1) | (turn == 4), m2, m3)
    )
    for_k = jnp.where(
        lane < 6, jnp.where((lane & 1) == 0, high, low), jnp.where(lane < 12, -slope_k, 0.0)
    )
    return for_q, for_k


def key_after_query(block):
    late = lax.broadcasted_iota(jnp.int32, (block, block), 0) - lax.broadcasted_iota(
        jnp.int32, (block, block), 1
    )
    return jnp.maximum(late, 0).astype(f32)


def fwd_kernel(
    parts_ref, qkv_ref, out_ref, lse_ref, q_s, k_s, v_s, corr_s, s_s, *, heads, length, unroll
):
    amount = length // BLOCK
    for h in range(heads):
        for_q, for_k = pos_features(length, [parts_ref[h, i] for i in range(3)])
        base = h * 3 * HEAD
        q = qkv_ref[:, base : base + HEAD].astype(f32) * HEAD**-0.5
        k = qkv_ref[:, base + HEAD : base + 2 * HEAD].astype(f32)
        v = qkv_ref[:, base + 2 * HEAD : base + 3 * HEAD].astype(f32)
        q_s[h, 0] = jnp.concatenate([q, for_q], axis=1).astype(bf16)
        q_s[h, 1] = jnp.concatenate([q, -for_q], axis=1).astype(bf16)
        k_s[h] = jnp.concatenate([k, for_k], axis=1).astype(bf16)
        v_s[h] = v.T.astype(bf16)
    late = key_after_query(BLOCK)

    def head(h, _):
        corr_s[...] = 2.0 * (parts_ref[h, 0] + parts_ref[h, 1] + parts_ref[h, 2]) * late

        def group(g, _):
            for u in range(unroll):
                b = g * unroll + u
                rows = pl.ds(pl.multiple_of(b * BLOCK, BLOCK), BLOCK)
                for c in range(amount):
                    after = (c > b).astype(jnp.int32)
                    keys = slice(c * BLOCK, (c + 1) * BLOCK)
                    s_s[u, keys, :] = dot(k_s[h, keys, :], q_s[h, after, rows, :], 1, 1)
                s_s[u, rows, :] = s_s[u, rows, :] - corr_s[...]
            for u in range(unroll):
                b = g * unroll + u
                rows = pl.ds(pl.multiple_of(b * BLOCK, BLOCK), BLOCK)
                s = s_s[u]
                top = jnp.max(s, axis=0, keepdims=True)
                p = jnp.exp(s - top)
                total = jnp.sum(p, axis=0, keepdims=True)
                o = dot(v_s[h], p.astype(bf16), 1, 0)
                out_ref[h, :, rows] = (o / total).astype(bf16)
                lse_ref[h, :, rows] = top + jnp.log(total)
            return 0

        lax.fori_loop(0, amount // unroll, group, 0)
        return 0

    lax.fori_loop(0, heads, head, 0)


def attention_forward(parts, qkv):
    length = qkv.shape[0]
    heads = qkv.shape[1] // (3 * HEAD)
    unroll = 2
    vmem = pl.BlockSpec(memory_space=pltpu.VMEM)
    work = heads * length * length
    return pl.pallas_call(
        functools.partial(fwd_kernel, heads=heads, length=length, unroll=unroll),
        out_shape=(
            jax.ShapeDtypeStruct((heads, HEAD, length), bf16),
            jax.ShapeDtypeStruct((heads, 1, length), f32),
        ),
        in_specs=[pl.BlockSpec(memory_space=pltpu.SMEM), vmem],
        out_specs=(vmem, vmem),
        scratch_shapes=[
            pltpu.VMEM((heads, 2, length, 128), bf16),
            pltpu.VMEM((heads, length, 128), bf16),
            pltpu.VMEM((heads, HEAD, length), bf16),
            pltpu.VMEM((BLOCK, BLOCK), f32),
            pltpu.VMEM((unroll, length, BLOCK), f32),
        ],
        compiler_params=pltpu.CompilerParams(vmem_limit_bytes=40 * 2**20),
        cost_estimate=pl.CostEstimate(
            flops=16 * work * HEAD, bytes_accessed=4 * qkv.size, transcendentals=work
        ),
        name="attention_forward",
    )(parts, qkv)


def bwd_kernel(
    parts_ref,
    qkv_ref,
    dot_ref,
    ot_ref,
    lse_ref,
    out_ref,
    q_s,
    qn_s,
    k_s,
    kt_s,
    v_s,
    do_s,
    centre_s,
    corr_s,
    s_s,
    dq_s,
    dk_s,
    dv_s,
    *,
    heads,
    length,
    unroll,
):
    amount = length // BLOCK
    for h in range(heads):
        for_q, for_k = pos_features(length, [parts_ref[h, i] for i in range(3)])
        base = h * 3 * HEAD
        q = qkv_ref[:, base : base + HEAD].astype(f32) * HEAD**-0.5
        k = qkv_ref[:, base + HEAD : base + 2 * HEAD].astype(f32)
        v = qkv_ref[:, base + 2 * HEAD : base + 3 * HEAD]
        turned = q.T
        turned_pos = for_q.T
        q_s[h, 0] = jnp.concatenate([turned, turned_pos], axis=0).astype(bf16)
        q_s[h, 1] = jnp.concatenate([turned, -turned_pos], axis=0).astype(bf16)
        qn_s[h] = q.astype(bf16)
        k_s[h] = jnp.concatenate([k, for_k], axis=1).astype(bf16)
        kt_s[h] = k.T.astype(bf16)
        v_s[h] = v
        grad = dot_ref[h].astype(f32)
        do_s[h] = grad.T.astype(bf16)
        centre_s[h] = jnp.sum(grad * ot_ref[h].astype(f32), axis=0, keepdims=True)
    late = key_after_query(BLOCK)

    def head(h, _):
        corr_s[...] = 2.0 * (parts_ref[h, 0] + parts_ref[h, 1] + parts_ref[h, 2]) * late
        dq_s[...] = jnp.zeros_like(dq_s)

        def group(g, _):
            for u in range(unroll):
                c = g * unroll + u
                rows = pl.ds(pl.multiple_of(c * BLOCK, BLOCK), BLOCK)
                keys = k_s[h, rows, :]
                for i in range(amount):
                    after = (i < c).astype(jnp.int32)
                    cols = slice(i * BLOCK, (i + 1) * BLOCK)
                    s_s[u, :, cols] = dot(keys, q_s[h, after, :, cols], 1, 0)
                s_s[u, :, rows] = s_s[u, :, rows] - corr_s[...]
            for u in range(unroll):
                c = g * unroll + u
                rows = pl.ds(pl.multiple_of(c * BLOCK, BLOCK), BLOCK)
                p = jnp.exp(s_s[u] - lse_ref[h])
                dp = dot(v_s[h, rows, :], dot_ref[h], 1, 0)
                dv_s[rows, :] = dot(p.astype(bf16), do_s[h], 1, 0)
                ds = (p * (dp - centre_s[h])).astype(bf16)
                dk_s[rows, :] = dot(ds, qn_s[h], 1, 0)
                dq_s[...] += dot(kt_s[h, :, rows], ds, 1, 0)
            return 0

        lax.fori_loop(0, amount // unroll, group, 0)
        out_ref[h, 0] = (dq_s[...] * HEAD**-0.5).astype(bf16)
        out_ref[h, 1] = dk_s[...].T.astype(bf16)
        out_ref[h, 2] = dv_s[...].T.astype(bf16)
        return 0

    lax.fori_loop(0, heads, head, 0)


def attention_backward(parts, qkv, grad_t, out_t, lse):
    length = qkv.shape[0]
    heads = qkv.shape[1] // (3 * HEAD)
    unroll = 2
    vmem = pl.BlockSpec(memory_space=pltpu.VMEM)
    work = heads * length * length
    return pl.pallas_call(
        functools.partial(bwd_kernel, heads=heads, length=length, unroll=unroll),
        out_shape=jax.ShapeDtypeStruct((heads, 3, HEAD, length), bf16),
        in_specs=[pl.BlockSpec(memory_space=pltpu.SMEM)] + [vmem] * 4,
        out_specs=vmem,
        scratch_shapes=[
            pltpu.VMEM((heads, 2, 128, length), bf16),
            pltpu.VMEM((heads, length, HEAD), bf16),
            pltpu.VMEM((heads, length, 128), bf16),
            pltpu.VMEM((heads, HEAD, length), bf16),
            pltpu.VMEM((heads, length, HEAD), bf16),
            pltpu.VMEM((heads, length, HEAD), bf16),
            pltpu.VMEM((heads, 1, length), f32),
            pltpu.VMEM((BLOCK, BLOCK), f32),
            pltpu.VMEM((unroll, BLOCK, length), f32),
            pltpu.VMEM((HEAD, length), f32),
            pltpu.VMEM((length, HEAD), f32),
            pltpu.VMEM((length, HEAD), f32),
        ],
        compiler_params=pltpu.CompilerParams(vmem_limit_bytes=48 * 2**20),
        cost_estimate=pl.CostEstimate(
            flops=40 * work * HEAD, bytes_accessed=8 * qkv.size, transcendentals=work
        ),
        name="attention_backward",
    )(parts, qkv, grad_t, out_t, lse)


def lamb_terms(weight, gradient, moments):
    first_moment = 0.5 * moments[0] + 0.5 * gradient
    root_moment = jnp.sqrt(0.5 * moments[1] * moments[1] + 0.5 * gradient * gradient)
    direction = first_moment / (root_moment + moment_eps) + decay_rate * weight
    return (jnp.stack([first_moment, root_moment]), direction)


def piece_sums(tensor_val, stacked):
    squares = tensor_val * tensor_val
    if stacked:
        return jnp.sum(squares.reshape(squares.shape[0], -1), axis=1)
    return jnp.sum(squares).reshape(1)


def local(
    inputs,
    cotangent,
    attn_w,
    out_w,
    glu_w,
    down_w,
    qv_bias,
    vectors,
    attn_mom,
    out_mom,
    glu_mom,
    down_mom,
    qv_mom,
    vector_mom,
    *,
    n_dp,
    n_tensor,
):
    tensor_pos = lax.axis_index("tensor")
    rows = attn_w.shape[1]
    head_cols = attn_w.shape[2]
    head_count = head_cols // HEAD
    width = rows * n_dp
    hidden_cols = glu_w.shape[2]
    tokens = inputs.shape[0]
    length = tokens * n_tensor
    qv_cols = qv_bias.shape[1]
    parts = lax.dynamic_slice_in_dim(
        jnp.asarray(slope_parts(HEADS)), tensor_pos * head_count, head_count
    )

    attn_rows = (
        attn_w.astype(bf16)
        .reshape(3, rows, head_count, HEAD)
        .transpose(1, 2, 0, 3)
        .reshape(rows, 3 * head_cols)
    )
    out_rows = out_w.astype(bf16).T
    glu_rows = glu_w.astype(bf16).transpose(1, 0, 2).reshape(rows, 2 * hidden_cols)
    down_rows = down_w.astype(bf16).T

    small = jnp.concatenate(
        [
            vectors.astype(bf16).T,
            jnp.pad(qv_bias.astype(bf16).reshape(-1), (0, rows - 2 * qv_cols)).reshape(rows, 1),
            jnp.zeros((rows, 57), bf16),
        ],
        axis=1,
    )
    own = lax.all_gather(jnp.concatenate([attn_rows, small], axis=1), "dp", axis=0, tiled=True)
    attn_own = own[:, : 3 * head_cols]
    vector_rows = own[:, 3 * head_cols : 3 * head_cols + 6].T.astype(f32)
    qv_rows = (
        own[:, 3 * head_cols + 6]
        .reshape(n_dp, rows)[:, : 2 * qv_cols]
        .reshape(n_dp, 2, qv_cols)
        .transpose(1, 0, 2)
        .reshape(2, head_cols)
        .astype(f32)
    )
    qkv_bias = (
        jnp.stack([qv_rows[0], jnp.zeros_like(qv_rows[0]), qv_rows[1]])
        .reshape(3, head_count, HEAD)
        .transpose(1, 0, 2)
        .reshape(3 * head_cols)
    )
    inputs_full = lax.all_gather(inputs, "tensor", axis=0, tiled=True)

    sizes = (head_cols, 2 * hidden_cols, hidden_cols, 3 * head_cols)
    packed = lax.all_gather(
        jnp.concatenate([out_rows, glu_rows, down_rows, attn_rows], axis=1), "tensor"
    )
    gathered = []
    offset = 0
    for size in sizes:
        mine = packed[:, :, offset : offset + size].transpose(1, 0, 2).reshape(rows, -1)
        gathered.append(lax.all_gather(mine, "dp", axis=0, tiled=True))
        offset += size
    out_all, glu_all, down_all, attn_all = gathered

    qkv = (dot(inputs_full, attn_own, 1, 0) + qkv_bias).astype(bf16)
    out_t, lse = attention_forward(parts, qkv)
    attended = lax.all_to_all(
        out_t.reshape(head_cols, length), "tensor", split_axis=1, concat_axis=0, tiled=True
    )
    summed_one = inputs.astype(f32) + dot(attended, out_all, 0, 1) + vector_rows[0]
    normed_one, norm_one_back = jax.vjp(layer_norm, summed_one, vector_rows[1], vector_rows[2])
    normed_low = normed_one.astype(bf16)
    gate_up = dot(normed_low, glu_all, 1, 0).reshape(tokens, n_tensor, 2, hidden_cols)
    hidden_val, gated_back = jax.vjp(gated, gate_up[:, :, 0], gate_up[:, :, 1])
    hidden = hidden_val.astype(bf16).reshape(tokens, n_tensor * hidden_cols)
    summed_two = normed_one + dot(hidden, down_all, 1, 1) + vector_rows[3]
    output, norm_two_back = jax.vjp(layer_norm, summed_two, vector_rows[4], vector_rows[5])
    grad_two, grad_gain_two, grad_shift_two = norm_two_back(cotangent.astype(f32))
    grad_branch = grad_two.astype(bf16)
    down_grad = dot(grad_branch, hidden, 0, 0).astype(bf16)
    down_part = lax.psum_scatter(down_grad, "dp", scatter_dimension=0, tiled=True)
    grad_hidden = dot(grad_branch, down_all, 1, 0).reshape(tokens, n_tensor, hidden_cols)
    grad_gate, grad_up = gated_back(grad_hidden)
    grad_glu = (
        jnp.stack([grad_gate, grad_up], axis=2)
        .astype(bf16)
        .reshape(tokens, 2 * n_tensor * hidden_cols)
    )
    glu_grad = dot(normed_low, grad_glu, 0, 0).astype(bf16)
    glu_part = lax.psum_scatter(glu_grad, "dp", scatter_dimension=0, tiled=True)
    grad_normed = grad_two + dot(grad_glu, glu_all, 1, 1)
    grad_one, grad_gain_one, grad_shift_one = norm_one_back(grad_normed)
    grad_attn = grad_one.astype(bf16)
    out_grad = dot(grad_attn, attended, 0, 1).astype(bf16)
    out_part = lax.psum_scatter(out_grad, "dp", scatter_dimension=0, tiled=True)
    grad_attended = dot(out_all, grad_attn, 0, 1).astype(bf16)
    vector_part = jnp.stack(
        [
            jnp.sum(grad_one, axis=0),
            grad_gain_one,
            grad_shift_one,
            jnp.sum(grad_two, axis=0),
            grad_gain_two,
            grad_shift_two,
        ]
    )
    vector_all = lax.psum(vector_part, ("dp", "tensor"))
    slice_width = vector_mom.shape[2]
    vector_sum = lax.dynamic_slice_in_dim(
        vector_all, (lax.axis_index("dp") * n_tensor + tensor_pos) * slice_width, slice_width, 1
    )
    late_parts = jnp.concatenate(
        [
            out_part.reshape(rows, n_tensor, head_cols),
            glu_part.reshape(rows, n_tensor, 2 * hidden_cols),
            down_part.reshape(rows, n_tensor, hidden_cols),
        ],
        axis=2,
    )
    late_sum = lax.psum_scatter(late_parts, "tensor", scatter_dimension=1, tiled=True)[:, 0].astype(f32)
    out_sum = late_sum[:, :head_cols].T
    glu_sum = (
        late_sum[:, head_cols : head_cols + 2 * hidden_cols]
        .reshape(rows, 2, hidden_cols)
        .transpose(1, 0, 2)
    )
    down_sum = late_sum[:, head_cols + 2 * hidden_cols :].T

    grad_heads = lax.all_to_all(
        grad_attended, "tensor", split_axis=0, concat_axis=1, tiled=True
    ).reshape(head_count, HEAD, length)
    grad_qkv = attention_backward(parts, qkv, grad_heads, out_t, lse).reshape(3 * head_cols, length)
    attn_grad = dot(inputs_full, grad_qkv, 0, 1)
    qv_grad = jnp.sum(grad_qkv.reshape(head_count, 3, HEAD, length).astype(f32), axis=3)
    qv_grad = jnp.stack([qv_grad[:, 0], qv_grad[:, 2]]).reshape(2, n_dp, qv_cols)
    qv_grad = jnp.pad(
        qv_grad.transpose(1, 0, 2).reshape(n_dp, 2 * qv_cols), ((0, 0), (0, rows - 2 * qv_cols))
    ).reshape(width, 1)
    attn_part = jnp.concatenate([attn_grad, qv_grad, jnp.zeros((width, 63), f32)], axis=1)
    attn_part = lax.psum_scatter(attn_part.astype(bf16), "dp", scatter_dimension=0, tiled=True)
    attn_part = attn_part.astype(f32)
    attn_sum = (
        attn_part[:, : 3 * head_cols]
        .reshape(rows, head_count, 3, HEAD)
        .transpose(2, 0, 1, 3)
        .reshape(3, rows, head_cols)
    )
    qv_sum = attn_part[: 2 * qv_cols, 3 * head_cols].reshape(2, qv_cols)

    grad_tokens = lax.all_to_all(grad_qkv, "tensor", split_axis=1, concat_axis=0, tiled=True)
    input_grad = grad_one + dot(grad_tokens, attn_all, 0, 1)

    vector_own = lax.dynamic_slice_in_dim(vectors, tensor_pos * slice_width, slice_width, 1)
    owned_parts = (attn_w, out_w, glu_w, down_w, qv_bias, vector_own)
    gradients = (attn_sum, out_sum, glu_sum, down_sum, qv_sum, vector_sum)
    moments = (attn_mom, out_mom, glu_mom, down_mom, qv_mom, vector_mom)
    stack_flags = (True, False, True, False, True, True)
    new_moments = []
    directions = []
    for weight, gradient, moment in zip(owned_parts, gradients, moments):
        pair, direction = lamb_terms(weight, gradient, moment)
        new_moments.append(pair)
        directions.append(direction)
    weight_sums = jnp.concatenate([piece_sums(w, f) for w, f in zip(owned_parts, stack_flags)])
    dir_sums = jnp.concatenate([piece_sums(r, f) for r, f in zip(directions, stack_flags)])
    totals = lax.psum(jnp.stack([weight_sums, dir_sums]), ("dp", "tensor"))
    norm_values = jnp.sqrt(totals + 1e-12)
    ratios = norm_values[0] / norm_values[1]
    new_weights = []
    offset = 0
    for weight, direction, stacked in zip(owned_parts, directions, stack_flags):
        amount = weight.shape[0] if stacked else 1
        factor = ratios[offset : offset + amount]
        if stacked:
            factor = factor.reshape((amount,) + (1,) * (weight.ndim - 1))
        else:
            factor = factor[0]
        new_weights.append(weight - learn_rate * factor * direction)
        offset = offset + amount
    return (
        output.astype(bf16),
        input_grad,
        *gradients,
        *new_moments,
        *new_weights,
        norm_values,
        ratios,
    )


def solution(mesh):
    tokens = P(("dp", "tensor"), None)
    attn = P(None, "dp", "tensor")
    cols = P("tensor", "dp")
    moments = (
        P(None, None, "dp", "tensor"),
        P(None, "tensor", "dp"),
        P(None, None, "dp", "tensor"),
        P(None, "tensor", "dp"),
        P(None, None, ("tensor", "dp")),
        P(None, None, ("dp", "tensor")),
    )
    weights = (attn, cols, attn, cols, P(None, ("tensor", "dp")))
    split = P(None, ("dp", "tensor"))
    return jax.shard_map(
        functools.partial(local, n_dp=mesh.shape["dp"], n_tensor=mesh.shape["tensor"]),
        mesh=mesh,
        in_specs=(tokens, tokens, *weights, P(None, "dp"), *moments),
        out_specs=(tokens, tokens, *weights, split, *moments, *weights, split, P(), P()),
        check_vma=False,
    )
```

time: 1210 us -> 758 us (0.63)
  waiting for transfers between devices: 513 us -> 274 us
  matrix products: 262 us -> 77.6 us
  Pallas kernels: 0 us -> 67.4 us
  blocking collectives: 146 us -> 90.1 us
  local copies, waits for them, and re-layouts: 154 us -> 108 us
  starting transfers between devices: 1.39 us -> 13.6 us
    reduce_scatter x5 -> x4, waiting for transfers between devices: 316 us -> 93.4 us  [the longest x1 72.3 us: local(): glu_part = lax.psum_scatter(glu_grad, 'dp', scatter_dimension=0, tiled=True)]
    dot_general x95 -> x12, matrix products: 258 us -> 77.6 us  [dot(): lax.dot_general(a, b, (((ca,), (cb,)), ((), ())), preferred_element_type=...]
    pallas_call x0 -> x2, Pallas kernels: none -> 67.4 us  [the longest x1 42.2 us: attention_backward(): pl.pallas_call(functools.partial(bwd_kernel, heads=heads, length=length,...]
    all_gather x5, waiting for transfers between devices: 166 us -> 99.5 us  [the longest x1 52.1 us: local(): lax.all_gather(jnp.concatenate([out_rows, glu_rows, down_rows, attn_rows]...]
    unnamed x2 -> x0, blocking collectives: 55.2 us -> none
    while x225 -> x0, local copies, waits for them, and re-layouts: 48.1 us -> none
    psum x0 -> x1, blocking collectives: none -> 39.6 us  [local(): vector_all = lax.psum(vector_part, ('dp', 'tensor'))]
    all_to_all x0 -> x3, waiting for transfers between devices: none -> 36.1 us  [the longest x1 20.2 us: local(): lax.all_to_all(grad_attended, 'tensor', split_axis=0, concat_axis=1, tile...]
  transfers between devices with their start and end apart: 14 -> 14, of which waited for: 7 -> 8; matrix products, arithmetic and copies ran while one was open for 24% -> 24% of each run, Pallas kernels for 0% -> 9%
where the time goes in v1:
time: 758 us; the launch traced here: 752 us
  waiting for transfers between devices  274 us (36%)
  local copies, waits for them, and re-layouts  108 us (14%)
  other arithmetic  105 us (14%)
  blocking collectives  90.1 us (12%)
  matrix products  77.6 us (10%)
  Pallas kernels  67.4 us (9%)
  between operations  16.4 us (2%)
  starting transfers between devices  13.6 us (2%)
    dot_general x12, matrix products, dot(): lax.dot_general(a, b, (((ca,), (cb,)), ((), ())), preferred_element_type=...  77.6 us
    reduce_scatter x1, waiting for transfers between devices, local(): glu_part = lax.psum_scatter(glu_grad, 'dp', scatter_dimension=0, tiled=True)  72.3 us
    all_gather x1, waiting for transfers between devices, local(): lax.all_gather(jnp.concatenate([out_rows, glu_rows, down_rows, attn_rows]...  52.1 us
    all_gather x4, waiting for transfers between devices, local(): gathered.append(lax.all_gather(mine, 'dp', axis=0, tiled=True))  47.4 us
    all_gather x1, waiting for transfers between devices, local(): inputs_full = lax.all_gather(inputs, 'tensor', axis=0, tiled=True)  44 us
    pallas_call x1, Pallas kernels, attention_backward(): pl.pallas_call(functools.partial(bwd_kernel, heads=heads, length=length,...  42.2 us
    psum x1, blocking collectives, local(): vector_all = lax.psum(vector_part, ('dp', 'tensor'))  39.6 us
    psum x1, blocking collectives, local(): totals = lax.psum(jnp.stack([weight_sums, dir_sums]), ('dp', 'tensor'))  39.5 us
  transfers between devices with their start and end apart: 14, of which 8 were waited for; matrix products, arithmetic and copies ran while one was open for 24% of the time, Pallas kernels for 9%

profile of v1, /device:TPU:0, one launch (start us, length us, event | category | flops | bytes accessed | tf_op | source)
XLA Modules:
  0.0 752.1 jit_solution(12833079341343521541)
XLA Ops:
  15.4 52.1 %all-gather.18.cloned.1.call-done = bf16[384,3072]{1,0:T(8,128)(2,1)} async-done(((bf16[96,3072]{1,0:T(8,128)(2,1)}), bf16[384,3072]{1,0:T(8,128)(2,1)}) %all-gather.18.cloned.1.call-update) | async-done | bytes 2359312 | tf_op jit(solution)/shard_map/all_gather | solution.py:347
  74.6 11.0 %all_gather.24 = bf16[768,640]{1,0:T(8,128)(2,1)S(1)} all-gather(bf16[96,640]{1,0:T(8,128)(2,1)S(1)} %copy.234), channel_id=1, replica_groups=mesh['dp'=8,'tensor'=4] {'dp'}, dimensions={0}, use_global_device_ids=true | all-gather | bytes 1105920 | tf_op jit(solution)/shard_map/all_gather | solution.py:327
  87.3 44.0 %all-gather.8.cloned.1.call-done = bf16[2048,768]{1,0:T(8,128)(2,1)} async-done(((bf16[512,768]{1,0:T(8,128)(2,1)}), bf16[2048,768]{1,0:T(8,128)(2,1)}) %all-gather.8.cloned.1.call-update) | async-done | bytes 3145744 | tf_op jit(solution)/shard_map/all_gather | solution.py:344
  131.3 4.5 fusion.24.qkv_ref
  135.8 25.2 %attention_forward.1 = (bf16[3,64,2048]{2,1,0:T(8,128)(2,1)S(1)}, f32[3,1,2048]{2,1,0:T(1,128)S(1)}) custom-call(f32[3,3]{1,0:T(4,128)S(1)} %constant_dynamic-slice_fusion.1.parts_ref, bf16[2048,576]{1,0:T(8,128)(2,1)S(1)} %fusion.24.qkv_ref), custom_call_target="tpu_custom_call" | custom-call | flops 12884901888 | bytes 4718592 | tf_op jit(solution)/shard_map/attention_forward/pallas_call | solution.py:129
  162.6 3.5 all-to-all-start
  170.4 15.9 %all-to-all-done = bf16[192,4,512]{2,0,1:T(8,128)(2,1)S(1)} async-done(((bf16[192,4,512]{2,0,1:T(8,128)(2,1)}), bf16[192,4,512]{2,0,1:T(8,128)(2,1)S(1)}, u32[]{:S(2)}, u32[]{:S(2)}) %all-to-all-start) | async-done | bytes 786464 | tf_op jit(solution)/shard_map/all_to_all | solution.py:360
  187.2 3.0 fusion.76
  190.6 26.9 %all-gather.12.cloned.1.call-done = bf16[768,6144]{1,0:T(8,128)(2,1)} async-done(((bf16[96,6144]{1,0:T(8,128)(2,1)}), bf16[768,6144]{1,0:T(8,128)(2,1)}) %all-gather.12.cloned.1.call-update) | async-done | bytes 9437200 | tf_op jit(solution)/shard_map/all_gather | solution.py:354
  217.4 14.6 %fusion.66 = f32[512,6144]{0,1:T(8,128)} fusion(bf16[768,6144]{1,0:T(8,128)(2,1)} %all-gather.12.cloned.1.call-done, f32[512,768]{1,0:T(8,128)S(1)} %get-tuple-element.253, f32[768]{0:T(1024)S(1)} %get-tuple-element.189, f32[768]{0:T(1024)S(1)} %get-tuple-element.190, f32[512]{0:T(512)S(1)} %fusion.55, f32[512]{0:T(512)S(1)} %broadcast_multiply_fusion.2), kind=kOutput, calls=%fused_computation.213 | convolution fusion | flops 4833804288 | bytes 23603200 | tf_op jit(solution)/shard_map/dot_general | solution.py:26
  232.0 10.9 %fusion.72 = (f32[512,4,1,768]{0,3,2,1:T(8,128)}, f32[512,4,1,768]{0,3,2,1:T(8,128)}) fusion(f32[512,4,2,768]{0,3,2,1:T(8,128)} %bitcast.281), kind=kLoop, calls=%fused_computation.216 | loop fusion | bytes 25165824 | tf_op jit(solution)/shard_map/slice | solution.py:367
  243.0 6.6 copy.285
  249.6 8.6 %broadcast_multiply_fusion = (f32[512,4,1,768]{3,0,2,1:T(8,128)}, f32[512,4,1,768]{3,0,2,1:T(8,128)}) fusion(f32[512,4,1,768]{3,0,2,1:T(8,128)} %copy.285), kind=kLoop, calls=%fused_computation.44 | loop fusion | flops 4718592 | bytes 18874368 | tf_op jit(solution)/shard_map/jvp()/mul | solution.py:49
  258.2 6.5 copy.247
  264.7 6.5 copy.246
  271.3 6.5 copy.286
  277.8 16.6 %fusion.3 = bf16[512,3072]{0,1:T(8,128)(2,1)} fusion(f32[512,4,1,768]{0,3,2,1:T(8,128)} %get-tuple-element.218, f32[512,4,1,768]{0,3,1,2:T(8,128)} %copy.247, f32[512,4,1,768]{0,3,1,2:T(8,128)} %copy.246), kind=kLoop, calls=%fused_computation.6 | loop fusion | flops 99090432 | bytes 22020096 | tf_op jit(solution)/shard_map/convert_element_type | solution.py:368
  294.4 6.5 fusion.77
  303.6 4.7 fusion.64
  308.3 6.7 copy.252
  315.0 17.5 %add_convert_fusion = (bf16[512,4,1,768]{3,0,2,1:T(8,128)(2,1)S(1)}, f32[512,4,1,768]{3,0,2,1:T(8,128)}) fusion(f32[512,4,1,768]{3,0,2,1:T(8,128)} %copy.252, f32[512,4,1,768]{3,0,2,1:T(8,128)} %copy.286, f32[512,4,1,768]{3,0,2,1:T(8,128)} %copy.285), kind=kLoop, calls=%fused_computation.15 | loop fusion | flops 114819072 | bytes 28311552 | tf_op jit(solution)/shard_map/convert.19
  332.4 9.5 %multiply_convert_fusion = bf16[512,4,1,768]{3,0,2,1:T(8,128)(2,1)} fusion(f32[512,4,1,768]{3,0,2,1:T(8,128)} %copy.252, f32[512,4,1,768]{3,0,2,1:T(8,128)} %get-tuple-element.214, f32[512,4,1,768]{3,0,2,1:T(8,128)} %copy.285), kind=kLoop, calls=%fused_computation.14 | loop fusion | flops 6291456 | bytes 22020096 | tf_op jit(solution)/shard_map/convert.20
  341.9 5.1 pad_maximum_fusion
  347.0 8.7 %copy.254 = bf16[512,4,2,768]{0,3,2,1:T(8,128)(2,1)} copy(bf16[512,4,2,768]{3,0,2,1:T(8,128)(2,1)} %pad_maximum_fusion) | data formatting | bytes 12582912 | tf_op jit(solution)/shard_map/stack | solution.py:378
  355.8 11.2 %multiply_reduce_fusion = (f32[768]{0:T(1024)S(1)}, f32[512]{0:T(512)S(1)}, f32[768]{0:T(1024)S(1)}, f32[512,768]{1,0:T(8,128)S(1)}) fusion(f32[512,768]{1,0:T(8,128)} %copy-done.5, f32[512]{0:T(512)S(1)} %fusion.55, f32[512]{0:T(512)S(1)} %broadcast_multiply_fusion.2, f32[768]{0:T(1024)S(1)} %get-tuple-element.190, bf16[512,6144]{0,1:T(8,128)(2,1)} %bitcast.282, ...), kind=kOutput, calls=%fused_computation.55 | convolution fusion | flops 4835768320 | bytes 20464640 | tf_op jit(solution)/shard_map/dot_general | solution.py:26
  369.7 7.4 convolution_convert_fusion.1
  377.2 10.7 %convolution_convert_fusion = bf16[768,6144]{1,0:T(8,128)(2,1)} fusion(bf16[512,6144]{0,1:T(8,128)(2,1)} %bitcast.283, f32[512,768]{1,0:T(8,128)} %copy-done.5, f32[768]{0:T(1024)S(1)} %get-tuple-element.189, f32[768]{0:T(1024)S(1)} %get-tuple-element.190, f32[512]{0:T(512)S(1)} %fusion.55, f32[512]{0:T(512)S(1)} %broadcast_multiply_fusion.2), kind=kOutput, calls=%fused_computation | convolution fusion | flops 4838522880 | bytes 17311744 | tf_op jit(solution)/shard_map/dot_general | solution.py:26
  387.9 3.1 convolution_convert_fusion.4
  391.0 4.6 all-to-all-start.1
  395.9 20.2 %all-to-all-done.1 = bf16[4,192,512]{2,1,0:T(8,128)(2,1)S(1)} async-done(((bf16[4,192,512]{2,1,0:T(8,128)(2,1)}), bf16[4,192,512]{2,1,0:T(8,128)(2,1)S(1)}, u32[]{:S(2)}, u32[]{:S(2)}) %all-to-all-start.1) | async-done | bytes 786464 | tf_op jit(solution)/shard_map/all_to_all | solution.py:422
  419.3 42.2 %attention_backward.1 = bf16[3,3,64,2048]{3,2,1,0:T(8,128)(2,1)S(1)} custom-call(f32[3,3]{1,0:T(4,128)S(1)} %constant_dynamic-slice_fusion.1.parts_ref, bf16[2048,576]{1,0:T(8,128)(2,1)} %copy-done.1, bf16[3,64,2048]{2,1,0:T(8,128)(2,1)S(1)} %copy-done, bf16[3,64,2048]{2,1,0:T(8,128)(2,1)S(1)} %get-tuple-element.24.ot_ref, ...), custom_call_target="tpu_custom_call" | custom-call | flops 32212254720 | bytes 9437184 | tf_op jit(solution)/shard_map/attention_backward/pallas_call | solution.py:236
  462.3 3.9 fusion.29
  467.4 2.2 copy.281
  472.1 72.3 %reduce-scatter.10.cloned.1.call-done = bf16[96,6144]{1,0:T(8,128)(2,1)} async-done(((bf16[768,6144]{1,0:T(8,128)(2,1)}), bf16[96,6144]{1,0:T(8,128)(2,1)}) %reduce-scatter.10.cloned.1.call-update) | async-done | bytes 1179664 | tf_op jit(solution)/shard_map/reduce_scatter | solution.py:383
  544.4 2.4 copy.324
  546.8 4.3 concatenate.24
  560.7 39.6 %psum.14 = f32[6,768]{1,0:T(8,128)S(1)} all-reduce(f32[6,768]{1,0:T(8,128)S(1)} %stack.91), channel_id=1, replica_groups=mesh['dp'=8,'tensor'=4] {'dp','tensor'}, use_global_device_ids=true, to_apply=%region_20.21 | all-reduce | flops 4608 | bytes 36864 | tf_op jit(solution)/shard_map/psum | solution.py:400
  601.0 3.0 all_to_all.47
  604.0 3.5 copy.256
  607.6 4.6 all-to-all-start.2
  620.1 2.5 multiply_reduce_fusion.7
  622.5 21.1 %reduce-scatter.14.cloned.1.call-done = bf16[96,1,2496]{2,0,1:T(8,128)(2,1)} async-done(((bf16[96,4,2496]{2,0,1:T(8,128)(2,1)}), bf16[96,1,2496]{2,0,1:T(8,128)(2,1)}) %reduce-scatter.14.cloned.1.call-update) | async-done | bytes 479248 | tf_op jit(solution)/shard_map/reduce_scatter | solution.py:413
  646.5 2.4 multiply_reduce_fusion.10
  649.0 2.7 multiply_reduce_fusion.6
  651.7 3.0 multiply_reduce_fusion.4
  659.2 20.5 %all-gather.16.cloned.1.call-done = bf16[768,2304]{1,0:T(8,128)(2,1)} async-done(((bf16[96,2304]{1,0:T(8,128)(2,1)}), bf16[768,2304]{1,0:T(8,128)(2,1)}) %all-gather.16.cloned.1.call-update) | async-done | bytes 3538960 | tf_op jit(solution)/shard_map/all_gather | solution.py:354
  679.7 6.0 convolution_add_fusion.1
  685.7 39.5 %psum.15 = f32[2,15]{1,0:T(2,128)S(1)} all-reduce(f32[2,15]{1,0:T(2,128)} %pad_maximum_fusion.8), channel_id=1, replica_groups=mesh['dp'=8,'tensor'=4] {'dp','tensor'}, use_global_device_ids=true, to_apply=%region_33.34 | all-reduce | flops 30 | bytes 240 | tf_op jit(solution)/shard_map/psum | solution.py:459
  (232 shorter events, 81.2 us)
Async XLA Ops:
  7.2 60.3 %all-gather.18.cloned.1.call-start = ((), (), s32[]{:S(2)}) async-start(), calls=%async_computation.17 | async-start | bytes 2949120 | tf_op jit(solution)/shard_map/all_gather | solution.py:347
  8.3 65.1 %copy-start.8 = (f32[3,96,192]{1,2,0:T(8,128)}, f32[3,96,192]{1,2,0:T(8,128)S(1)}, u32[]{:S(2)}) copy-start(f32[3,96,192]{1,2,0:T(8,128)S(1)} %copy.232) | copy-start | bytes 663556
  13.2 60.3 %copy-start.23 = (f32[2,24]{1,0:T(2,128)S(1)}, f32[2,24]{1,0:T(2,128)}, u32[]{:S(2)}) copy-start(f32[2,24]{1,0:T(2,128)} %param.21) | copy-start | bytes 580
  13.2 61.1 %copy-start.20 = (f32[6,96]{1,0:T(8,128)S(1)}, f32[6,96]{1,0:T(8,128)}, u32[]{:S(2)}) copy-start(f32[6,96]{1,0:T(8,128)} %param.22) | copy-start | bytes 6916
  14.6 116.7 %all-gather.8.cloned.1.call-start = ((), (), s32[]{:S(2)}) async-start(), calls=%async_computation.8 | async-start | bytes 3932160 | tf_op jit(solution)/shard_map/all_gather | solution.py:344
  15.4 155.0 %all-gather.10.cloned.1.call-start = ((), (), s32[]{:S(2)}) async-start(), calls=%async_computation.9 | async-start | bytes 1327104 | tf_op jit(solution)/shard_map/all_gather | solution.py:354
  69.5 147.9 %all-gather.12.cloned.1.call-start = ((), (), s32[]{:S(2)}) async-start(), calls=%async_computation.10 | async-start | bytes 10616832 | tf_op jit(solution)/shard_map/all_gather | solution.py:354
  135.8 25.2 %copy-start.1 = (bf16[2048,576]{1,0:T(8,128)(2,1)}, bf16[2048,576]{1,0:T(8,128)(2,1)S(1)}, u32[]{:S(2)}) copy-start(bf16[2048,576]{1,0:T(8,128)(2,1)S(1)} %fusion.24.qkv_ref) | copy-start | bytes 7077892
  161.0 26.2 %copy-start.16 = (bf16[512,768]{1,0:T(8,128)(2,1)S(1)}, bf16[512,768]{1,0:T(8,128)(2,1)}, u32[]{:S(2)}) copy-start(bf16[512,768]{1,0:T(8,128)(2,1)} %param.15) | copy-start | bytes 2359300
  162.6 23.7 %all-to-all-start = ((bf16[192,4,512]{2,0,1:T(8,128)(2,1)}), bf16[192,4,512]{2,0,1:T(8,128)(2,1)S(1)}, u32[]{:S(2)}, u32[]{:S(2)}) async-start(bf16[192,4,512]{2,0,1:T(8,128)(2,1)} %copy.238), calls=%async_computation | async-start | bytes 1572864 | tf_op jit(solution)/shard_map/all_to_all | solution.py:360
  166.2 128.2 %all-gather.14.cloned.1.call-start = ((), (), s32[]{:S(2)}) async-start(), calls=%async_computation.11 | async-start | bytes 5308416 | tf_op jit(solution)/shard_map/all_gather | solution.py:354
  169.0 300.8 %reduce-scatter.8.cloned.1.call-start = ((), (), s32[]{:S(2)}) async-start(), calls=%async_computation.13 | async-start | bytes 1327104 | tf_op jit(solution)/shard_map/reduce_scatter | solution.py:388
  186.3 0.9 copy-start.17
  190.2 104.2 %copy-start.5 = (f32[512,768]{1,0:T(8,128)}, f32[512,768]{1,0:T(8,128)S(1)}, u32[]{:S(2)}) copy-start(f32[512,768]{1,0:T(8,128)S(1)} %get-tuple-element.253) | copy-start | bytes 4718596
  294.4 9.2 %slice-start = ((s8[4718592]{0:T(1024)(128)(4,1)}), s8[4194304]{0:T(1024)(128)(4,1)S(1)}, s32[]{:S(2)}) async-start(s8[4718592]{0:T(1024)(128)(4,1)} %bitcast.314), calls=%async_computation.19 | async-start | bytes 8388608
  294.4 6.8 copy-start.10
  294.4 9.2 %slice-start.1 = ((s8[4718592]{0:T(1024)(128)(4,1)}), s8[524288]{0:T(1024)(128)(4,1)S(1)}, s32[]{:S(2)}) async-start(s8[4718592]{0:T(1024)(128)(4,1)} %bitcast.314), calls=%async_computation.20 | async-start | bytes 1048576
  303.6 52.2 %copy-start.4 = (f32[512,768]{1,0:T(8,128)}, f32[512,768]{1,0:T(8,128)S(1)}, u32[]{:S(2)}) copy-start(f32[512,768]{1,0:T(8,128)S(1)} %get-tuple-element.216) | copy-start | bytes 4718596
  355.7 11.2 %copy-start.6 = (f32[512,768]{1,0:T(8,128)S(1)}, f32[512,768]{1,0:T(8,128)}, u32[]{:S(2)}) copy-start(f32[512,768]{1,0:T(8,128)} %copy-done.5) | copy-start | bytes 4718596
  355.7 11.9 %copy-start.18 = (bf16[192,4,512]{2,0,1:T(8,128)(2,1)S(1)}, bf16[192,4,512]{2,0,1:T(8,128)(2,1)}, u32[]{:S(2)}) copy-start(bf16[192,4,512]{2,0,1:T(8,128)(2,1)} %copy-done.17) | copy-start | bytes 2359300
  367.6 20.3 %copy-start.2 = (f32[512,768]{1,0:T(8,128)}, f32[512,768]{1,0:T(8,128)S(1)}, u32[]{:S(2)}) copy-start(f32[512,768]{1,0:T(8,128)S(1)} %get-tuple-element.212) | copy-start | bytes 4718596
  367.6 189.7 %copy-start.25 = (f32[512]{0:T(512)}, f32[512]{0:T(512)S(1)}, u32[]{:S(2)}) copy-start(f32[512]{0:T(512)S(1)} %negate_multiply_fusion.1) | copy-start | bytes 6148
  369.6 101.3 %reduce-scatter.12.cloned.1.call-start = ((), (), s32[]{:S(2)}) async-start(), calls=%async_computation.15 | async-start | bytes 5308416 | tf_op jit(solution)/shard_map/reduce_scatter | solution.py:374
  377.1 167.2 %reduce-scatter.10.cloned.1.call-start = ((), (), s32[]{:S(2)}) async-start(), calls=%async_computation.14 | async-start | bytes 10616832 | tf_op jit(solution)/shard_map/reduce_scatter | solution.py:383
  391.0 25.1 %all-to-all-start.1 = ((bf16[4,192,512]{2,1,0:T(8,128)(2,1)}), bf16[4,192,512]{2,1,0:T(8,128)(2,1)S(1)}, u32[]{:S(2)}, u32[]{:S(2)}) async-start(bf16[4,192,512]{2,1,0:T(8,128)(2,1)} %bitcast.24), calls=%async_computation.1 | async-start | bytes 1572864 | tf_op jit(solution)/shard_map/all_to_all | solution.py:422
  395.6 217.3 %reduce-scatter.16.cloned.1.call-start = ((), (), s32[]{:S(2)}) async-start(), calls=%async_computation.18 | async-start | bytes 1105920
  418.1 1.2 copy-start
  469.7 173.9 %reduce-scatter.14.cloned.1.call-start = ((), (), s32[]{:S(2)}) async-start(), calls=%async_computation.16 | async-start | bytes 2457600 | tf_op jit(solution)/shard_map/reduce_scatter | solution.py:413
  546.8 10.5 %copy-start.28 = (f32[2,6,24]{2,0,1:T(2,128)S(1)}, f32[2,6,24]{2,0,1:T(2,128)}, u32[]{:S(2)}) copy-start(f32[2,6,24]{2,0,1:T(2,128)} %param.28) | copy-start | bytes 3460
  551.1 49.2 %copy-start.21 = (f32[6,96]{1,0:T(8,128)S(1)}, f32[6,96]{1,0:T(8,128)}, u32[]{:S(2)}) copy-start(f32[6,96]{1,0:T(8,128)} %param.22) | copy-start | bytes 6916
  551.1 128.6 %all-gather.16.cloned.1.call-start = ((), (), s32[]{:S(2)}) async-start(), calls=%async_computation.12 | async-start | bytes 3981312 | tf_op jit(solution)/shard_map/all_gather | solution.py:354
  555.5 59.4 %copy-start.12 = (f32[1,3,96,192]{2,3,1,0:T(8,128)}, f32[1,3,96,192]{2,3,1,0:T(8,128)S(1)}, u32[]{:S(2)}) copy-start(f32[1,3,96,192]{2,3,1,0:T(8,128)S(1)} %copy.290) | copy-start | bytes 663556
  601.0 11.2 %copy-start.22 = (f32[6,24]{1,0:T(8,128)}, f32[6,24]{1,0:T(8,128)S(1)}, u32[]{:S(2)}) copy-start(f32[6,24]{1,0:T(8,128)S(1)} %get-tuple-element.198) | copy-start | bytes 1732
  607.5 10.7 %copy-start.27 = (f32[2,2,24]{2,1,0:T(2,128)S(1)}, f32[2,2,24]{2,1,0:T(2,128)}, u32[]{:S(2)}) copy-start(f32[2,2,24]{2,1,0:T(2,128)} %param.27) | copy-start | bytes 1156
  607.6 11.3 %copy-start.24 = (f32[2,24]{1,0:T(2,128)S(1)}, f32[2,24]{1,0:T(2,128)}, u32[]{:S(2)}) copy-start(f32[2,24]{1,0:T(2,128)} %param.21) | copy-start | bytes 580
  607.6 12.5 %copy-start.9 = (f32[3,96,192]{1,2,0:T(8,128)S(1)}, f32[3,96,192]{1,2,0:T(8,128)}, u32[]{:S(2)}) copy-start(f32[3,96,192]{1,2,0:T(8,128)} %copy-done.8) | copy-start | bytes 663556
  607.6 72.2 %all-to-all-start.2 = ((bf16[576,4,512]{2,0,1:T(8,128)(2,1)}), bf16[576,4,512]{2,0,1:T(8,128)(2,1)}, u32[]{:S(2)}, u32[]{:S(2)}) async-start(bf16[576,4,512]{2,0,1:T(8,128)(2,1)} %copy.256), calls=%async_computation.2 | async-start | bytes 4718592 | tf_op jit(solution)/shard_map/all_to_all | solution.py:443
  613.9 37.8 %copy-start.7 = (f32[2,96,768]{2,1,0:T(8,128)S(1)}, f32[2,96,768]{2,1,0:T(8,128)}, u32[]{:S(2)}) copy-start(f32[2,96,768]{2,1,0:T(8,128)} %param.19) | copy-start | bytes 1769476
  615.0 29.7 %copy-start.31 = (f32[2,24]{1,0:T(2,128)}, f32[2,24]{1,0:T(2,128)S(1)}, u32[]{:S(2)}) copy-start(f32[2,24]{1,0:T(2,128)S(1)} %reshape_squeeze.9) | copy-start | bytes 580
  615.1 64.6 %copy-start.3 = (f32[512,768]{1,0:T(8,128)S(1)}, f32[512,768]{1,0:T(8,128)}, u32[]{:S(2)}) copy-start(f32[512,768]{1,0:T(8,128)} %copy-done.2) | copy-start | bytes 4718596
  615.1 64.6 %copy-start.26 = (f32[512]{0:T(512)S(1)}, f32[512]{0:T(512)}, u32[]{:S(2)}) copy-start(f32[512]{0:T(512)} %copy-done.25) | copy-start | bytes 6148
  679.7 49.7 %copy-start.13 = (f32[2,768,96]{1,2,0:T(8,128)S(1)}, f32[2,768,96]{1,2,0:T(8,128)}, u32[]{:S(2)}) copy-start(f32[2,768,96]{1,2,0:T(8,128)} %param.26) | copy-start | bytes 1769476
  679.7 54.8 %copy-start.19 = (f32[1,192,96]{2,1,0:T(8,128)S(1)}, f32[1,192,96]{2,1,0:T(8,128)}, u32[]{:S(2)}) copy-start(f32[1,192,96]{2,1,0:T(8,128)} %get-tuple-element.234) | copy-start | bytes 221188
  685.7 53.4 %copy-start.15 = (f32[192,96]{1,0:T(8,128)S(1)}, f32[192,96]{1,0:T(8,128)}, u32[]{:S(2)}) copy-start(f32[192,96]{1,0:T(8,128)} %param.18) | copy-start | bytes 221188
  685.7 56.1 %copy-start.11 = (f32[768,96]{0,1:T(8,128)S(1)}, f32[768,96]{0,1:T(8,128)}, u32[]{:S(2)}) copy-start(f32[768,96]{0,1:T(8,128)} %param.20) | copy-start | bytes 884740
  685.7 56.1 %copy-start.14 = (f32[768,96]{0,1:T(8,128)S(1)}, f32[768,96]{0,1:T(8,128)}, u32[]{:S(2)}) copy-start(f32[768,96]{0,1:T(8,128)} %get-tuple-element.202) | copy-start | bytes 884740
  725.2 2.5 copy-start.30
  727.7 14.9 %copy-start.29 = (f32[2,24]{1,0:T(2,128)S(1)}, f32[2,24]{1,0:T(2,128)}, u32[]{:S(2)}) copy-start(f32[2,24]{1,0:T(2,128)} %get-tuple-element.200) | copy-start | bytes 580
Sparse Core Ops, SparseCore 0:
  14.8 52.6 all-gather.17
  69.1 62.1 all-gather.7
  133.8 22.5 all-gather.9
  158.7 58.7 all-gather.11
  219.7 38.7 all-gather.13
  369.8 36.9 reduce-scatter.7
  410.2 53.7 reduce-scatter.11
  467.5 76.8 reduce-scatter.9
  547.6 35.7 reduce-scatter.15
  585.6 57.9 reduce-scatter.13
  646.1 33.5 all-gather.15

commit v2 on v1

--- a/solution.py
+++ b/solution.py
@@ -9,6 +9,7 @@
 from jax.experimental.pallas import tpu as pltpu
 from jax.sharding import PartitionSpec as P
 
+
 HEADS = 12
 HEAD = 64
 BLOCK = 256
@@ -17,6 +18,7 @@
 learn_rate = 0.2
 decay_rate = 0.01
 moment_eps = 1e-06
+
 
 bf16 = jnp.bfloat16
 f32 = jnp.float32
@@ -37,16 +39,6 @@
         parts.append(part)
         rest = rest - part
     return np.stack(parts, axis=1)
-
-
-def layer_norm(tensor_in, gain_row, shift_row):
-    center = tensor_in - jnp.mean(tensor_in, axis=-1, keepdims=True)
-    spread = jnp.mean(center * center, axis=-1, keepdims=True)
-    return center * lax.rsqrt(spread + norm_eps) * gain_row + shift_row
-
-
-def gated(gate_val, up_val):
-    return jax.nn.gelu(gate_val, approximate=False) * up_val
 
 
 def pos_features(length, parts):
@@ -260,6 +252,584 @@
     )(parts, qkv, grad_t, out_t, lse)
 
 
+def normed(z):
+    center = z - jnp.mean(z, axis=1, keepdims=True)
+    scale = lax.rsqrt(jnp.mean(center * center, axis=1, keepdims=True) + norm_eps)
+    return center * scale, scale
+
+
+def norm_back(grad, unit, scale, gain):
+    inner = grad * gain
+    mean = jnp.mean(inner, axis=1, keepdims=True)
+    return scale * (inner - mean - unit * jnp.mean(inner * unit, axis=1, keepdims=True))
+
+
+def ff_kernel(
+    att_ref,
+    x_ref,
+    cot_ref,
+    vec_ref,
+    wall_ref,
+    out_ref,
+    dz1_ref,
+    do_ref,
+    dvec_ref,
+    gglu_ref,
+    grest_ref,
+    wgu_s,
+    wd_s,
+    wo_s,
+    act_s,
+    der_s,
+    hid_s,
+    atn_s,
+    h1_s,
+    x1_s,
+    h1r_s,
+    h1t_s,
+    df_s,
+    dft_s,
+    acc_s,
+    sglu_s,
+    sdown_s,
+    sout_s,
+    load_sem,
+    store_sem,
+    *,
+    head_cols,
+    hid_cols,
+):
+    n_row, n_t, rows = wall_ref.shape[:3]
+    width = h1_s.shape[1]
+    pad = wo_s.shape[2]
+    sizes = (2 * hid_cols, hid_cols, pad)
+
+    def loads(kind, t):
+        into = (wgu_s, wd_s, wo_s)[kind]
+        low = sum(sizes[:kind])
+        return [
+            pltpu.make_async_copy(
+                wall_ref.at[p, t, :, pl.ds(low, sizes[kind])],
+                into.at[t, pl.ds(p * rows, rows), :],
+                load_sem.at[kind, t, p],
+            )
+            for p in range(n_row)
+        ]
+
+    def stores(kind, t):
+        source = (sglu_s, sdown_s, sout_s)[kind]
+        into = (gglu_ref, grest_ref, grest_ref)[kind]
+        low = (0, 0, hid_cols)[kind]
+        return [
+            pltpu.make_async_copy(
+                source.at[pl.ds(p * rows, rows), :],
+                into.at[p, t, :, pl.ds(low, sizes[kind])],
+                store_sem.at[kind, p],
+            )
+            for p in range(n_row)
+        ]
+
+    for kind in (2, 0, 1):
+        for t in range(n_t):
+            for copy in loads(kind, t):
+                copy.start()
+    for t in range(n_t):
+        atn_s[t] = att_ref[t * head_cols : (t + 1) * head_cols, :].astype(f32).T.astype(bf16)
+        for copy in loads(2, t):
+            copy.wait()
+    branch = jnp.zeros_like(acc_s)
+    for t in range(n_t):
+        branch = branch + dot(atn_s[t], wo_s[t, :, :head_cols], 1, 1)
+    x1, r1 = normed(x_ref[...].astype(f32) + branch + vec_ref[0:1, :])
+    x1_s[...] = x1
+    h1 = x1 * vec_ref[1:2, :] + vec_ref[2:3, :]
+    h1_s[...] = h1
+    h1r_s[...] = h1.astype(bf16)
+    h1t_s[...] = h1.T.astype(bf16)
+    acc_s[...] = jnp.zeros_like(acc_s)
+    for kind in (0, 1):
+        for t in range(n_t):
+            for copy in loads(kind, t):
+                copy.wait()
+
+    def forward(t, _):
+        g = dot(h1r_s[...], wgu_s[t, :, :hid_cols], 1, 0)
+        u = dot(h1r_s[...], wgu_s[t, :, hid_cols:], 1, 0)
+        below = 0.5 * (1.0 + lax.erf(g * np.float32(math.sqrt(0.5))))
+        dense = jnp.exp(-0.5 * g * g) * np.float32(1.0 / math.sqrt(2.0 * math.pi))
+        act = g * below
+        act_s[t] = act
+        der_s[t] = u * (below + g * dense)
+        hidden = (act * u).astype(bf16)
+        hid_s[t] = hidden
+        acc_s[...] += dot(hidden, wd_s[t], 1, 1)
+        return 0
+
+    lax.fori_loop(0, n_t, forward, 0)
+    x2, r2 = normed(h1_s[...] + acc_s[...] + vec_ref[3:4, :])
+    out_ref[...] = (x2 * vec_ref[4:5, :] + vec_ref[5:6, :]).astype(bf16)
+    cot = cot_ref[...].astype(f32)
+    dz2 = norm_back(cot, x2, r2, vec_ref[4:5, :])
+    dvec_ref[3:4, :] = jnp.sum(dz2, axis=0, keepdims=True)
+    dvec_ref[4:5, :] = jnp.sum(cot * x2, axis=0, keepdims=True)
+    dvec_ref[5:6, :] = jnp.sum(cot, axis=0, keepdims=True)
+    df_s[...] = dz2.astype(bf16)
+    dft_s[...] = dz2.T.astype(bf16)
+    acc_s[...] = dz2
+
+    def backward(t, _):
+        def waits(kind):
+            @pl.when(t > 0)
+            def _():
+                for copy in stores(kind, t - 1):
+                    copy.wait()
+
+        waits(1)
+        sdown_s[...] = dot(dft_s[...], hid_s[t], 1, 0).astype(bf16)
+        for copy in stores(1, t):
+            copy.start()
+        dh = dot(df_s[...], wd_s[t], 1, 0)
+        dg = (dh * der_s[t]).astype(bf16)
+        du = (dh * act_s[t]).astype(bf16)
+        acc_s[...] += dot(dg, wgu_s[t, :, :hid_cols], 1, 1) + dot(du, wgu_s[t, :, hid_cols:], 1, 1)
+        waits(0)
+        sglu_s[:, :hid_cols] = dot(h1t_s[...], dg, 1, 0).astype(bf16)
+        sglu_s[:, hid_cols:] = dot(h1t_s[...], du, 1, 0).astype(bf16)
+        for copy in stores(0, t):
+            copy.start()
+        return 0
+
+    lax.fori_loop(0, n_t, backward, 0)
+    dh1 = acc_s[...]
+    x1 = x1_s[...]
+    dz1 = norm_back(dh1, x1, r1, vec_ref[1:2, :])
+    dvec_ref[0:1, :] = jnp.sum(dz1, axis=0, keepdims=True)
+    dvec_ref[1:2, :] = jnp.sum(dh1 * x1, axis=0, keepdims=True)
+    dvec_ref[2:3, :] = jnp.sum(dh1, axis=0, keepdims=True)
+    dvec_ref[6:8, :] = jnp.zeros((2, width), f32)
+    dz1_ref[...] = dz1
+    da = dz1.astype(bf16)
+    dat = dz1.T.astype(bf16)
+    sout_s[...] = jnp.zeros_like(sout_s)
+    for t in range(n_t):
+        do_ref[t * head_cols : (t + 1) * head_cols, :] = dot(
+            da, wo_s[t, :, :head_cols], 1, 0
+        ).T.astype(bf16)
+        if t > 0:
+            for copy in stores(2, t - 1):
+                copy.wait()
+        sout_s[:, :head_cols] = dot(dat, atn_s[t], 1, 0).astype(bf16)
+        for copy in stores(2, t):
+            copy.start()
+    for kind in range(3):
+        for copy in stores(kind, n_t - 1):
+            copy.wait()
+
+
+def feed_forward(attended, inputs, cotangent, vector_rows, wall, head_cols, hid_cols):
+    tokens, width = inputs.shape
+    n_row, n_t, rows = wall.shape[:3]
+    pad = wall.shape[3] - 3 * hid_cols
+    vmem = pl.BlockSpec(memory_space=pltpu.VMEM)
+    hbm = pl.BlockSpec(memory_space=pl.ANY)
+    shape = jax.ShapeDtypeStruct
+    size = tokens * width * n_t
+    return pl.pallas_call(
+        functools.partial(ff_kernel, head_cols=head_cols, hid_cols=hid_cols),
+        out_shape=(
+            shape((tokens, width), bf16),
+            shape((tokens, width), f32),
+            shape((n_t * head_cols, tokens), bf16),
+            shape((8, width), f32),
+            shape((n_row, n_t, rows, 2 * hid_cols), bf16),
+            shape((n_row, n_t, rows, hid_cols + pad), bf16),
+        ),
+        in_specs=[vmem] * 4 + [hbm],
+        out_specs=(vmem, vmem, vmem, vmem, hbm, hbm),
+        scratch_shapes=[
+            pltpu.VMEM((n_t, width, 2 * hid_cols), bf16),
+            pltpu.VMEM((n_t, width, hid_cols), bf16),
+            pltpu.VMEM((n_t, width, pad), bf16),
+            pltpu.VMEM((n_t, tokens, hid_cols), f32),
+            pltpu.VMEM((n_t, tokens, hid_cols), f32),
+            pltpu.VMEM((n_t, tokens, hid_cols), bf16),
+            pltpu.VMEM((n_t, tokens, head_cols), bf16),
+            pltpu.VMEM((tokens, width), f32),
+            pltpu.VMEM((tokens, width), f32),
+            pltpu.VMEM((tokens, width), bf16),
+            pltpu.VMEM((width, tokens), bf16),
+            pltpu.VMEM((tokens, width), bf16),
+            pltpu.VMEM((width, tokens), bf16),
+            pltpu.VMEM((tokens, width), f32),
+            pltpu.VMEM((width, 2 * hid_cols), bf16),
+            pltpu.VMEM((width, hid_cols), bf16),
+            pltpu.VMEM((width, pad), bf16),
+            pltpu.SemaphoreType.DMA((3, n_t, n_row)),
+            pltpu.SemaphoreType.DMA((3, n_row)),
+        ],
+        compiler_params=pltpu.CompilerParams(vmem_limit_bytes=63 * 2**20),
+        cost_estimate=pl.CostEstimate(
+            flops=6 * size * (3 * hid_cols + head_cols),
+            bytes_accessed=4 * wall.size,
+            transcendentals=2 * tokens * n_t * hid_cols,
+        ),
+        name="feed_forward",
+    )(attended, inputs, cotangent, vector_rows, wall)
+
+
+def on(axis, place):
+    return {"device_id": {axis: place}, "device_id_type": pl.DeviceIdType.MESH}
+
+
+def meet_all(barrier, axis, size):
+    place = lax.axis_index(axis)
+
+    def tell(k, _):
+        pl.semaphore_signal(barrier, inc=1, **on(axis, lax.rem(place + k, size)))
+        return 0
+
+    lax.fori_loop(1, size, tell, 0)
+
+
+def gather_kernel(*refs, n_chain, n_flat, chain, flat):
+    ins, refs = refs[: n_chain + n_flat], refs[n_chain + n_flat :]
+    outs, refs = refs[: n_chain + n_flat], refs[n_chain + n_flat :]
+    send_sem, recv_sem, local_sem, flat_send, flat_recv = refs
+    z = lax.axis_index("tensor")
+    p = lax.axis_index("dp")
+    barrier = pltpu.get_barrier_semaphore()
+
+    @pl.when(z > 0)
+    def _():
+        pl.semaphore_signal(barrier, inc=1, **on("tensor", z - 1))
+
+    @pl.when(z < chain - 1)
+    def _():
+        pl.semaphore_signal(barrier, inc=1, **on("tensor", z + 1))
+
+    met = jnp.where(z > 0, 1, 0) + jnp.where(z < chain - 1, 1, 0)
+    if n_flat:
+        meet_all(barrier, "dp", flat)
+        met = met + flat - 1
+    pl.semaphore_wait(barrier, met)
+
+    own = []
+    for i in range(n_chain):
+        own.append(pltpu.make_async_copy(ins[i], outs[i].at[z], local_sem.at[i]))
+    for j in range(n_flat):
+        i = n_chain + j
+        own.append(pltpu.make_async_copy(ins[i], outs[i].at[p], local_sem.at[i]))
+
+        def push(k, _):
+            pltpu.make_async_remote_copy(
+                ins[i],
+                outs[i].at[p],
+                flat_send.at[j, k],
+                flat_recv.at[j, p],
+                **on("dp", lax.rem(p + k, flat)),
+            ).start()
+            return 0
+
+        lax.fori_loop(1, flat, push, 0)
+    for copy in own:
+        copy.start()
+
+    def hop(i, way, step):
+        block = z - step if way == 0 else z + step
+        target = z + 1 if way == 0 else z - 1
+        return pltpu.make_async_remote_copy(
+            ins[i] if step == 0 else outs[i].at[block],
+            outs[i].at[block],
+            send_sem.at[i, way, step],
+            recv_sem.at[i, block],
+            **on("tensor", target),
+        )
+
+    def sends(way, step):
+        if way == 0:
+            return (z < chain - 1) & (z >= step)
+        return (z > 0) & (z + step < chain)
+
+    def arrived(i, block):
+        pltpu.make_async_remote_copy(
+            outs[i].at[block],
+            outs[i].at[block],
+            send_sem.at[i, 0, 0],
+            recv_sem.at[i, block],
+            **on("tensor", lax.rem(z + 1, chain)),
+        ).wait_recv()
+
+    for i in range(n_chain):
+        for step in range(chain - 1):
+            for way in range(2):
+
+                @pl.when(sends(way, step))
+                def _():
+                    if step > 0:
+                        arrived(i, z - step if way == 0 else z + step)
+                    hop(i, way, step).start()
+
+    for i in range(n_chain):
+        for step in range(1, chain):
+
+            @pl.when((z == chain - 1) & (z >= step))
+            def _():
+                arrived(i, z - step)
+
+            @pl.when((z == 0) & (z + step < chain))
+            def _():
+                arrived(i, z + step)
+
+        for step in range(chain - 1):
+            for way in range(2):
+
+                @pl.when(sends(way, step))
+                def _():
+                    hop(i, way, step).wait_send()
+
+    for j in range(n_flat):
+        i = n_chain + j
+
+        def finish(k, _):
+            q = lax.rem(p + k, flat)
+            copy = pltpu.make_async_remote_copy(
+                ins[i], outs[i].at[q], flat_send.at[j, k], flat_recv.at[j, q], **on("dp", q)
+            )
+            copy.wait_send()
+            copy.wait_recv()
+            return 0
+
+        lax.fori_loop(1, flat, finish, 0)
+    for copy in own:
+        copy.wait()
+
+
+def gather_blocks(on_chain, to_all, n_tensor, n_dp, call_id):
+    arrays = [*on_chain, *to_all]
+    sizes = [n_tensor] * len(on_chain) + [n_dp] * len(to_all)
+    vmem = pl.BlockSpec(memory_space=pltpu.VMEM)
+    hbm = pl.BlockSpec(memory_space=pl.ANY)
+    count = len(arrays)
+    dma = pltpu.SemaphoreType.DMA
+    return pl.pallas_call(
+        functools.partial(
+            gather_kernel, n_chain=len(on_chain), n_flat=len(to_all), chain=n_tensor, flat=n_dp
+        ),
+        out_shape=[jax.ShapeDtypeStruct((n,) + a.shape, a.dtype) for n, a in zip(sizes, arrays)],
+        in_specs=[vmem] * count,
+        out_specs=[hbm] * count,
+        scratch_shapes=[
+            dma((count, 2, n_tensor)),
+            dma((count, n_tensor)),
+            dma((count,)),
+            dma((max(len(to_all), 1), n_dp)),
+            dma((max(len(to_all), 1), n_dp)),
+        ],
+        compiler_params=pltpu.CompilerParams(collective_id=call_id, has_side_effects=True),
+    )(*arrays)
+
+
+def collect_kernel(*refs, ops, sizes):
+    count = len(ops)
+    ins, outs, refs = refs[:count], refs[count : 2 * count], refs[2 * count :]
+    sums = [i for i, (kind, _) in enumerate(ops) if kind == "sum"]
+    got = dict(zip(sums, refs))
+    send_sem, recv_sem, local_sem = refs[len(sums) :]
+    barrier = pltpu.get_barrier_semaphore()
+    axes = sorted({axis for _, axis in ops})
+    for axis in axes:
+        meet_all(barrier, axis, sizes[axis])
+    pl.semaphore_wait(barrier, sum(sizes[axis] - 1 for axis in axes))
+
+    def cut_lanes(ref, index, size):
+        lanes = ref.shape[1] // size
+        return ref.at[:, pl.ds(pl.multiple_of(index * lanes, 128), lanes)]
+
+    def cut_rows(ref, index, size):
+        rows = ref.shape[0] // size
+        return ref.at[pl.ds(pl.multiple_of(index * rows, 16), rows), :]
+
+    def cuts(i, source, target):
+        kind, axis = ops[i]
+        size = sizes[axis]
+        if kind == "rows":
+            return cut_lanes(ins[i], source, size), cut_rows(outs[i], target, size)
+        if kind == "lanes":
+            return cut_rows(ins[i], source, size), cut_lanes(outs[i], target, size)
+        return ins[i].at[source], got[i].at[target]
+
+    def copy(i, k, landing):
+        axis = ops[i][1]
+        d = lax.rem(lax.axis_index(axis) + k, sizes[axis])
+        place = d if landing is None else landing
+        source, target = cuts(i, d, place)
+        return pltpu.make_async_remote_copy(
+            source, target, send_sem.at[i, k], recv_sem.at[i, place], **on(axis, d)
+        )
+
+    def own(i):
+        z = lax.axis_index(ops[i][1])
+        return pltpu.make_async_copy(*cuts(i, z, z), local_sem.at[i])
+
+    for i, (kind, axis) in enumerate(ops):
+
+        def push(k, _):
+            copy(i, k, lax.axis_index(axis)).start()
+            return 0
+
+        lax.fori_loop(1, sizes[axis], push, 0)
+        if kind != "sum":
+            own(i).start()
+    for i, (kind, axis) in enumerate(ops):
+        if kind == "sum":
+            outs[i][...] = ins[i][lax.axis_index(axis)].astype(f32)
+
+        def take(k, _):
+            copy(i, k, None).wait_recv()
+            if kind == "sum":
+                outs[i][...] += got[i][lax.rem(lax.axis_index(axis) + k, sizes[axis])].astype(f32)
+            copy(i, k, None).wait_send()
+            return 0
+
+        lax.fori_loop(1, sizes[axis], take, 0)
+        if kind != "sum":
+            own(i).wait()
+
+
+def collect(ops, arrays, sizes, call_id):
+    def shape_of(op, a):
+        kind, axis = op
+        n = sizes[axis]
+        if kind == "rows":
+            return jax.ShapeDtypeStruct((a.shape[0] * n, a.shape[1] // n), a.dtype)
+        if kind == "lanes":
+            return jax.ShapeDtypeStruct((a.shape[0] // n, a.shape[1] * n), a.dtype)
+        return jax.ShapeDtypeStruct(a.shape[1:], f32)
+
+    vmem = pl.BlockSpec(memory_space=pltpu.VMEM)
+    dma = pltpu.SemaphoreType.DMA
+    most = max(sizes[axis] for _, axis in ops)
+    count = len(ops)
+    return pl.pallas_call(
+        functools.partial(collect_kernel, ops=ops, sizes=sizes),
+        out_shape=[shape_of(op, a) for op, a in zip(ops, arrays)],
+        in_specs=[vmem] * count,
+        out_specs=[vmem] * count,
+        scratch_shapes=[
+            pltpu.VMEM(a.shape, a.dtype) for op, a in zip(ops, arrays) if op[0] == "sum"
+        ]
+        + [dma((count, most)), dma((count, most)), dma((count,))],
+        compiler_params=pltpu.CompilerParams(
+            collective_id=call_id, has_side_effects=True, vmem_limit_bytes=40 * 2**20
+        ),
+    )(*arrays)
+
+
+def input_kernel(heads_ref, grad_ref, w_ref, out_ref, w_s, sem):
+    n_row, n_t, rows, cols = w_ref.shape
+    loads = [
+        pltpu.make_async_copy(
+            w_ref.at[p, t], w_s.at[t, pl.ds(p * rows, rows), :], sem.at[t, p]
+        )
+        for t in range(n_t)
+        for p in range(n_row)
+    ]
+    for load in loads:
+        load.start()
+    for load in loads:
+        load.wait()
+    out_ref[...] = grad_ref[...]
+    for t in range(n_t):
+        part = heads_ref[t * cols : (t + 1) * cols, :].astype(f32).T.astype(bf16)
+        out_ref[...] += dot(part, w_s[t], 1, 1)
+
+
+def input_gradient(grad_heads, grad_one, weights):
+    n_row, n_t, rows, cols = weights.shape
+    vmem = pl.BlockSpec(memory_space=pltpu.VMEM)
+    return pl.pallas_call(
+        input_kernel,
+        out_shape=jax.ShapeDtypeStruct(grad_one.shape, f32),
+        in_specs=[vmem, vmem, pl.BlockSpec(memory_space=pl.ANY)],
+        out_specs=vmem,
+        scratch_shapes=[
+            pltpu.VMEM((n_t, n_row * rows, cols), bf16),
+            pltpu.SemaphoreType.DMA((n_t, n_row)),
+        ],
+        compiler_params=pltpu.CompilerParams(vmem_limit_bytes=32 * 2**20),
+        cost_estimate=pl.CostEstimate(
+            flops=2 * grad_heads.size * grad_one.shape[1],
+            bytes_accessed=2 * weights.size + 4 * grad_heads.size,
+            transcendentals=0,
+        ),
+        name="input_gradient",
+    )(grad_heads, grad_one, weights)
+
+
+def sum_kernel(in_ref, out_ref, first, second, part, send_sem, recv_sem, local_sem, *, sizes):
+    barrier = pltpu.get_barrier_semaphore()
+    for axis, size in sizes:
+        meet_all(barrier, axis, size)
+    pl.semaphore_wait(barrier, sum(size - 1 for _, size in sizes))
+    for stage, (axis, size) in enumerate(sizes):
+        source = in_ref if stage == 0 else part
+        into = first if stage == 0 else second
+        z = lax.axis_index(axis)
+        own = pltpu.make_async_copy(source, into.at[z], local_sem.at[stage])
+        own.start()
+
+        def push(k, _):
+            pltpu.make_async_remote_copy(
+                source,
+                into.at[z],
+                send_sem.at[stage, k],
+                recv_sem.at[stage, z],
+                **on(axis, lax.rem(z + k, size)),
+            ).start()
+            return 0
+
+        def take(k, _):
+            d = lax.rem(z + k, size)
+            copy = pltpu.make_async_remote_copy(
+                source, into.at[d], send_sem.at[stage, k], recv_sem.at[stage, d], **on(axis, d)
+            )
+            copy.wait_recv()
+            copy.wait_send()
+            return 0
+
+        lax.fori_loop(1, size, push, 0)
+        lax.fori_loop(1, size, take, 0)
+        own.wait()
+        total = into[0]
+        for k in range(1, size):
+            total = total + into[k]
+        if stage == 0:
+            part[...] = total
+        else:
+            out_ref[...] = total
+
+
+def sum_everywhere(value, n_dp, n_tensor, call_id):
+    vmem = pl.BlockSpec(memory_space=pltpu.VMEM)
+    dma = pltpu.SemaphoreType.DMA
+    most = max(n_dp, n_tensor)
+    return pl.pallas_call(
+        functools.partial(sum_kernel, sizes=(("dp", n_dp), ("tensor", n_tensor))),
+        out_shape=jax.ShapeDtypeStruct(value.shape, f32),
+        in_specs=[vmem],
+        out_specs=vmem,
+        scratch_shapes=[
+            pltpu.VMEM((n_dp,) + value.shape, f32),
+            pltpu.VMEM((n_tensor,) + value.shape, f32),
+            pltpu.VMEM(value.shape, f32),
+            dma((2, most)),
+            dma((2, most)),
+            dma((2,)),
+        ],
+        compiler_params=pltpu.CompilerParams(collective_id=call_id, has_side_effects=True),
+    )(value)
+
+
 def lamb_terms(weight, gradient, moments):
     first_moment = 0.5 * moments[0] + 0.5 * gradient
     root_moment = jnp.sqrt(0.5 * moments[1] * moments[1] + 0.5 * gradient * gradient)
@@ -324,7 +894,23 @@
         ],
         axis=1,
     )
-    own = lax.all_gather(jnp.concatenate([attn_rows, small], axis=1), "dp", axis=0, tiled=True)
+    wall_rows = jnp.concatenate(
+        [glu_rows, down_rows, jnp.pad(out_rows, ((0, 0), (0, -head_cols % 128)))], axis=1
+    )
+    wall_chain, own = gather_blocks(
+        [wall_rows], [jnp.concatenate([attn_rows, small], axis=1)], n_tensor, n_dp, 0
+    )
+    own = own.reshape(width, -1)
+    first_inputs, own = lax.optimization_barrier((inputs, own))
+    inputs_full, attn_chain = gather_blocks([first_inputs, attn_rows], [], n_tensor, n_dp, 1)
+    inputs_full = inputs_full.reshape(length, width)
+    wall = lax.all_gather(wall_chain, "dp")
+    attn_all = lax.all_gather(attn_chain, "dp")
+    if rows % 16:
+        wall, attn_all = [
+            w.transpose(1, 0, 2, 3).reshape(1, n_tensor, width, -1) for w in (wall, attn_all)
+        ]
+
     attn_own = own[:, : 3 * head_cols]
     vector_rows = own[:, 3 * head_cols : 3 * head_cols + 6].T.astype(f32)
     qv_rows = (
@@ -341,87 +927,33 @@
         .transpose(1, 0, 2)
         .reshape(3 * head_cols)
     )
-    inputs_full = lax.all_gather(inputs, "tensor", axis=0, tiled=True)
-
-    sizes = (head_cols, 2 * hidden_cols, hidden_cols, 3 * head_cols)
-    packed = lax.all_gather(
-        jnp.concatenate([out_rows, glu_rows, down_rows, attn_rows], axis=1), "tensor"
-    )
-    gathered = []
-    offset = 0
-    for size in sizes:
-        mine = packed[:, :, offset : offset + size].transpose(1, 0, 2).reshape(rows, -1)
-        gathered.append(lax.all_gather(mine, "dp", axis=0, tiled=True))
-        offset += size
-    out_all, glu_all, down_all, attn_all = gathered
 
     qkv = (dot(inputs_full, attn_own, 1, 0) + qkv_bias).astype(bf16)
     out_t, lse = attention_forward(parts, qkv)
-    attended = lax.all_to_all(
-        out_t.reshape(head_cols, length), "tensor", split_axis=1, concat_axis=0, tiled=True
-    )
-    summed_one = inputs.astype(f32) + dot(attended, out_all, 0, 1) + vector_rows[0]
-    normed_one, norm_one_back = jax.vjp(layer_norm, summed_one, vector_rows[1], vector_rows[2])
-    normed_low = normed_one.astype(bf16)
-    gate_up = dot(normed_low, glu_all, 1, 0).reshape(tokens, n_tensor, 2, hidden_cols)
-    hidden_val, gated_back = jax.vjp(gated, gate_up[:, :, 0], gate_up[:, :, 1])
-    hidden = hidden_val.astype(bf16).reshape(tokens, n_tensor * hidden_cols)
-    summed_two = normed_one + dot(hidden, down_all, 1, 1) + vector_rows[3]
-    output, norm_two_back = jax.vjp(layer_norm, summed_two, vector_rows[4], vector_rows[5])
-    grad_two, grad_gain_two, grad_shift_two = norm_two_back(cotangent.astype(f32))
-    grad_branch = grad_two.astype(bf16)
-    down_grad = dot(grad_branch, hidden, 0, 0).astype(bf16)
-    down_part = lax.psum_scatter(down_grad, "dp", scatter_dimension=0, tiled=True)
-    grad_hidden = dot(grad_branch, down_all, 1, 0).reshape(tokens, n_tensor, hidden_cols)
-    grad_gate, grad_up = gated_back(grad_hidden)
-    grad_glu = (
-        jnp.stack([grad_gate, grad_up], axis=2)
-        .astype(bf16)
-        .reshape(tokens, 2 * n_tensor * hidden_cols)
-    )
-    glu_grad = dot(normed_low, grad_glu, 0, 0).astype(bf16)
-    glu_part = lax.psum_scatter(glu_grad, "dp", scatter_dimension=0, tiled=True)
-    grad_normed = grad_two + dot(grad_glu, glu_all, 1, 1)
-    grad_one, grad_gain_one, grad_shift_one = norm_one_back(grad_normed)
-    grad_attn = grad_one.astype(bf16)
-    out_grad = dot(grad_attn, attended, 0, 1).astype(bf16)
-    out_part = lax.psum_scatter(out_grad, "dp", scatter_dimension=0, tiled=True)
-    grad_attended = dot(out_all, grad_attn, 0, 1).astype(bf16)
-    vector_part = jnp.stack(
-        [
-            jnp.sum(grad_one, axis=0),
-            grad_gain_one,
-            grad_shift_one,
-            jnp.sum(grad_two, axis=0),
-            grad_gain_two,
-            grad_shift_two,
+    sizes = {"dp": n_dp, "tensor": n_tensor}
+    (attended,) = collect([("rows", "tensor")], [out_t.reshape(head_cols, length)], sizes, 2)
+    output, grad_one, grad_attended, vector_part, grad_glu, grad_rest = feed_forward(
+        attended,
+        inputs,
+        cotangent,
+        jnp.pad(vector_rows, ((0, 2), (0, 0))),
+        wall,
+        head_cols,
+        hidden_cols,
+    )
+    if rows % 16:
+        grad_glu, grad_rest = [
+            g.reshape(n_tensor, n_dp, rows, -1).transpose(1, 0, 2, 3) for g in (grad_glu, grad_rest)
         ]
-    )
-    vector_all = lax.psum(vector_part, ("dp", "tensor"))
+    glu_part = lax.psum_scatter(grad_glu, "dp", scatter_dimension=0, tiled=False)
+    rest_part = lax.psum_scatter(grad_rest, "dp", scatter_dimension=0, tiled=False)
+    vector_all = sum_everywhere(vector_part, n_dp, n_tensor, 5)[:6]
     slice_width = vector_mom.shape[2]
     vector_sum = lax.dynamic_slice_in_dim(
         vector_all, (lax.axis_index("dp") * n_tensor + tensor_pos) * slice_width, slice_width, 1
     )
-    late_parts = jnp.concatenate(
-        [
-            out_part.reshape(rows, n_tensor, head_cols),
-            glu_part.reshape(rows, n_tensor, 2 * hidden_cols),
-            down_part.reshape(rows, n_tensor, hidden_cols),
-        ],
-        axis=2,
-    )
-    late_sum = lax.psum_scatter(late_parts, "tensor", scatter_dimension=1, tiled=True)[:, 0].astype(f32)
-    out_sum = late_sum[:, :head_cols].T
-    glu_sum = (
-        late_sum[:, head_cols : head_cols + 2 * hidden_cols]
-        .reshape(rows, 2, hidden_cols)
-        .transpose(1, 0, 2)
-    )
-    down_sum = late_sum[:, head_cols + 2 * hidden_cols :].T
-
-    grad_heads = lax.all_to_all(
-        grad_attended, "tensor", split_axis=0, concat_axis=1, tiled=True
-    ).reshape(head_count, HEAD, length)
+    (grad_heads,) = collect([("lanes", "tensor")], [grad_attended], sizes, 6)
+    grad_heads = grad_heads.reshape(head_count, HEAD, length)
     grad_qkv = attention_backward(parts, qkv, grad_heads, out_t, lse).reshape(3 * head_cols, length)
     attn_grad = dot(inputs_full, grad_qkv, 0, 1)
     qv_grad = jnp.sum(grad_qkv.reshape(head_count, 3, HEAD, length).astype(f32), axis=3)
@@ -430,8 +962,17 @@
         qv_grad.transpose(1, 0, 2).reshape(n_dp, 2 * qv_cols), ((0, 0), (0, rows - 2 * qv_cols))
     ).reshape(width, 1)
     attn_part = jnp.concatenate([attn_grad, qv_grad, jnp.zeros((width, 63), f32)], axis=1)
-    attn_part = lax.psum_scatter(attn_part.astype(bf16), "dp", scatter_dimension=0, tiled=True)
-    attn_part = attn_part.astype(f32)
+    attn_part = attn_part.astype(bf16).reshape(n_dp, rows, -1)
+    grad_tokens, attn_part, glu_sum = collect(
+        [("rows", "tensor"), ("sum", "dp"), ("sum", "tensor")],
+        [grad_qkv, attn_part, glu_part],
+        sizes,
+        3,
+    )
+    (rest_sum,) = collect([("sum", "tensor")], [rest_part], sizes, 4)
+    glu_sum = glu_sum.reshape(rows, 2, hidden_cols).transpose(1, 0, 2)
+    down_sum = rest_sum[:, :hidden_cols].T
+    out_sum = rest_sum[:, hidden_cols : hidden_cols + head_cols].T
     attn_sum = (
         attn_part[:, : 3 * head_cols]
         .reshape(rows, head_count, 3, HEAD)
@@ -440,8 +981,7 @@
     )
     qv_sum = attn_part[: 2 * qv_cols, 3 * head_cols].reshape(2, qv_cols)
 
-    grad_tokens = lax.all_to_all(grad_qkv, "tensor", split_axis=1, concat_axis=0, tiled=True)
-    input_grad = grad_one + dot(grad_tokens, attn_all, 0, 1)
+    input_grad = input_gradient(grad_tokens, grad_one, attn_all)
 
     vector_own = lax.dynamic_slice_in_dim(vectors, tensor_pos * slice_width, slice_width, 1)
     owned_parts = (attn_w, out_w, glu_w, down_w, qv_bias, vector_own)
@@ -456,7 +996,8 @@
         directions.append(direction)
     weight_sums = jnp.concatenate([piece_sums(w, f) for w, f in zip(owned_parts, stack_flags)])
     dir_sums = jnp.concatenate([piece_sums(r, f) for r, f in zip(directions, stack_flags)])
-    totals = lax.psum(jnp.stack([weight_sums, dir_sums]), ("dp", "tensor"))
+    totals = jnp.pad(jnp.stack([weight_sums, dir_sums]), ((0, 6), (0, 113)))
+    totals = sum_everywhere(totals, n_dp, n_tensor, 9)[:2, :15]
     norm_values = jnp.sqrt(totals + 1e-12)
     ratios = norm_values[0] / norm_values[1]
     new_weights = []
@@ -471,7 +1012,7 @@
         new_weights.append(weight - learn_rate * factor * direction)
         offset = offset + amount
     return (
-        output.astype(bf16),
+        output,
         input_grad,
         *gradients,
         *new_moments,

time: 758 us -> 503 us (0.66)
  Pallas kernels: 67.4 us -> 381 us
  waiting for transfers between devices: 274 us -> 20.3 us
  blocking collectives: 90.1 us -> 0 us
  other arithmetic: 105 us -> 31.2 us
  local copies, waits for them, and re-layouts: 108 us -> 38.9 us
  matrix products: 77.6 us -> 9.08 us
  starting transfers between devices: 13.6 us -> 0.16 us
    pallas_call x0 -> x10, Pallas kernels: none -> 313 us  [the longest x4 125 us: collect(): pl.pallas_call(functools.partial(collect_kernel, ops=ops, sizes=sizes), o...]
    all_gather x6 -> x2, waiting for transfers between devices: 143 us -> 0.01 us  [the longest x1 0.01 us: local(): wall = lax.all_gather(wall_chain, 'dp')]
    psum x2 -> x0, blocking collectives: 79.1 us -> none  [the longest x1 39.6 us: local(): vector_all = lax.psum(vector_part, ('dp', 'tensor'))]
    reduce_scatter x4 -> x2, waiting for transfers between devices: 93.4 us -> 19.1 us  [the longest x1 19.1 us: local(): lax.psum_scatter(grad_glu, 'dp', scatter_dimension=0, tiled=False)]
    dot_general x12 -> x2, matrix products: 77.6 us -> 9.08 us  [dot(): lax.dot_general(a, b, (((ca,), (cb,)), ((), ())), preferred_element_type=...]
    all_to_all x3 -> x0, waiting for transfers between devices: 36.1 us -> none  [the longest x1 20.2 us: local(): lax.all_to_all(grad_attended, 'tensor', split_axis=0, concat_axis=1, tile...]
    another operation x4 -> x1, other arithmetic: 32.6 us -> 1.21 us  [local(): totals = jnp.pad(jnp.stack([weight_sums, dir_sums]), ((0, 6), (0, 113)))]
    slice x7 -> x0, local copies, waits for them, and re-layouts: 18.5 us -> none  [the longest x1 10.9 us: local(): hidden_val, gated_back = jax.vjp(gated, gate_up[:, :, 0], gate_up[:, :, 1])]
  transfers between devices with their start and end apart: 14 -> 4, of which waited for: 8 -> 1; matrix products, arithmetic and copies ran while one was open for 24% -> 12% of each run, Pallas kernels for 9% -> 57%
where the time goes in v2:
time: 503 us; the launch traced here: 496 us
  Pallas kernels  381 us (76%)
  local copies, waits for them, and re-layouts  38.9 us (8%)
  other arithmetic  31.2 us (6%)
  waiting for transfers between devices  20.3 us (4%)
  between operations  15.9 us (3%)
  matrix products  9.08 us (2%)
    pallas_call x4, Pallas kernels, collect(): pl.pallas_call(functools.partial(collect_kernel, ops=ops, sizes=sizes), o...  125 us
    pallas_call x2, Pallas kernels, gather_blocks(): pl.pallas_call(functools.partial(gather_kernel, n_chain=len(on_chain), n_...  105 us
    pallas_call x1, Pallas kernels, feed_forward(): pl.pallas_call(functools.partial(ff_kernel, head_cols=head_cols, hid_cols...  45.9 us
    pallas_call x1, Pallas kernels, attention_backward(): pl.pallas_call(functools.partial(bwd_kernel, heads=heads, length=length,...  41.9 us
    pallas_call x2, Pallas kernels, sum_everywhere(): pl.pallas_call(functools.partial(sum_kernel, sizes=(('dp', n_dp), ('tenso...  28.2 us
    pallas_call x1, Pallas kernels, attention_forward(): pl.pallas_call(functools.partial(fwd_kernel, heads=heads, length=length,...  25.6 us
    unnamed x97, local copies, waits for them, and re-layouts  22.5 us
    reduce_scatter x1, waiting for transfers between devices, local(): lax.psum_scatter(grad_glu, 'dp', scatter_dimension=0, tiled=False)  19.1 us
  transfers between devices with their start and end apart: 4, of which 1 were waited for; matrix products, arithmetic and copies ran while one was open for 12% of the time, Pallas kernels for 57%

profile of v2, /device:TPU:0, one launch (start us, length us, event | category | flops | bytes accessed | tf_op | source)
XLA Modules:
  0.0 496.4 jit_solution(4167222986083070677)
XLA Ops:
  7.3 1.0 copy.127
  8.3 1.4 multiply_reduce_fusion.1
  9.8 1.8 multiply_reduce_fusion.4
  14.1 43.6 %shard_map.318 = (bf16[4,96,2560]{2,1,0:T(8,128)(2,1)}, bf16[8,96,640]{2,1,0:T(8,128)(2,1)}) custom-call(bf16[96,2560]{1,0:T(8,128)(2,1)} %fusion.4.refs_0_, bf16[96,640]{1,0:T(8,128)(2,1)} %maximum_maximum_fusion.1.refs_1_), custom_call_target="tpu_custom_call" | custom-call | tf_op jit(solution)/shard_map/pallas_call | solution.py:614
  57.8 1.1 copy-done.23
  60.5 61.1 %shard_map.319 = (bf16[4,512,768]{2,1,0:T(8,128)(2,1)}, bf16[4,96,576]{2,1,0:T(8,128)(2,1)}) custom-call(bf16[512,768]{1,0:T(8,128)(2,1)} %x_ref.1, bf16[96,576]{1,0:T(8,128)(2,1)} %copy-done.28), custom_call_target="tpu_custom_call" | custom-call | tf_op jit(solution)/shard_map/pallas_call | solution.py:614
  122.3 4.5 add_convert_fusion.qkv_ref
  126.8 25.6 %attention_forward.1 = (bf16[3,64,2048]{2,1,0:T(8,128)(2,1)S(1)}, f32[3,1,2048]{2,1,0:T(1,128)S(1)}) custom-call(f32[3,3]{1,0:T(4,128)S(1)} %constant_dynamic-slice_fusion.1.parts_ref, bf16[2048,576]{1,0:T(8,128)(2,1)S(1)} %add_convert_fusion.qkv_ref), custom_call_target="tpu_custom_call" | custom-call | flops 12884901888 | bytes 4718592 | tf_op jit(solution)/shard_map/attention_forward/pallas_call | solution.py:121
  152.4 14.1 %shard_map.320.att_ref = bf16[768,512]{1,0:T(8,128)(2,1)S(1)} custom-call(bf16[192,2048]{1,0:T(8,128)(2,1)S(1)} %bitcast.186), custom_call_target="tpu_custom_call" | custom-call | tf_op jit(solution)/shard_map/pallas_call | solution.py:713
  166.6 0.9 copy-done.8
  168.1 45.9 %feed_forward.1 = (bf16[512,768]{1,0:T(8,128)(2,1)}, f32[512,768]{1,0:T(8,128)}, bf16[768,512]{1,0:T(8,128)(2,1)}, f32[8,768]{1,0:T(8,128)}, bf16[8,4,96,1536]{3...) custom-call(bf16[768,512]{1,0:T(8,128)(2,1)} %copy-done.8, bf16[512,768]{1,0:T(8,128)(2,1)} %x_ref.1, ...), custom_call_target="tpu_custom_call" | custom-call | flops 23555211264 | bytes 31457280 | tf_op jit(solution)/shard_map/feed_forward/pallas_call | solution.py:437
  216.1 4.9 copy.137
  221.2 0.9 copy.162
  222.0 0.9 copy.163
  224.4 18.8 %shard_map.321 = bf16[192,2048]{1,0:T(8,128)(2,1)S(1)} custom-call(bf16[768,512]{1,0:T(8,128)(2,1)S(1)} %copy-done.7), custom_call_target="tpu_custom_call" | custom-call | tf_op jit(solution)/shard_map/pallas_call | solution.py:713
  243.2 41.9 %attention_backward.1 = bf16[3,3,64,2048]{3,2,1,0:T(8,128)(2,1)S(1)} custom-call(f32[3,3]{1,0:T(4,128)S(1)} %constant_dynamic-slice_fusion.1.parts_ref, bf16[2048,576]{1,0:T(8,128)(2,1)} %copy-done.12, bf16[3,64,2048]{2,1,0:T(8,128)(2,1)S(1)} %bitcast.187, bf16[3,64,2048]{2,1,0:T(8,128)(2,1)S(1)} %get-tuple-element.43.ot_ref, ...), custom_call_target="tpu_custom_call" | custom-call | flops 32212254720 | bytes 9437184 | tf_op jit(solution)/shard_map/attention_backward/pallas_call | solution.py:228
  286.7 13.1 %shard_map.324 = f32[8,768]{1,0:T(8,128)} custom-call(f32[8,768]{1,0:T(8,128)} %get-tuple-element.55.in_ref), custom_call_target="tpu_custom_call" | custom-call | tf_op jit(solution)/shard_map/pallas_call | solution.py:816
  299.9 1.4 multiply_reduce_fusion.8
  301.9 4.6 convolution_convert_fusion
  306.8 1.9 concatenate.25
  308.7 1.1 copy-done.6
  309.8 16.6 %shard_map.323 = f32[96,1024]{1,0:T(8,128)S(1)} custom-call(bf16[4,96,1024]{2,1,0:T(8,128)(2,1)S(1)} %bitcast.185), custom_call_target="tpu_custom_call" | custom-call | tf_op jit(solution)/shard_map/pallas_call | solution.py:713
  327.2 2.3 multiply_reduce_fusion.6
  330.3 0.9 slice_bitcast_fusion.1
  331.9 2.8 multiply_reduce_fusion.2
  335.4 1.2 fusion.17
  336.6 0.9 pad_maximum_fusion.2
  337.5 19.1 %reduce-scatter.3.cloned.1.call-done = bf16[1,4,96,1536]{3,2,1,0:T(8,128)(2,1)} async-done(((bf16[8,4,96,1536]{3,2,1,0:T(8,128)(2,1)}), bf16[1,4,96,1536]{3,2,1,0:T(8,128)(2,1)}) %reduce-scatter.3.cloned.1.call-update) | async-done | bytes 1179664 | tf_op jit(solution)/shard_map/reduce_scatter | solution.py:948
  356.6 1.3 copy-done.5
  357.8 75.6 %shard_map.322 = (bf16[2304,512]{1,0:T(8,128)(2,1)S(1)}, f32[96,640]{1,0:T(8,128)S(1)}, f32[96,1536]{1,0:T(8,128)S(1)}) custom-call(bf16[576,2048]{1,0:T(8,128)(2,1)S(1)} %bitcast.182, bf16[8,96,640]{2,1,0:T(8,128)(2,1)S(1)} %maximum_maximum_fusion.refs_1_, bf16[4,96,1536]{2,1,0:T(8,128)(2,1)S(1)} %bitcast.184), custom_call_target="tpu_custom_call" | custom-call | tf_op jit(solution)/shard_map/pallas_call | solution.py:713
  433.5 1.4 copy-done.1
  437.3 1.1 copy.140
  438.5 1.2 multiply_reduce_fusion.10
  439.6 2.1 multiply_reduce_fusion.3
  441.8 1.9 multiply_reduce_fusion
  443.7 2.0 concatenate.26
  445.7 1.2 select_maximum_fusion.in_ref
  447.0 15.1 %shard_map.325 = f32[8,128]{1,0:T(8,128)} custom-call(f32[8,128]{1,0:T(8,128)} %select_maximum_fusion.in_ref), custom_call_target="tpu_custom_call" | custom-call | tf_op jit(solution)/shard_map/pallas_call | solution.py:816
  464.7 1.0 multiply_subtract_fusion.3
  466.4 1.1 multiply_subtract_fusion.2
  467.4 0.9 copy.159
  468.5 1.1 copy.156
  469.6 0.9 copy.154
  472.1 1.1 pad_maximum_fusion
  475.9 0.9 multiply_subtract_fusion
  476.9 2.1 copy-done
  479.0 1.4 copy-done.4
  480.4 9.2 %input_gradient.1 = f32[512,768]{1,0:T(8,128)} custom-call(bf16[2304,512]{1,0:T(8,128)(2,1)S(1)} %copy-done.2, f32[512,768]{1,0:T(8,128)S(1)} %copy-done.4, bf16[8,4,96,576]{3,2,1,0:T(8,128)(2,1)S(1)} %bitcast.183), custom_call_target="tpu_custom_call" | custom-call | flops 1811939328 | bytes 8257536 | tf_op jit(solution)/shard_map/input_gradient/pallas_call | solution.py:750
  (165 shorter events, 23.7 us)
Async XLA Ops:
  7.2 4.4 copy-start.24
  7.2 4.7 copy-start.35
  7.2 5.1 %copy-start.33 = (f32[6,96]{1,0:T(8,128)S(1)}, f32[6,96]{1,0:T(8,128)}, u32[]{:S(2)}) copy-start(f32[6,96]{1,0:T(8,128)} %param.22) | copy-start | bytes 6916
  7.2 160.8 %all-gather.5.cloned.1.call-start = ((), (), s32[]{:S(2)}) async-start(), calls=%async_computation.4 | async-start | bytes 17694720 | tf_op jit(solution)/shard_map/all_gather | solution.py:907
  8.3 318.2 %copy-start.22 = (f32[192,96]{0,1:T(8,128)}, f32[192,96]{0,1:T(8,128)S(1)}, u32[]{:S(2)}) copy-start(f32[192,96]{0,1:T(8,128)S(1)} %copy.127) | copy-start | bytes 221188
  11.7 46.0 %copy-start.14 = (f32[3,96,192]{1,2,0:T(8,128)}, f32[3,96,192]{1,2,0:T(8,128)S(1)}, u32[]{:S(2)}) copy-start(f32[3,96,192]{1,2,0:T(8,128)S(1)} %copy.128) | copy-start | bytes 663556
  11.9 47.6 %copy-start.28 = (bf16[96,576]{1,0:T(8,128)(2,1)}, bf16[96,576]{1,0:T(8,128)(2,1)S(1)}, u32[]{:S(2)}) copy-start(bf16[96,576]{1,0:T(8,128)(2,1)S(1)} %copy.131.refs_1_) | copy-start | bytes 331780
  57.7 1.2 copy-start.23
  57.7 251.0 %reduce-scatter.5.cloned.1.call-start = ((), (), s32[]{:S(2)}) async-start(), calls=%async_computation.3 | async-start | bytes 7077888 | tf_op jit(solution)/shard_map/reduce_scatter | solution.py:949
  126.8 25.6 %copy-start.12 = (bf16[2048,576]{1,0:T(8,128)(2,1)}, bf16[2048,576]{1,0:T(8,128)(2,1)S(1)}, u32[]{:S(2)}) copy-start(bf16[2048,576]{1,0:T(8,128)(2,1)S(1)} %add_convert_fusion.qkv_ref) | copy-start | bytes 7077892
  166.6 0.9 copy-start.8
  214.0 142.5 %reduce-scatter.3.cloned.1.call-start = ((), (), s32[]{:S(2)}) async-start(), calls=%async_computation.2 | async-start | bytes 10616832 | tf_op jit(solution)/shard_map/reduce_scatter | solution.py:948
  214.1 1.3 copy-start.31
  214.1 1.9 copy-start.25
  214.8 262.1 %all-gather.7.cloned.1.call-start = ((), (), s32[]{:S(2)}) async-start(), calls=%async_computation.5 | async-start | bytes 4423680 | tf_op jit(solution)/shard_map/all_gather | solution.py:908
  216.1 5.0 %copy-start.30 = (f32[2,3,96,192]{3,2,1,0:T(8,128)S(1)}, f32[2,3,96,192]{3,2,1,0:T(8,128)}, u32[]{:S(2)}) copy-start(f32[2,3,96,192]{3,2,1,0:T(8,128)} %param.23) | copy-start | bytes 1327108
  221.0 1.9 copy-start.37
  221.0 1.9 copy-start.32
  221.0 3.4 copy-start.7
  301.3 5.2 %copy-start.34 = (f32[6,24]{1,0:T(8,128)}, f32[6,24]{1,0:T(8,128)S(1)}, u32[]{:S(2)}) copy-start(f32[6,24]{1,0:T(8,128)S(1)} %get-tuple-element.150) | copy-start | bytes 1732
  301.9 4.6 copy-start.29
  308.7 1.1 copy-start.6
  326.5 0.7 copy-start.3
  334.7 0.7 copy-start.27
  356.6 1.3 copy-start.5
  357.8 80.6 %copy-start.36 = (f32[2,2,24]{2,1,0:T(2,128)S(1)}, f32[2,2,24]{2,1,0:T(2,128)}, u32[]{:S(2)}) copy-start(f32[2,2,24]{2,1,0:T(2,128)} %param.27) | copy-start | bytes 1156
  433.5 1.4 copy-start.1
  434.9 0.8 copy-start.9
  435.7 0.7 copy-start.11
  435.7 6.0 %copy-start.13 = (f32[2,96,768]{2,1,0:T(8,128)S(1)}, f32[2,96,768]{2,1,0:T(8,128)}, u32[]{:S(2)}) copy-start(f32[2,96,768]{2,1,0:T(8,128)} %param.19) | copy-start | bytes 1769476
  435.7 6.0 %copy-start.16 = (f32[2,2,96,768]{3,2,1,0:T(8,128)S(1)}, f32[2,2,96,768]{3,2,1,0:T(8,128)}, u32[]{:S(2)}) copy-start(f32[2,2,96,768]{3,2,1,0:T(8,128)} %param.25) | copy-start | bytes 3538948
  436.4 5.3 %copy-start.10 = (f32[96,1536]{1,0:T(8,128)S(1)}, f32[96,1536]{1,0:T(8,128)}, u32[]{:S(2)}) copy-start(f32[96,1536]{1,0:T(8,128)} %copy-done.9) | copy-start | bytes 1769476
  436.7 5.1 %copy-start.41 = (f32[2,24]{1,0:T(2,128)}, f32[2,24]{1,0:T(2,128)S(1)}, u32[]{:S(2)}) copy-start(f32[2,24]{1,0:T(2,128)S(1)} %reshape_squeeze.9) | copy-start | bytes 580
  441.7 24.6 %copy-start.15 = (f32[3,96,192]{1,2,0:T(8,128)S(1)}, f32[3,96,192]{1,2,0:T(8,128)}, u32[]{:S(2)}) copy-start(f32[3,96,192]{1,2,0:T(8,128)} %copy-done.14) | copy-start | bytes 663556
  441.8 26.5 %copy-start.18 = (f32[1,3,96,192]{2,3,1,0:T(8,128)S(1)}, f32[1,3,96,192]{2,3,1,0:T(8,128)}, u32[]{:S(2)}) copy-start(f32[1,3,96,192]{2,3,1,0:T(8,128)} %copy.162) | copy-start | bytes 663556
  441.8 26.5 %copy-start.19 = (f32[1,3,96,192]{2,3,1,0:T(8,128)S(1)}, f32[1,3,96,192]{2,3,1,0:T(8,128)}, u32[]{:S(2)}) copy-start(f32[1,3,96,192]{2,3,1,0:T(8,128)} %copy.163) | copy-start | bytes 663556
  462.7 1.9 copy-start.39
  468.5 3.3 copy-start.20
  471.8 1.6 copy-start.40
  471.8 2.1 copy-start.38
  471.8 3.4 copy-start.17
  471.8 3.4 copy-start.26
  472.1 3.8 copy-start.21
  472.1 4.8 copy-start.2
  476.9 2.1 copy-start
  479.0 1.4 copy-start.4
Sparse Core Ops, SparseCore 0:
  57.8 81.6 all-gather.4
  214.1 62.0 reduce-scatter.4
  279.7 76.7 reduce-scatter.2
  358.3 39.3 all-gather.6

commit v3 on v2

--- a/solution.py
+++ b/solution.py
@@ -141,34 +141,108 @@
     )(parts, qkv)
 
 
+def on(axis, place):
+    return {"device_id": {axis: place}, "device_id_type": pl.DeviceIdType.MESH}
+
+
+def meet_all(barrier, axis, size):
+    place = lax.axis_index(axis)
+
+    def tell(k, _):
+        pl.semaphore_signal(barrier, inc=1, **on(axis, lax.rem(place + k, size)))
+        return 0
+
+    lax.fori_loop(1, size, tell, 0)
+
+
 def bwd_kernel(
     parts_ref,
     qkv_ref,
-    dot_ref,
+    own_ref,
     ot_ref,
     lse_ref,
-    out_ref,
+    x_ref,
+    tok_ref,
+    dw_ref,
+    bias_ref,
     q_s,
     qn_s,
     k_s,
     kt_s,
     v_s,
     do_s,
-    centre_s,
+    dot_s,
     corr_s,
     s_s,
     dq_s,
     dk_s,
     dv_s,
+    stage_s,
+    dwt_s,
+    in_send,
+    in_recv,
+    in_own,
+    out_send,
+    out_recv,
+    out_own,
     *,
     heads,
     length,
     unroll,
+    size,
 ):
     amount = length // BLOCK
+    tokens = length // size
+    group = 3 * HEAD
+    z = lax.axis_index("tensor")
+    barrier = pltpu.get_barrier_semaphore()
+    meet_all(barrier, "tensor", size)
+    pl.semaphore_wait(barrier, size - 1)
+
+    def taking(h, k, landing):
+        d = lax.rem(z + k, size)
+        place = d if landing is None else landing
+        return pltpu.make_async_remote_copy(
+            own_ref.at[pl.ds(pl.multiple_of((d * heads + h) * HEAD, HEAD), HEAD), :],
+            dot_s.at[h, :, pl.ds(pl.multiple_of(place * tokens, 128), tokens)],
+            in_send.at[h, k],
+            in_recv.at[h, place],
+            **on("tensor", d),
+        )
+
+    def taking_own(h):
+        return pltpu.make_async_copy(
+            own_ref.at[pl.ds(pl.multiple_of((z * heads + h) * HEAD, HEAD), HEAD), :],
+            dot_s.at[h, :, pl.ds(pl.multiple_of(z * tokens, 128), tokens)],
+            in_own.at[h],
+        )
+
+    def giving(h, k, landing):
+        d = lax.rem(z + k, size)
+        place = d if landing is None else landing
+        return pltpu.make_async_remote_copy(
+            stage_s.at[h, :, pl.ds(pl.multiple_of(d * tokens, 128), tokens)],
+            tok_ref.at[pl.ds(pl.multiple_of((place * heads + h) * group, HEAD), group), :],
+            out_send.at[h, k],
+            out_recv.at[h, place],
+            **on("tensor", d),
+        )
+
+    def giving_own(h):
+        return pltpu.make_async_copy(
+            stage_s.at[h, :, pl.ds(pl.multiple_of(z * tokens, 128), tokens)],
+            tok_ref.at[pl.ds(pl.multiple_of((z * heads + h) * group, HEAD), group), :],
+            out_own.at[h],
+        )
+
+    for h in range(heads):
+        for k in range(1, size):
+            taking(h, k, z).start()
+        taking_own(h).start()
+
     for h in range(heads):
         for_q, for_k = pos_features(length, [parts_ref[h, i] for i in range(3)])
-        base = h * 3 * HEAD
+        base = h * group
         q = qkv_ref[:, base : base + HEAD].astype(f32) * HEAD**-0.5
         k = qkv_ref[:, base + HEAD : base + 2 * HEAD].astype(f32)
         v = qkv_ref[:, base + 2 * HEAD : base + 3 * HEAD]
@@ -180,16 +254,19 @@
         k_s[h] = jnp.concatenate([k, for_k], axis=1).astype(bf16)
         kt_s[h] = k.T.astype(bf16)
         v_s[h] = v
-        grad = dot_ref[h].astype(f32)
-        do_s[h] = grad.T.astype(bf16)
-        centre_s[h] = jnp.sum(grad * ot_ref[h].astype(f32), axis=0, keepdims=True)
     late = key_after_query(BLOCK)
 
     def head(h, _):
         corr_s[...] = 2.0 * (parts_ref[h, 0] + parts_ref[h, 1] + parts_ref[h, 2]) * late
         dq_s[...] = jnp.zeros_like(dq_s)
-
-        def group(g, _):
+        for k in range(1, size):
+            taking(h, k, None).wait_recv()
+        taking_own(h).wait()
+        grad = dot_s[h].astype(f32)
+        do_s[...] = grad.T.astype(bf16)
+        centre = jnp.sum(grad * ot_ref[h].astype(f32), axis=0, keepdims=True)
+
+        def part(g, _):
             for u in range(unroll):
                 c = g * unroll + u
                 rows = pl.ds(pl.multiple_of(c * BLOCK, BLOCK), BLOCK)
@@ -203,53 +280,83 @@
                 c = g * unroll + u
                 rows = pl.ds(pl.multiple_of(c * BLOCK, BLOCK), BLOCK)
                 p = jnp.exp(s_s[u] - lse_ref[h])
-                dp = dot(v_s[h, rows, :], dot_ref[h], 1, 0)
-                dv_s[rows, :] = dot(p.astype(bf16), do_s[h], 1, 0)
-                ds = (p * (dp - centre_s[h])).astype(bf16)
+                dp = dot(v_s[h, rows, :], dot_s[h], 1, 0)
+                dv_s[rows, :] = dot(p.astype(bf16), do_s[...], 1, 0)
+                ds = (p * (dp - centre)).astype(bf16)
                 dk_s[rows, :] = dot(ds, qn_s[h], 1, 0)
                 dq_s[...] += dot(kt_s[h, :, rows], ds, 1, 0)
             return 0
 
-        lax.fori_loop(0, amount // unroll, group, 0)
-        out_ref[h, 0] = (dq_s[...] * HEAD**-0.5).astype(bf16)
-        out_ref[h, 1] = dk_s[...].T.astype(bf16)
-        out_ref[h, 2] = dv_s[...].T.astype(bf16)
+        lax.fori_loop(0, amount // unroll, part, 0)
+        stage_s[h, :HEAD] = (dq_s[...] * HEAD**-0.5).astype(bf16)
+        stage_s[h, HEAD : 2 * HEAD] = dk_s[...].T.astype(bf16)
+        stage_s[h, 2 * HEAD :] = dv_s[...].T.astype(bf16)
+        dwt_s[h] = dot(stage_s[h], x_ref[...], 1, 0)
+        bias_ref[h] = jnp.sum(stage_s[h].astype(f32), axis=1, keepdims=True)
+        for k in range(1, size):
+            giving(h, k, z).start()
+        giving_own(h).start()
         return 0
 
     lax.fori_loop(0, heads, head, 0)
-
-
-def attention_backward(parts, qkv, grad_t, out_t, lse):
-    length = qkv.shape[0]
+    for h in range(heads):
+        dw_ref[:, h * group : (h + 1) * group] = dwt_s[h].T.astype(bf16)
+    for h in range(heads):
+        for k in range(1, size):
+            taking(h, k, None).wait_send()
+            giving(h, k, None).wait_recv()
+            giving(h, k, None).wait_send()
+        giving_own(h).wait()
+
+
+def attention_backward(parts, qkv, grad_own, out_t, lse, inputs_full, size, call_id):
+    length, width = inputs_full.shape
     heads = qkv.shape[1] // (3 * HEAD)
     unroll = 2
+    tokens = length // size
     vmem = pl.BlockSpec(memory_space=pltpu.VMEM)
+    shape = jax.ShapeDtypeStruct
+    dma = pltpu.SemaphoreType.DMA
     work = heads * length * length
     return pl.pallas_call(
-        functools.partial(bwd_kernel, heads=heads, length=length, unroll=unroll),
-        out_shape=jax.ShapeDtypeStruct((heads, 3, HEAD, length), bf16),
-        in_specs=[pl.BlockSpec(memory_space=pltpu.SMEM)] + [vmem] * 4,
-        out_specs=vmem,
+        functools.partial(bwd_kernel, heads=heads, length=length, unroll=unroll, size=size),
+        out_shape=(
+            shape((size * heads * 3 * HEAD, tokens), bf16),
+            shape((width, heads * 3 * HEAD), bf16),
+            shape((heads, 3 * HEAD, 1), f32),
+        ),
+        in_specs=[pl.BlockSpec(memory_space=pltpu.SMEM)] + [vmem] * 5,
+        out_specs=(vmem, vmem, vmem),
         scratch_shapes=[
             pltpu.VMEM((heads, 2, 128, length), bf16),
             pltpu.VMEM((heads, length, HEAD), bf16),
             pltpu.VMEM((heads, length, 128), bf16),
             pltpu.VMEM((heads, HEAD, length), bf16),
             pltpu.VMEM((heads, length, HEAD), bf16),
-            pltpu.VMEM((heads, length, HEAD), bf16),
-            pltpu.VMEM((heads, 1, length), f32),
+            pltpu.VMEM((length, HEAD), bf16),
+            pltpu.VMEM((heads, HEAD, length), bf16),
             pltpu.VMEM((BLOCK, BLOCK), f32),
             pltpu.VMEM((unroll, BLOCK, length), f32),
             pltpu.VMEM((HEAD, length), f32),
             pltpu.VMEM((length, HEAD), f32),
             pltpu.VMEM((length, HEAD), f32),
+            pltpu.VMEM((heads, 3 * HEAD, length), bf16),
+            pltpu.VMEM((heads, 3 * HEAD, width), f32),
+            dma((heads, size)),
+            dma((heads, size)),
+            dma((heads,)),
+            dma((heads, size)),
+            dma((heads, size)),
+            dma((heads,)),
         ],
-        compiler_params=pltpu.CompilerParams(vmem_limit_bytes=48 * 2**20),
+        compiler_params=pltpu.CompilerParams(
+            collective_id=call_id, has_side_effects=True, vmem_limit_bytes=56 * 2**20
+        ),
         cost_estimate=pl.CostEstimate(
             flops=40 * work * HEAD, bytes_accessed=8 * qkv.size, transcendentals=work
         ),
         name="attention_backward",
-    )(parts, qkv, grad_t, out_t, lse)
+    )(parts, qkv, grad_own, out_t, lse, inputs_full)
 
 
 def normed(z):
@@ -477,20 +584,6 @@
     )(attended, inputs, cotangent, vector_rows, wall)
 
 
-def on(axis, place):
-    return {"device_id": {axis: place}, "device_id_type": pl.DeviceIdType.MESH}
-
-
-def meet_all(barrier, axis, size):
-    place = lax.axis_index(axis)
-
-    def tell(k, _):
-        pl.semaphore_signal(barrier, inc=1, **on(axis, lax.rem(place + k, size)))
-        return 0
-
-    lax.fori_loop(1, size, tell, 0)
-
-
 def gather_kernel(*refs, n_chain, n_flat, chain, flat):
     ins, refs = refs[: n_chain + n_flat], refs[n_chain + n_flat :]
     outs, refs = refs[: n_chain + n_flat], refs[n_chain + n_flat :]
@@ -902,10 +995,12 @@
     )
     own = own.reshape(width, -1)
     first_inputs, own = lax.optimization_barrier((inputs, own))
-    inputs_full, attn_chain = gather_blocks([first_inputs, attn_rows], [], n_tensor, n_dp, 1)
+    (inputs_full,) = gather_blocks([first_inputs], [], n_tensor, n_dp, 1)
     inputs_full = inputs_full.reshape(length, width)
     wall = lax.all_gather(wall_chain, "dp")
-    attn_all = lax.all_gather(attn_chain, "dp")
+    attn_all = lax.all_gather(attn_rows, ("dp", "tensor")).reshape(
+        n_dp, n_tensor, rows, -1
+    )
     if rows % 16:
         wall, attn_all = [
             w.transpose(1, 0, 2, 3).reshape(1, n_tensor, width, -1) for w in (wall, attn_all)
@@ -952,20 +1047,18 @@
     vector_sum = lax.dynamic_slice_in_dim(
         vector_all, (lax.axis_index("dp") * n_tensor + tensor_pos) * slice_width, slice_width, 1
     )
-    (grad_heads,) = collect([("lanes", "tensor")], [grad_attended], sizes, 6)
-    grad_heads = grad_heads.reshape(head_count, HEAD, length)
-    grad_qkv = attention_backward(parts, qkv, grad_heads, out_t, lse).reshape(3 * head_cols, length)
-    attn_grad = dot(inputs_full, grad_qkv, 0, 1)
-    qv_grad = jnp.sum(grad_qkv.reshape(head_count, 3, HEAD, length).astype(f32), axis=3)
+    grad_tokens, attn_grad, qv_grad = attention_backward(
+        parts, qkv, grad_attended, out_t, lse, inputs_full, n_tensor, 6
+    )
+    qv_grad = qv_grad.reshape(head_count, 3, HEAD)
     qv_grad = jnp.stack([qv_grad[:, 0], qv_grad[:, 2]]).reshape(2, n_dp, qv_cols)
     qv_grad = jnp.pad(
-        qv_grad.transpose(1, 0, 2).reshape(n_dp, 2 * qv_cols), ((0, 0), (0, rows - 2 * qv_cols))
-    ).reshape(width, 1)
-    attn_part = jnp.concatenate([attn_grad, qv_grad, jnp.zeros((width, 63), f32)], axis=1)
-    attn_part = attn_part.astype(bf16).reshape(n_dp, rows, -1)
-    grad_tokens, attn_part, glu_sum = collect(
-        [("rows", "tensor"), ("sum", "dp"), ("sum", "tensor")],
-        [grad_qkv, attn_part, glu_part],
+        qv_grad.transpose(1, 0, 2).reshape(n_dp, 1, 2 * qv_cols),
+        ((0, 0), (0, 7), (0, -2 * qv_cols % 128)),
+    )
+    qv_sum, attn_part, glu_sum = collect(
+        [("sum", "dp"), ("sum", "dp"), ("sum", "tensor")],
+        [qv_grad, attn_grad.reshape(n_dp, rows, -1), glu_part],
         sizes,
         3,
     )
@@ -974,12 +1067,11 @@
     down_sum = rest_sum[:, :hidden_cols].T
     out_sum = rest_sum[:, hidden_cols : hidden_cols + head_cols].T
     attn_sum = (
-        attn_part[:, : 3 * head_cols]
-        .reshape(rows, head_count, 3, HEAD)
+        attn_part.reshape(rows, head_count, 3, HEAD)
         .transpose(2, 0, 1, 3)
         .reshape(3, rows, head_cols)
     )
-    qv_sum = attn_part[: 2 * qv_cols, 3 * head_cols].reshape(2, qv_cols)
+    qv_sum = qv_sum[0, : 2 * qv_cols].reshape(2, qv_cols)
 
     input_grad = input_gradient(grad_tokens, grad_one, attn_all)
 

time: 503 us -> 443 us (0.88)
  Pallas kernels: 381 us -> 356 us
  waiting for transfers between devices: 20.3 us -> 0.57 us
  local copies, waits for them, and re-layouts: 38.9 us -> 26.3 us
    pallas_call x4 -> x3, Pallas kernels: 125 us -> 61.8 us  [collect(): pl.pallas_call(functools.partial(collect_kernel, ops=ops, sizes=sizes), o...]
    pallas_call x1, Pallas kernels: 41.9 us -> 84.7 us  [attention_backward(): pl.pallas_call(functools.partial(bwd_kernel, heads=heads, length=length,...]
    reduce_scatter x1, waiting for transfers between devices: 19.1 us -> 0.01 us  [local(): lax.psum_scatter(grad_glu, 'dp', scatter_dimension=0, tiled=False)]
    pallas_call x2, Pallas kernels: 105 us -> 96.7 us  [gather_blocks(): pl.pallas_call(functools.partial(gather_kernel, n_chain=len(on_chain), n_...]
    unnamed x97 -> x91, local copies, waits for them, and re-layouts: 22.5 us -> 17.4 us
  transfers between devices with their start and end apart: 4 -> 4, of which waited for: 1 -> 0; matrix products, arithmetic and copies ran while one was open for 12% -> 4% of each run, Pallas kernels for 57% -> 62%
where the time goes in v3:
time: 443 us; the launch traced here: 436 us
  Pallas kernels  356 us (80%)
  other arithmetic  32.7 us (7%)
  local copies, waits for them, and re-layouts  26.3 us (6%)
  between operations  15.9 us (4%)
  matrix products  4.51 us (1%)
    pallas_call x2, Pallas kernels, gather_blocks(): pl.pallas_call(functools.partial(gather_kernel, n_chain=len(on_chain), n_...  96.7 us
    pallas_call x1, Pallas kernels, attention_backward(): pl.pallas_call(functools.partial(bwd_kernel, heads=heads, length=length,...  84.7 us
    pallas_call x3, Pallas kernels, collect(): pl.pallas_call(functools.partial(collect_kernel, ops=ops, sizes=sizes), o...  61.8 us
    pallas_call x1, Pallas kernels, feed_forward(): pl.pallas_call(functools.partial(ff_kernel, head_cols=head_cols, hid_cols...  45.9 us
    pallas_call x2, Pallas kernels, sum_everywhere(): pl.pallas_call(functools.partial(sum_kernel, sizes=(('dp', n_dp), ('tenso...  32.3 us
    pallas_call x1, Pallas kernels, attention_forward(): pl.pallas_call(functools.partial(fwd_kernel, heads=heads, length=length,...  25.6 us
    unnamed x91, local copies, waits for them, and re-layouts  17.4 us
    pallas_call x1, Pallas kernels, input_gradient(): pl.pallas_call(input_kernel, out_shape=jax.ShapeDtypeStruct(grad_one.shap...  9.2 us
  transfers between devices with their start and end apart: 4, of which 0 were waited for; matrix products, arithmetic and copies ran while one was open for 4% of the time, Pallas kernels for 62%

profile of v3, /device:TPU:0, one launch (start us, length us, event | category | flops | bytes accessed | tf_op | source)
XLA Modules:
  0.0 436.3 jit_solution(15844567992706334012)
XLA Ops:
  7.3 1.0 copy.127
  8.3 1.4 multiply_reduce_fusion.1
  9.7 1.7 multiply_reduce_fusion.4
  11.4 1.1 copy.128
  13.3 0.8 fusion.4.refs_0_
  14.1 0.7 maximum_maximum_fusion.refs_1_
  14.9 43.6 %shard_map.318 = (bf16[4,96,2560]{2,1,0:T(8,128)(2,1)}, bf16[8,96,640]{2,1,0:T(8,128)(2,1)}) custom-call(bf16[96,2560]{1,0:T(8,128)(2,1)} %fusion.4.refs_0_, bf16[96,640]{1,0:T(8,128)(2,1)} %maximum_maximum_fusion.refs_1_), custom_call_target="tpu_custom_call" | custom-call | tf_op jit(solution)/shard_map/pallas_call | solution.py:707
  58.6 0.8 copy.137
  61.3 53.0 %shard_map.319 = bf16[4,512,768]{2,1,0:T(8,128)(2,1)} custom-call(bf16[512,768]{1,0:T(8,128)(2,1)} %x_ref.1), custom_call_target="tpu_custom_call" | custom-call | tf_op jit(solution)/shard_map/pallas_call | solution.py:707
  115.1 4.5 %add_convert_fusion.qkv_ref = bf16[2048,576]{1,0:T(8,128)(2,1)S(1)} fusion(bf16[2048,768]{1,0:T(8,128)(2,1)} %bitcast.182, f32[576]{0:T(1024)S(1)} %add.142, bf16[768,640]{1,0:T(8,128)(2,1)S(1)} %bitcast.186), kind=kOutput, calls=%fused_computation | convolution fusion | flops 1814298624 | bytes 6490368 | tf_op jit(solution)/shard_map/dot_general | solution.py:28
  119.6 25.6 %attention_forward.1 = (bf16[3,64,2048]{2,1,0:T(8,128)(2,1)S(1)}, f32[3,1,2048]{2,1,0:T(1,128)S(1)}) custom-call(f32[3,3]{1,0:T(4,128)S(1)} %constant_dynamic-slice_fusion.1.parts_ref, bf16[2048,576]{1,0:T(8,128)(2,1)S(1)} %add_convert_fusion.qkv_ref), custom_call_target="tpu_custom_call" | custom-call | flops 12884901888 | bytes 4718592 | tf_op jit(solution)/shard_map/attention_forward/pallas_call | solution.py:121
  145.3 16.7 %shard_map.320.att_ref = bf16[768,512]{1,0:T(8,128)(2,1)S(1)} custom-call(bf16[192,2048]{1,0:T(8,128)(2,1)S(1)} %bitcast.179), custom_call_target="tpu_custom_call" | custom-call | tf_op jit(solution)/shard_map/pallas_call | solution.py:806
  162.0 0.9 copy-done.7
  163.5 45.9 %feed_forward.1 = (bf16[512,768]{1,0:T(8,128)(2,1)}, f32[512,768]{1,0:T(8,128)}, bf16[768,512]{1,0:T(8,128)(2,1)}, f32[8,768]{1,0:T(8,128)}, bf16[8,4,96,1536]{3...) custom-call(bf16[768,512]{1,0:T(8,128)(2,1)} %copy-done.7, bf16[512,768]{1,0:T(8,128)(2,1)} %x_ref.1, ...), custom_call_target="tpu_custom_call" | custom-call | flops 23555211264 | bytes 31457280 | tf_op jit(solution)/shard_map/feed_forward/pallas_call | solution.py:544
  212.2 84.7 %attention_backward.1 = (bf16[2304,512]{1,0:T(8,128)(2,1)}, bf16[768,576]{1,0:T(8,128)(2,1)}, f32[3,192,1]{2,1,0:T(8,128)}) custom-call(f32[3,3]{1,0:T(4,128)} %copy-done.8, bf16[2048,576]{1,0:T(8,128)(2,1)} %copy-done.9, bf16[768,512]{1,0:T(8,128)(2,1)} %get-tuple-element.46.own_ref, bf16[3,64,2048]{2,1,0:T(8,128)(2,1)} %copy-done.6, ...), custom_call_target="tpu_custom_call" | custom-call | flops 32212254720 | bytes 9437184 | tf_op jit(solution)/shard_map/attention_backward/pallas_call | solution.py:321
  296.9 1.1 reduce.7
  298.5 16.1 %shard_map.323 = f32[8,768]{1,0:T(8,128)} custom-call(f32[8,768]{1,0:T(8,128)} %get-tuple-element.57.in_ref), custom_call_target="tpu_custom_call" | custom-call | tf_op jit(solution)/shard_map/pallas_call | solution.py:909
  314.6 1.5 multiply_reduce_fusion.8
  317.3 1.4 concatenate.15
  318.7 2.3 copy-done
  321.0 1.7 copy-done.1
  322.7 9.2 %input_gradient.1 = f32[512,768]{1,0:T(8,128)} custom-call(bf16[2304,512]{1,0:T(8,128)(2,1)S(1)} %copy-done.1, f32[512,768]{1,0:T(8,128)S(1)} %copy-done.2, bf16[8,4,96,576]{3,2,1,0:T(8,128)(2,1)S(1)} %bitcast.175), custom_call_target="tpu_custom_call" | custom-call | flops 1811939328 | bytes 8257536 | tf_op jit(solution)/shard_map/input_gradient/pallas_call | solution.py:843
  332.0 1.2 copy-done.5
  333.1 17.8 %shard_map.322 = f32[96,1024]{1,0:T(8,128)S(1)} custom-call(bf16[4,96,1024]{2,1,0:T(8,128)(2,1)S(1)} %bitcast.178), custom_call_target="tpu_custom_call" | custom-call | tf_op jit(solution)/shard_map/pallas_call | solution.py:806
  351.7 0.8 copy.157
  352.5 0.7 copy.155
  353.2 1.5 multiply_reduce_fusion.2
  354.9 0.9 pad_maximum_fusion.2
  355.8 1.3 copy-done.3
  357.0 27.3 %shard_map.321 = (f32[8,128]{1,0:T(8,128)S(1)}, f32[96,576]{1,0:T(8,128)S(1)}, f32[96,1536]{1,0:T(8,128)S(1)}) custom-call(f32[8,8,128]{2,1,0:T(8,128)S(1)} %pad.26.refs_0_, bf16[8,96,576]{2,1,0:T(8,128)(2,1)S(1)} %bitcast.177, bf16[4,96,1536]{2,1,0:T(8,128)(2,1)S(1)} %bitcast.176), custom_call_target="tpu_custom_call" | custom-call | tf_op jit(solution)/shard_map/pallas_call | solution.py:806
  385.2 2.6 multiply_reduce_fusion
  388.6 0.9 multiply_reduce_fusion.3
  389.5 1.4 concatenate.16
  391.5 16.2 %shard_map.324 = f32[8,128]{1,0:T(8,128)} custom-call(f32[8,128]{1,0:T(8,128)} %select_maximum_fusion.in_ref), custom_call_target="tpu_custom_call" | custom-call | tf_op jit(solution)/shard_map/pallas_call | solution.py:909
  410.8 0.9 multiply_add_fusion.4
  413.1 0.7 copy.160
  413.8 1.1 multiply_subtract_fusion.2
  414.9 0.9 copy.159
  415.8 0.7 reshape_squeeze.10
  417.1 2.2 fusion.14
  419.4 1.1 copy.156
  420.5 0.9 copy.154
  421.3 1.3 multiply_subtract_fusion.4
  422.7 1.3 multiply_subtract_fusion.5
  424.0 1.7 multiply_subtract_fusion.1
  425.7 1.5 multiply_subtract_fusion
  427.2 1.3 pad_maximum_fusion.6
  428.5 1.1 pad_maximum_fusion
  (153 shorter events, 15.2 us)
Async XLA Ops:
  7.2 5.6 %copy-start.31 = (f32[2,24]{1,0:T(2,128)S(1)}, f32[2,24]{1,0:T(2,128)}, u32[]{:S(2)}) copy-start(f32[2,24]{1,0:T(2,128)} %param.21) | copy-start | bytes 580
  7.2 5.9 %copy-start.27 = (f32[6,96]{1,0:T(8,128)S(1)}, f32[6,96]{1,0:T(8,128)}, u32[]{:S(2)}) copy-start(f32[6,96]{1,0:T(8,128)} %param.22) | copy-start | bytes 6916
  7.2 156.3 %all-gather.6.cloned.1.call-start = ((), (), s32[]{:S(2)}) async-start(), calls=%async_computation.5 | async-start | bytes 17694720 | tf_op jit(solution)/shard_map/all_gather | solution.py:1000
  12.5 46.9 %copy-start.12 = (f32[3,96,192]{1,2,0:T(8,128)}, f32[3,96,192]{1,2,0:T(8,128)S(1)}, u32[]{:S(2)}) copy-start(f32[3,96,192]{1,2,0:T(8,128)S(1)} %copy.128) | copy-start | bytes 663556
  58.5 1.2 copy-start.19
  58.6 260.1 %all-gather.4.cloned.1.call-start = ((), (), s32[]{:S(2)}) async-start(), calls=%async_computation.2 | async-start | bytes 4055040 | tf_op jit(solution)/shard_map/all_gather | solution.py:1001
  59.4 272.5 %reduce-scatter.5.cloned.1.call-start = ((), (), s32[]{:S(2)}) async-start(), calls=%async_computation.4 | async-start | bytes 7077888 | tf_op jit(solution)/shard_map/reduce_scatter | solution.py:1044
  115.1 4.5 %copy-start.8 = (f32[3,3]{1,0:T(4,128)}, f32[3,3]{1,0:T(4,128)S(1)}, u32[]{:S(2)}) copy-start(f32[3,3]{1,0:T(4,128)S(1)} %constant_dynamic-slice_fusion.1.parts_ref) | copy-start | bytes 112
  119.6 25.6 %copy-start.9 = (bf16[2048,576]{1,0:T(8,128)(2,1)}, bf16[2048,576]{1,0:T(8,128)(2,1)S(1)}, u32[]{:S(2)}) copy-start(bf16[2048,576]{1,0:T(8,128)(2,1)S(1)} %add_convert_fusion.qkv_ref) | copy-start | bytes 7077892
  145.2 16.7 %copy-start.10 = (f32[3,1,2048]{2,1,0:T(1,128)}, f32[3,1,2048]{2,1,0:T(1,128)S(1)}, u32[]{:S(2)}) copy-start(f32[3,1,2048]{2,1,0:T(1,128)S(1)} %get-tuple-element.47.lse_ref) | copy-start | bytes 73732
  145.3 64.1 %copy-start.6 = (bf16[3,64,2048]{2,1,0:T(8,128)(2,1)}, bf16[3,64,2048]{2,1,0:T(8,128)(2,1)S(1)}, u32[]{:S(2)}) copy-start(bf16[3,64,2048]{2,1,0:T(8,128)(2,1)S(1)} %get-tuple-element.43.ot_ref) | copy-start | bytes 2359300
  162.0 0.9 copy-start.7
  209.4 146.4 %reduce-scatter.3.cloned.1.call-start = ((), (), s32[]{:S(2)}) async-start(), calls=%async_computation.3 | async-start | bytes 10616832 | tf_op jit(solution)/shard_map/reduce_scatter | solution.py:1043
  209.4 1.1 copy-start.24
  209.4 1.4 copy-start.26
  210.5 0.9 copy-start.25
  210.5 1.5 copy-start.20
  210.5 1.7 copy-start.35
  212.2 106.5 %copy-start.2 = (f32[512,768]{1,0:T(8,128)S(1)}, f32[512,768]{1,0:T(8,128)}, u32[]{:S(2)}) copy-start(f32[512,768]{1,0:T(8,128)} %get-tuple-element.49.grad_ref) | copy-start | bytes 4718596
  316.1 0.6 copy-start.30
  318.7 2.3 copy-start
  321.0 1.7 copy-start.1
  322.7 30.5 %copy-start.15 = (f32[768,96]{0,1:T(8,128)S(1)}, f32[768,96]{0,1:T(8,128)}, u32[]{:S(2)}) copy-start(f32[768,96]{0,1:T(8,128)} %param.20) | copy-start | bytes 884740
  332.0 1.2 copy-start.5
  333.1 20.1 %copy-start.16 = (f32[2,768,96]{1,2,0:T(8,128)S(1)}, f32[2,768,96]{1,2,0:T(8,128)}, u32[]{:S(2)}) copy-start(f32[2,768,96]{1,2,0:T(8,128)} %param.26) | copy-start | bytes 1769476
  351.6 4.1 copy-start.4
  354.7 1.0 copy-start.21
  354.9 30.3 %copy-start.11 = (f32[2,96,768]{2,1,0:T(8,128)S(1)}, f32[2,96,768]{2,1,0:T(8,128)}, u32[]{:S(2)}) copy-start(f32[2,96,768]{2,1,0:T(8,128)} %param.19) | copy-start | bytes 1769476
  355.8 1.3 copy-start.3
  384.4 3.5 copy-start.32
  384.4 3.5 copy-start.34
  384.4 4.2 copy-start.13
  385.2 2.7 copy-start.38
  387.9 29.2 %copy-start.14 = (f32[2,2,96,768]{3,2,1,0:T(8,128)S(1)}, f32[2,2,96,768]{3,2,1,0:T(8,128)}, u32[]{:S(2)}) copy-start(f32[2,2,96,768]{3,2,1,0:T(8,128)} %param.25) | copy-start | bytes 3538948
  408.4 8.7 %copy-start.37 = (f32[2,15]{1,0:T(2,128)}, f32[2,15]{1,0:T(2,128)S(1)}, u32[]{:S(2)}) copy-start(f32[2,15]{1,0:T(2,128)S(1)} %add_sqrt_fusion) | copy-start | bytes 364
  416.5 2.8 copy-start.22
  416.5 2.8 copy-start.23
  417.1 4.2 copy-start.28
  417.1 4.2 copy-start.29
  417.1 5.6 %copy-start.33 = (f32[2,24]{1,0:T(2,128)S(1)}, f32[2,24]{1,0:T(2,128)}, u32[]{:S(2)}) copy-start(f32[2,24]{1,0:T(2,128)} %param.21) | copy-start | bytes 580
  417.1 5.6 %copy-start.36 = (f32[2,24]{1,0:T(2,128)S(1)}, f32[2,24]{1,0:T(2,128)}, u32[]{:S(2)}) copy-start(f32[2,24]{1,0:T(2,128)} %get-tuple-element.154) | copy-start | bytes 580
  419.3 6.4 %copy-start.18 = (f32[2,96,768]{2,1,0:T(8,128)S(1)}, f32[2,96,768]{2,1,0:T(8,128)}, u32[]{:S(2)}) copy-start(f32[2,96,768]{2,1,0:T(8,128)} %get-tuple-element.159) | copy-start | bytes 1769476
  419.3 9.1 %copy-start.17 = (f32[1,2,96,768]{3,2,1,0:T(8,128)S(1)}, f32[1,2,96,768]{3,2,1,0:T(8,128)}, u32[]{:S(2)}) copy-start(f32[1,2,96,768]{3,2,1,0:T(8,128)} %get-tuple-element.166) | copy-start | bytes 1769476
Sparse Core Ops, SparseCore 0:
  58.7 81.6 all-gather.5
  143.7 63.5 all-gather.3
  210.7 62.2 reduce-scatter.4
  276.4 78.9 reduce-scatter.2

commit v4 on v3

--- a/solution.py
+++ b/solution.py
@@ -142,11 +142,22 @@
 
 
 def on(axis, place):
-    return {"device_id": {axis: place}, "device_id_type": pl.DeviceIdType.MESH}
+    if axis == "all":
+        n = lax.axis_size("tensor")
+        at = {"dp": lax.div(place, n), "tensor": lax.rem(place, n)}
+    else:
+        at = {axis: place}
+    return {"device_id": at, "device_id_type": pl.DeviceIdType.MESH}
+
+
+def place_on(axis):
+    if axis == "all":
+        return lax.axis_index("dp") * lax.axis_size("tensor") + lax.axis_index("tensor")
+    return lax.axis_index(axis)
 
 
 def meet_all(barrier, axis, size):
-    place = lax.axis_index(axis)
+    place = place_on(axis)
 
     def tell(k, _):
         pl.semaphore_signal(barrier, inc=1, **on(axis, lax.rem(place + k, size)))
@@ -162,9 +173,13 @@
     ot_ref,
     lse_ref,
     x_ref,
+    grad_ref,
+    vec_ref,
     tok_ref,
     dw_ref,
     bias_ref,
+    sum_ref,
+    vsum_ref,
     q_s,
     qn_s,
     k_s,
@@ -182,14 +197,26 @@
     in_send,
     in_recv,
     in_own,
-    out_send,
-    out_recv,
+    kv_send,
+    kv_recv,
+    q_send,
+    q_recv,
     out_own,
+    first_own,
+    first_got,
+    second_got,
+    load_sem,
+    sum_send,
+    sum_recv,
+    vec_got,
+    vec_send,
+    vec_recv,
     *,
     heads,
     length,
     unroll,
     size,
+    paired,
 ):
     amount = length // BLOCK
     tokens = length // size
@@ -197,7 +224,53 @@
     z = lax.axis_index("tensor")
     barrier = pltpu.get_barrier_semaphore()
     meet_all(barrier, "tensor", size)
-    pl.semaphore_wait(barrier, size - 1)
+    met = size - 1
+    if paired:
+        p = lax.axis_index("dp")
+        x = lax.rem(lax.div(p, 2), 2)
+        y = lax.div(p, 4)
+        partners = (p + 2 - 4 * x, p + 4 - 8 * y)
+        for partner in partners:
+            pl.semaphore_signal(barrier, inc=1, **on("dp", partner))
+        met += 2
+    pl.semaphore_wait(barrier, met)
+    part = size // 2
+
+    def blocks(way, place, other):
+        index = 2 * other + place if way == 0 else 2 * place + other
+        return grad_ref.at[index, way * part : (way + 1) * part]
+
+    def first(way, other):
+        place = (x, y)[way]
+        return pltpu.make_async_remote_copy(
+            blocks(way, 1 - place, other),
+            first_got.at[way, other],
+            sum_send.at[0, way, other],
+            sum_recv.at[0, way, other],
+            **on("dp", partners[way]),
+        )
+
+    def first_load(way, other):
+        return pltpu.make_async_copy(
+            blocks(way, (x, y)[way], other), first_own.at[way, other], load_sem.at[way, other]
+        )
+
+    def second(way):
+        place = (y, x)[way]
+        return pltpu.make_async_remote_copy(
+            first_got.at[way, 1 - place],
+            second_got.at[way],
+            sum_send.at[1, way, 0],
+            sum_recv.at[1, way, 0],
+            **on("dp", partners[1 - way]),
+        )
+
+    def telling(k, landing):
+        d = lax.rem(z + k, size)
+        place = d if landing is None else landing
+        return pltpu.make_async_remote_copy(
+            vec_ref, vec_got.at[place], vec_send.at[k], vec_recv.at[place], **on("tensor", d)
+        )
 
     def taking(h, k, landing):
         d = lax.rem(z + k, size)
@@ -217,14 +290,18 @@
             in_own.at[h],
         )
 
-    def giving(h, k, landing):
+    def giving(h, k, landing, keys):
         d = lax.rem(z + k, size)
         place = d if landing is None else landing
+        low, count = (HEAD, 2 * HEAD) if keys else (0, HEAD)
+        send, recv = (kv_send, kv_recv) if keys else (q_send, q_recv)
         return pltpu.make_async_remote_copy(
-            stage_s.at[h, :, pl.ds(pl.multiple_of(d * tokens, 128), tokens)],
-            tok_ref.at[pl.ds(pl.multiple_of((place * heads + h) * group, HEAD), group), :],
-            out_send.at[h, k],
-            out_recv.at[h, place],
+            stage_s.at[h, low : low + count, pl.ds(pl.multiple_of(d * tokens, 128), tokens)],
+            tok_ref.at[
+                pl.ds(pl.multiple_of((place * heads + h) * group + low, HEAD), count), :
+            ],
+            send.at[h, k],
+            recv.at[h, place],
             **on("tensor", d),
         )
 
@@ -239,6 +316,13 @@
         for k in range(1, size):
             taking(h, k, z).start()
         taking_own(h).start()
+    for k in range(1, size):
+        telling(k, z).start()
+    if paired:
+        for way in range(2):
+            for other in range(2):
+                first(way, other).start()
+                first_load(way, other).start()
 
     for h in range(heads):
         for_q, for_k = pos_features(length, [parts_ref[h, i] for i in range(3)])
@@ -265,8 +349,15 @@
         grad = dot_s[h].astype(f32)
         do_s[...] = grad.T.astype(bf16)
         centre = jnp.sum(grad * ot_ref[h].astype(f32), axis=0, keepdims=True)
-
-        def part(g, _):
+        if paired:
+
+            @pl.when(h == heads - 1)
+            def _():
+                for way in range(2):
+                    second(way).start()
+
+        def owner(i, _):
+            g = lax.rem(z + 1 + i, size)
             for u in range(unroll):
                 c = g * unroll + u
                 rows = pl.ds(pl.multiple_of(c * BLOCK, BLOCK), BLOCK)
@@ -276,26 +367,45 @@
                     cols = slice(i * BLOCK, (i + 1) * BLOCK)
                     s_s[u, :, cols] = dot(keys, q_s[h, after, :, cols], 1, 0)
                 s_s[u, :, rows] = s_s[u, :, rows] - corr_s[...]
+
             for u in range(unroll):
                 c = g * unroll + u
                 rows = pl.ds(pl.multiple_of(c * BLOCK, BLOCK), BLOCK)
+                here = slice(u * BLOCK, (u + 1) * BLOCK)
                 p = jnp.exp(s_s[u] - lse_ref[h])
                 dp = dot(v_s[h, rows, :], dot_s[h], 1, 0)
-                dv_s[rows, :] = dot(p.astype(bf16), do_s[...], 1, 0)
+                dv_s[here, :] = dot(p.astype(bf16), do_s[...], 1, 0)
                 ds = (p * (dp - centre)).astype(bf16)
-                dk_s[rows, :] = dot(ds, qn_s[h], 1, 0)
+                dk_s[here, :] = dot(ds, qn_s[h], 1, 0)
                 dq_s[...] += dot(kt_s[h, :, rows], ds, 1, 0)
+            lanes = pl.ds(pl.multiple_of(g * tokens, 128), tokens)
+            stage_s[h, HEAD : 2 * HEAD, lanes] = dk_s[...].T.astype(bf16)
+            stage_s[h, 2 * HEAD :, lanes] = dv_s[...].T.astype(bf16)
             return 0
 
-        lax.fori_loop(0, amount // unroll, part, 0)
+        lax.fori_loop(0, size, owner, 0)
         stage_s[h, :HEAD] = (dq_s[...] * HEAD**-0.5).astype(bf16)
-        stage_s[h, HEAD : 2 * HEAD] = dk_s[...].T.astype(bf16)
-        stage_s[h, 2 * HEAD :] = dv_s[...].T.astype(bf16)
         dwt_s[h] = dot(stage_s[h], x_ref[...], 1, 0)
         bias_ref[h] = jnp.sum(stage_s[h].astype(f32), axis=1, keepdims=True)
         for k in range(1, size):
-            giving(h, k, z).start()
+            giving(h, k, z, True).start()
+            giving(h, k, z, False).start()
         giving_own(h).start()
+        if paired:
+
+            @pl.when(h == heads - 2)
+            def _():
+                for way in range(2):
+                    for other in range(2):
+                        first(way, other).wait_recv()
+                        first(way, other).wait_send()
+                        first_load(way, other).wait()
+                        for t in range(part):
+                            first_got[way, other, t] = (
+                                first_got[way, other, t].astype(f32)
+                                + first_own[way, other, t].astype(f32)
+                            ).astype(bf16)
+
         return 0
 
     lax.fori_loop(0, heads, head, 0)
@@ -304,29 +414,55 @@
     for h in range(heads):
         for k in range(1, size):
             taking(h, k, None).wait_send()
-            giving(h, k, None).wait_recv()
-            giving(h, k, None).wait_send()
+            for keys in (True, False):
+                giving(h, k, None, keys).wait_recv()
+                giving(h, k, None, keys).wait_send()
         giving_own(h).wait()
-
-
-def attention_backward(parts, qkv, grad_own, out_t, lse, inputs_full, size, call_id):
+    vsum_ref[...] = vec_ref[...]
+    for k in range(1, size):
+        telling(k, None).wait_recv()
+        telling(k, None).wait_send()
+        vsum_ref[...] += vec_got[lax.rem(z + k, size)]
+    if paired:
+        for way in range(2):
+            second(way).wait_recv()
+            second(way).wait_send()
+            place = (y, x)[way]
+            for t in range(part):
+                sum_ref[way * part + t] = (
+                    first_got[way, place, t].astype(f32) + second_got[way, t].astype(f32)
+                ).astype(bf16)
+    else:
+        sum_ref[...] = jnp.zeros_like(sum_ref)
+
+
+def attention_backward(
+    parts, qkv, grad_own, out_t, lse, inputs_full, grad_sums, vector_part, size, paired, call_id
+):
     length, width = inputs_full.shape
     heads = qkv.shape[1] // (3 * HEAD)
-    unroll = 2
     tokens = length // size
+    unroll = tokens // BLOCK
+    half = (2, 2, size // 2) + (grad_sums.shape[2:] if paired else (16, 128))
     vmem = pl.BlockSpec(memory_space=pltpu.VMEM)
     shape = jax.ShapeDtypeStruct
     dma = pltpu.SemaphoreType.DMA
     work = heads * length * length
     return pl.pallas_call(
-        functools.partial(bwd_kernel, heads=heads, length=length, unroll=unroll, size=size),
+        functools.partial(
+            bwd_kernel, heads=heads, length=length, unroll=unroll, size=size, paired=paired
+        ),
         out_shape=(
             shape((size * heads * 3 * HEAD, tokens), bf16),
             shape((width, heads * 3 * HEAD), bf16),
             shape((heads, 3 * HEAD, 1), f32),
+            shape((size,) + half[3:], bf16),
+            shape(vector_part.shape, f32),
         ),
-        in_specs=[pl.BlockSpec(memory_space=pltpu.SMEM)] + [vmem] * 5,
-        out_specs=(vmem, vmem, vmem),
+        in_specs=[pl.BlockSpec(memory_space=pltpu.SMEM)]
+        + [vmem] * 5
+        + [pl.BlockSpec(memory_space=pl.ANY), vmem],
+        out_specs=(vmem,) * 5,
         scratch_shapes=[
             pltpu.VMEM((heads, 2, 128, length), bf16),
             pltpu.VMEM((heads, length, HEAD), bf16),
@@ -338,8 +474,8 @@
             pltpu.VMEM((BLOCK, BLOCK), f32),
             pltpu.VMEM((unroll, BLOCK, length), f32),
             pltpu.VMEM((HEAD, length), f32),
-            pltpu.VMEM((length, HEAD), f32),
-            pltpu.VMEM((length, HEAD), f32),
+            pltpu.VMEM((tokens, HEAD), f32),
+            pltpu.VMEM((tokens, HEAD), f32),
             pltpu.VMEM((heads, 3 * HEAD, length), bf16),
             pltpu.VMEM((heads, 3 * HEAD, width), f32),
             dma((heads, size)),
@@ -347,7 +483,18 @@
             dma((heads,)),
             dma((heads, size)),
             dma((heads, size)),
+            dma((heads, size)),
+            dma((heads, size)),
             dma((heads,)),
+            pltpu.VMEM(half, bf16),
+            pltpu.VMEM(half, bf16),
+            pltpu.VMEM(half[1:], bf16),
+            dma((2, 2)),
+            dma((2, 2, 2)),
+            dma((2, 2, 2)),
+            pltpu.VMEM((size,) + vector_part.shape, f32),
+            dma((size,)),
+            dma((size,)),
         ],
         compiler_params=pltpu.CompilerParams(
             collective_id=call_id, has_side_effects=True, vmem_limit_bytes=56 * 2**20
@@ -356,7 +503,7 @@
             flops=40 * work * HEAD, bytes_accessed=8 * qkv.size, transcendentals=work
         ),
         name="attention_backward",
-    )(parts, qkv, grad_own, out_t, lse, inputs_full)
+    )(parts, qkv, grad_own, out_t, lse, inputs_full, grad_sums, vector_part)
 
 
 def normed(z):
@@ -381,8 +528,7 @@
     dz1_ref,
     do_ref,
     dvec_ref,
-    gglu_ref,
-    grest_ref,
+    gall_ref,
     wgu_s,
     wd_s,
     wo_s,
@@ -400,11 +546,17 @@
     sglu_s,
     sdown_s,
     sout_s,
+    rglu_s,
+    rdown_s,
+    rout_s,
     load_sem,
     store_sem,
+    pair_send,
+    pair_recv,
     *,
     head_cols,
     hid_cols,
+    paired,
 ):
     n_row, n_t, rows = wall_ref.shape[:3]
     width = h1_s.shape[1]
@@ -423,18 +575,64 @@
             for p in range(n_row)
         ]
 
+    staged = (sglu_s, sdown_s, sout_s)
+    received = (rglu_s, rdown_s, rout_s)
+    n_out = n_row // 2 if paired else n_row
+    if paired:
+        p = lax.axis_index("dp")
+        core = lax.rem(p, 2)
+        partner = p + 1 - 2 * core
+        barrier = pltpu.get_barrier_semaphore()
+        pl.semaphore_signal(barrier, inc=1, **on("dp", partner))
+        pl.semaphore_wait(barrier, 1)
+
+    def mine(kind, q, whose):
+        return staged[kind].at[pl.ds(pl.multiple_of((2 * q + whose) * rows, 16), rows), :]
+
     def stores(kind, t):
-        source = (sglu_s, sdown_s, sout_s)[kind]
-        into = (gglu_ref, grest_ref, grest_ref)[kind]
-        low = (0, 0, hid_cols)[kind]
+        low = sum(sizes[:kind])
         return [
             pltpu.make_async_copy(
-                source.at[pl.ds(p * rows, rows), :],
-                into.at[p, t, :, pl.ds(low, sizes[kind])],
-                store_sem.at[kind, p],
+                received[kind].at[t, pl.ds(q * rows, rows), :]
+                if paired
+                else staged[kind].at[pl.ds(q * rows, rows), :],
+                gall_ref.at[q, t, :, pl.ds(low, sizes[kind])],
+                store_sem.at[kind, t, q],
             )
-            for p in range(n_row)
+            for q in range(n_out)
         ]
+
+    def swaps(kind, t):
+        return [
+            pltpu.make_async_remote_copy(
+                mine(kind, q, 1 - core),
+                received[kind].at[t, pl.ds(q * rows, rows), :],
+                pair_send.at[kind, t, q],
+                pair_recv.at[kind, t, q],
+                **on("dp", partner),
+            )
+            for q in range(n_out)
+        ]
+
+    def begin(kind, t):
+        for copy in swaps(kind, t) if paired else stores(kind, t):
+            copy.start()
+
+    def finish(kind, t):
+        if not paired:
+            for copy in stores(kind, t):
+                copy.wait()
+            return
+        for copy in swaps(kind, t):
+            copy.wait_send()
+            copy.wait_recv()
+        for q in range(n_out):
+            here = pl.ds(q * rows, rows)
+            received[kind][t, here, :] = (
+                received[kind][t, here, :].astype(f32) + mine(kind, q, core)[...].astype(f32)
+            ).astype(bf16)
+        for copy in stores(kind, t):
+            copy.start()
 
     for kind in (2, 0, 1):
         for t in range(n_t):
@@ -485,25 +683,24 @@
     acc_s[...] = dz2
 
     def backward(t, _):
-        def waits(kind):
-            @pl.when(t > 0)
-            def _():
-                for copy in stores(kind, t - 1):
-                    copy.wait()
-
-        waits(1)
+        @pl.when(t > 0)
+        def _():
+            finish(1, t - 1)
+
         sdown_s[...] = dot(dft_s[...], hid_s[t], 1, 0).astype(bf16)
-        for copy in stores(1, t):
-            copy.start()
         dh = dot(df_s[...], wd_s[t], 1, 0)
         dg = (dh * der_s[t]).astype(bf16)
         du = (dh * act_s[t]).astype(bf16)
-        acc_s[...] += dot(dg, wgu_s[t, :, :hid_cols], 1, 1) + dot(du, wgu_s[t, :, hid_cols:], 1, 1)
-        waits(0)
+        begin(1, t)
+
+        @pl.when(t > 0)
+        def _():
+            finish(0, t - 1)
+
         sglu_s[:, :hid_cols] = dot(h1t_s[...], dg, 1, 0).astype(bf16)
         sglu_s[:, hid_cols:] = dot(h1t_s[...], du, 1, 0).astype(bf16)
-        for copy in stores(0, t):
-            copy.start()
+        acc_s[...] += dot(dg, wgu_s[t, :, :hid_cols], 1, 1) + dot(du, wgu_s[t, :, hid_cols:], 1, 1)
+        begin(0, t)
         return 0
 
     lax.fori_loop(0, n_t, backward, 0)
@@ -523,36 +720,42 @@
             da, wo_s[t, :, :head_cols], 1, 0
         ).T.astype(bf16)
         if t > 0:
-            for copy in stores(2, t - 1):
-                copy.wait()
+            finish(2, t - 1)
         sout_s[:, :head_cols] = dot(dat, atn_s[t], 1, 0).astype(bf16)
-        for copy in stores(2, t):
-            copy.start()
-    for kind in range(3):
-        for copy in stores(kind, n_t - 1):
-            copy.wait()
-
-
-def feed_forward(attended, inputs, cotangent, vector_rows, wall, head_cols, hid_cols):
+        if t == 0:
+            for kind in (1, 0):
+                finish(kind, n_t - 1)
+        begin(2, t)
+    finish(2, n_t - 1)
+    if paired:
+        for kind in range(3):
+            for t in range(n_t):
+                for copy in stores(kind, t):
+                    copy.wait()
+
+
+def feed_forward(attended, inputs, cotangent, vector_rows, wall, head_cols, hid_cols, paired, call_id):
     tokens, width = inputs.shape
     n_row, n_t, rows = wall.shape[:3]
     pad = wall.shape[3] - 3 * hid_cols
+    n_out = n_row // 2 if paired else n_row
+    held = n_out * rows if paired else 16
+    dma = pltpu.SemaphoreType.DMA
     vmem = pl.BlockSpec(memory_space=pltpu.VMEM)
     hbm = pl.BlockSpec(memory_space=pl.ANY)
     shape = jax.ShapeDtypeStruct
     size = tokens * width * n_t
     return pl.pallas_call(
-        functools.partial(ff_kernel, head_cols=head_cols, hid_cols=hid_cols),
+        functools.partial(ff_kernel, head_cols=head_cols, hid_cols=hid_cols, paired=paired),
         out_shape=(
             shape((tokens, width), bf16),
             shape((tokens, width), f32),
             shape((n_t * head_cols, tokens), bf16),
             shape((8, width), f32),
-            shape((n_row, n_t, rows, 2 * hid_cols), bf16),
-            shape((n_row, n_t, rows, hid_cols + pad), bf16),
+            shape((n_out, n_t, rows, 3 * hid_cols + pad), bf16),
         ),
         in_specs=[vmem] * 4 + [hbm],
-        out_specs=(vmem, vmem, vmem, vmem, hbm, hbm),
+        out_specs=(vmem, vmem, vmem, vmem, hbm),
         scratch_shapes=[
             pltpu.VMEM((n_t, width, 2 * hid_cols), bf16),
             pltpu.VMEM((n_t, width, hid_cols), bf16),
@@ -571,10 +774,19 @@
             pltpu.VMEM((width, 2 * hid_cols), bf16),
             pltpu.VMEM((width, hid_cols), bf16),
             pltpu.VMEM((width, pad), bf16),
-            pltpu.SemaphoreType.DMA((3, n_t, n_row)),
-            pltpu.SemaphoreType.DMA((3, n_row)),
+            pltpu.VMEM((n_t, held, 2 * hid_cols), bf16),
+            pltpu.VMEM((n_t, held, hid_cols), bf16),
+            pltpu.VMEM((n_t, held, pad), bf16),
+            dma((3, n_t, n_row)),
+            dma((3, n_t, n_out)),
+            dma((3, n_t, n_out)),
+            dma((3, n_t, n_out)),
         ],
-        compiler_params=pltpu.CompilerParams(vmem_limit_bytes=63 * 2**20),
+        compiler_params=pltpu.CompilerParams(
+            collective_id=call_id if paired else None,
+            has_side_effects=True,
+            vmem_limit_bytes=63 * 2**20,
+        ),
         cost_estimate=pl.CostEstimate(
             flops=6 * size * (3 * hid_cols + head_cols),
             bytes_accessed=4 * wall.size,
@@ -722,103 +934,7 @@
     )(*arrays)
 
 
-def collect_kernel(*refs, ops, sizes):
-    count = len(ops)
-    ins, outs, refs = refs[:count], refs[count : 2 * count], refs[2 * count :]
-    sums = [i for i, (kind, _) in enumerate(ops) if kind == "sum"]
-    got = dict(zip(sums, refs))
-    send_sem, recv_sem, local_sem = refs[len(sums) :]
-    barrier = pltpu.get_barrier_semaphore()
-    axes = sorted({axis for _, axis in ops})
-    for axis in axes:
-        meet_all(barrier, axis, sizes[axis])
-    pl.semaphore_wait(barrier, sum(sizes[axis] - 1 for axis in axes))
-
-    def cut_lanes(ref, index, size):
-        lanes = ref.shape[1] // size
-        return ref.at[:, pl.ds(pl.multiple_of(index * lanes, 128), lanes)]
-
-    def cut_rows(ref, index, size):
-        rows = ref.shape[0] // size
-        return ref.at[pl.ds(pl.multiple_of(index * rows, 16), rows), :]
-
-    def cuts(i, source, target):
-        kind, axis = ops[i]
-        size = sizes[axis]
-        if kind == "rows":
-            return cut_lanes(ins[i], source, size), cut_rows(outs[i], target, size)
-        if kind == "lanes":
-            return cut_rows(ins[i], source, size), cut_lanes(outs[i], target, size)
-        return ins[i].at[source], got[i].at[target]
-
-    def copy(i, k, landing):
-        axis = ops[i][1]
-        d = lax.rem(lax.axis_index(axis) + k, sizes[axis])
-        place = d if landing is None else landing
-        source, target = cuts(i, d, place)
-        return pltpu.make_async_remote_copy(
-            source, target, send_sem.at[i, k], recv_sem.at[i, place], **on(axis, d)
-        )
-
-    def own(i):
-        z = lax.axis_index(ops[i][1])
-        return pltpu.make_async_copy(*cuts(i, z, z), local_sem.at[i])
-
-    for i, (kind, axis) in enumerate(ops):
-
-        def push(k, _):
-            copy(i, k, lax.axis_index(axis)).start()
-            return 0
-
-        lax.fori_loop(1, sizes[axis], push, 0)
-        if kind != "sum":
-            own(i).start()
-    for i, (kind, axis) in enumerate(ops):
-        if kind == "sum":
-            outs[i][...] = ins[i][lax.axis_index(axis)].astype(f32)
-
-        def take(k, _):
-            copy(i, k, None).wait_recv()
-            if kind == "sum":
-                outs[i][...] += got[i][lax.rem(lax.axis_index(axis) + k, sizes[axis])].astype(f32)
-            copy(i, k, None).wait_send()
-            return 0
-
-        lax.fori_loop(1, sizes[axis], take, 0)
-        if kind != "sum":
-            own(i).wait()
-
-
-def collect(ops, arrays, sizes, call_id):
-    def shape_of(op, a):
-        kind, axis = op
-        n = sizes[axis]
-        if kind == "rows":
-            return jax.ShapeDtypeStruct((a.shape[0] * n, a.shape[1] // n), a.dtype)
-        if kind == "lanes":
-            return jax.ShapeDtypeStruct((a.shape[0] // n, a.shape[1] * n), a.dtype)
-        return jax.ShapeDtypeStruct(a.shape[1:], f32)
-
-    vmem = pl.BlockSpec(memory_space=pltpu.VMEM)
-    dma = pltpu.SemaphoreType.DMA
-    most = max(sizes[axis] for _, axis in ops)
-    count = len(ops)
-    return pl.pallas_call(
-        functools.partial(collect_kernel, ops=ops, sizes=sizes),
-        out_shape=[shape_of(op, a) for op, a in zip(ops, arrays)],
-        in_specs=[vmem] * count,
-        out_specs=[vmem] * count,
-        scratch_shapes=[
-            pltpu.VMEM(a.shape, a.dtype) for op, a in zip(ops, arrays) if op[0] == "sum"
-        ]
-        + [dma((count, most)), dma((count, most)), dma((count,))],
-        compiler_params=pltpu.CompilerParams(
-            collective_id=call_id, has_side_effects=True, vmem_limit_bytes=40 * 2**20
-        ),
-    )(*arrays)
-
-
-def input_kernel(heads_ref, grad_ref, w_ref, out_ref, w_s, sem):
+def input_part(heads_ref, grad_ref, w_ref, out_ref, w_s, sem):
     n_row, n_t, rows, cols = w_ref.shape
     loads = [
         pltpu.make_async_copy(
@@ -837,26 +953,116 @@
         out_ref[...] += dot(part, w_s[t], 1, 1)
 
 
-def input_gradient(grad_heads, grad_one, weights):
-    n_row, n_t, rows, cols = weights.shape
+def collect_kernel(*refs, ops, sizes, beside):
+    count = len(ops)
+    ins, refs = refs[:count], refs[count:]
+    if beside:
+        beside_ins, refs = refs[:3], refs[3:]
+    outs, refs = refs[:count], refs[count:]
+    if beside:
+        beside_out, refs = refs[0], refs[1:]
+        beside_scratch, refs = refs[-2:], refs[:-2]
+    sums = [i for i, (kind, _) in enumerate(ops) if kind == "sum"]
+    got = dict(zip(sums, refs))
+    send_sem, recv_sem, local_sem = refs[len(sums) :]
+    barrier = pltpu.get_barrier_semaphore()
+    axes = sorted({axis for _, axis in ops})
+    if "all" in axes:
+        axes = ["all"]
+    for axis in axes:
+        meet_all(barrier, axis, sizes[axis])
+    pl.semaphore_wait(barrier, sum(sizes[axis] - 1 for axis in axes))
+
+    def cut_lanes(ref, index, size):
+        lanes = ref.shape[1] // size
+        return ref.at[:, pl.ds(pl.multiple_of(index * lanes, 128), lanes)]
+
+    def cut_rows(ref, index, size):
+        rows = ref.shape[0] // size
+        return ref.at[pl.ds(pl.multiple_of(index * rows, 16), rows), :]
+
+    def cuts(i, source, target):
+        kind, axis = ops[i]
+        size = sizes[axis]
+        if kind == "rows":
+            return cut_lanes(ins[i], source, size), cut_rows(outs[i], target, size)
+        if kind == "lanes":
+            return cut_rows(ins[i], source, size), cut_lanes(outs[i], target, size)
+        return ins[i].at[source], got[i].at[target]
+
+    def copy(i, k, landing):
+        axis = ops[i][1]
+        d = lax.rem(place_on(axis) + k, sizes[axis])
+        place = d if landing is None else landing
+        source, target = cuts(i, d, place)
+        return pltpu.make_async_remote_copy(
+            source, target, send_sem.at[i, k], recv_sem.at[i, place], **on(axis, d)
+        )
+
+    def own(i):
+        z = place_on(ops[i][1])
+        return pltpu.make_async_copy(*cuts(i, z, z), local_sem.at[i])
+
+    for i, (kind, axis) in enumerate(ops):
+
+        def push(k, _):
+            copy(i, k, place_on(axis)).start()
+            return 0
+
+        lax.fori_loop(1, sizes[axis], push, 0)
+        if kind != "sum":
+            own(i).start()
+    if beside:
+        input_part(*beside_ins, beside_out, *beside_scratch)
+    for i, (kind, axis) in enumerate(ops):
+        if kind == "sum":
+            outs[i][...] = ins[i][place_on(axis)].astype(f32)
+
+        def take(k, _):
+            copy(i, k, None).wait_recv()
+            if kind == "sum":
+                outs[i][...] += got[i][lax.rem(place_on(axis) + k, sizes[axis])].astype(f32)
+            copy(i, k, None).wait_send()
+            return 0
+
+        lax.fori_loop(1, sizes[axis], take, 0)
+        if kind != "sum":
+            own(i).wait()
+
+
+def collect(ops, arrays, sizes, call_id, beside=()):
+    def shape_of(op, a):
+        kind, axis = op
+        n = sizes[axis]
+        if kind == "rows":
+            return jax.ShapeDtypeStruct((a.shape[0] * n, a.shape[1] // n), a.dtype)
+        if kind == "lanes":
+            return jax.ShapeDtypeStruct((a.shape[0] // n, a.shape[1] * n), a.dtype)
+        return jax.ShapeDtypeStruct(a.shape[1:], f32)
+
     vmem = pl.BlockSpec(memory_space=pltpu.VMEM)
+    dma = pltpu.SemaphoreType.DMA
+    most = max(sizes[axis] for _, axis in ops)
+    count = len(ops)
+    out_shape = [shape_of(op, a) for op, a in zip(ops, arrays)]
+    in_specs = [vmem] * count
+    scratch = [pltpu.VMEM(a.shape, a.dtype) for op, a in zip(ops, arrays) if op[0] == "sum"]
+    scratch += [dma((count, most)), dma((count, most)), dma((count,))]
+    if beside:
+        n_row, n_t, rows, cols = beside[2].shape
+        out_shape.append(jax.ShapeDtypeStruct(beside[1].shape, f32))
+        in_specs += [vmem, vmem, pl.BlockSpec(memory_space=pl.ANY)]
+        scratch += [pltpu.VMEM((n_t, n_row * rows, cols), bf16), dma((n_t, n_row))]
     return pl.pallas_call(
-        input_kernel,
-        out_shape=jax.ShapeDtypeStruct(grad_one.shape, f32),
-        in_specs=[vmem, vmem, pl.BlockSpec(memory_space=pl.ANY)],
-        out_specs=vmem,
-        scratch_shapes=[
-            pltpu.VMEM((n_t, n_row * rows, cols), bf16),
-            pltpu.SemaphoreType.DMA((n_t, n_row)),
-        ],
-        compiler_params=pltpu.CompilerParams(vmem_limit_bytes=32 * 2**20),
-        cost_estimate=pl.CostEstimate(
-            flops=2 * grad_heads.size * grad_one.shape[1],
-            bytes_accessed=2 * weights.size + 4 * grad_heads.size,
-            transcendentals=0,
+        functools.partial(collect_kernel, ops=ops, sizes=sizes, beside=bool(beside)),
+        out_shape=out_shape,
+        in_specs=in_specs,
+        out_specs=[vmem] * len(out_shape),
+        scratch_shapes=scratch,
+        compiler_params=pltpu.CompilerParams(
+            collective_id=call_id, has_side_effects=True, vmem_limit_bytes=40 * 2**20
         ),
-        name="input_gradient",
-    )(grad_heads, grad_one, weights)
+    )(*arrays, *beside)
 
 
 def sum_kernel(in_ref, out_ref, first, second, part, send_sem, recv_sem, local_sem, *, sizes):
@@ -902,39 +1108,138 @@
             out_ref[...] = total
 
 
-def sum_everywhere(value, n_dp, n_tensor, call_id):
+def lane_of(index):
+    return lax.broadcasted_iota(jnp.int32, (8, 128), 1) == index
+
+
+def pieces(refs, stacked):
+    out = []
+    for i, (ref, many) in enumerate(zip(refs, stacked)):
+        two = len(ref.shape) == 2
+        for k in range(ref.shape[0] if many else 1):
+            out.append((i, (slice(k, k + 1) if two else k) if many else slice(None)))
+    return out
+
+
+def direction_kernel(*refs, count, stacked):
+    ins, outs, refs = refs[: 3 * count], refs[3 * count : 5 * count], refs[5 * count :]
+    sums_ref, refs = refs[0], refs[1:]
+    held, made, in_sem, out_sem = refs[: 3 * count], refs[3 * count : 5 * count], *refs[5 * count :]
+    loads = [pltpu.make_async_copy(ins[i], held[i], in_sem.at[i]) for i in range(3 * count)]
+    for load in loads:
+        load.start()
+    stores = [pltpu.make_async_copy(made[i], outs[i], out_sem.at[i]) for i in range(2 * count)]
+    row = lax.broadcasted_iota(jnp.int32, (8, 128), 0)
+    sums = jnp.zeros((8, 128), f32)
+    done = -1
+    for index, (i, at) in enumerate(pieces(ins[:count], stacked)):
+        if i != done:
+            if done >= 0:
+                stores[done].start()
+                stores[count + done].start()
+            for k in range(3):
+                loads[k * count + i].wait()
+            done = i
+        w, g = held[i][at], held[count + i][at]
+        old = held[2 * count + i][1, at]
+        first = 0.5 * held[2 * count + i][0, at] + 0.5 * g
+        root = jnp.sqrt(0.5 * old * old + 0.5 * g * g)
+        r = first / (root + moment_eps) + decay_rate * w
+        made[i][0, at] = first
+        made[i][1, at] = root
+        made[count + i][at] = r
+        for place, value in enumerate((w, r)):
+            total = jnp.sum(jnp.sum(value * value, axis=1, keepdims=True), axis=0, keepdims=True)
+            sums = sums + jnp.where(lane_of(index) & (row == place), total, 0.0)
+    stores[done].start()
+    stores[count + done].start()
+    sums_ref[...] = sums
+    for store in stores:
+        store.wait()
+
+
+def lamb_directions(weights, grads, moments, stacked):
     vmem = pl.BlockSpec(memory_space=pltpu.VMEM)
+    hbm = pl.BlockSpec(memory_space=pl.ANY)
+    shape = jax.ShapeDtypeStruct
+    count = len(weights)
+    dma = pltpu.SemaphoreType.DMA
+    made = [*moments, *weights]
+    outs = pl.pallas_call(
+        functools.partial(direction_kernel, count=count, stacked=stacked),
+        out_shape=[shape(a.shape, f32) for a in made] + [shape((8, 128), f32)],
+        in_specs=[hbm] * (3 * count),
+        out_specs=[hbm] * (2 * count) + [vmem],
+        scratch_shapes=[pltpu.VMEM(a.shape, f32) for a in (*weights, *grads, *moments, *made)]
+        + [dma((3 * count,)), dma((2 * count,))],
+        compiler_params=pltpu.CompilerParams(vmem_limit_bytes=60 * 2**20),
+        name="lamb_directions",
+    )(*weights, *grads, *moments)
+    return outs[:count], outs[count : 2 * count], outs[2 * count]
+
+
+def update_kernel(*refs, count, stacked, sizes):
+    ins, refs = refs[: 2 * count], refs[2 * count :]
+    sums_ref, refs = refs[0], refs[1:]
+    outs, refs = refs[:count], refs[count:]
+    norms_ref, refs = refs[0], refs[1:]
+    held, made = refs[: 2 * count], refs[2 * count : 3 * count]
+    in_sem, out_sem, total, *rest = refs[3 * count :]
+    loads = [pltpu.make_async_copy(ins[i], held[i], in_sem.at[i]) for i in range(2 * count)]
+    for load in loads:
+        load.start()
+    sum_kernel(sums_ref, total, *rest, sizes=sizes)
+    norms = jnp.sqrt(total[...] + 1e-12)
+    ratios = norms[0:1] / norms[1:2]
+    row = lax.broadcasted_iota(jnp.int32, (8, 128), 0)
+    norms_ref[...] = jnp.where(row == 2, ratios, norms)
+    for load in loads:
+        load.wait()
+    for index, (i, at) in enumerate(pieces(outs, stacked)):
+        factor = jnp.sum(jnp.where(lane_of(index)[0:1], ratios, 0.0), axis=1, keepdims=True)
+        made[i][at] = held[i][at] - learn_rate * factor * held[count + i][at]
+    stores = [pltpu.make_async_copy(made[i], outs[i], out_sem.at[i]) for i in range(count)]
+    for store in stores:
+        store.start()
+    for store in stores:
+        store.wait()
+
+
+def lamb_update(weights, directions, sums, stacked, n_dp, n_tensor, call_id):
+    vmem = pl.BlockSpec(memory_space=pltpu.VMEM)
+    hbm = pl.BlockSpec(memory_space=pl.ANY)
+    shape = jax.ShapeDtypeStruct
+    count = len(weights)
     dma = pltpu.SemaphoreType.DMA
     most = max(n_dp, n_tensor)
-    return pl.pallas_call(
-        functools.partial(sum_kernel, sizes=(("dp", n_dp), ("tensor", n_tensor))),
-        out_shape=jax.ShapeDtypeStruct(value.shape, f32),
-        in_specs=[vmem],
-        out_specs=vmem,
-        scratch_shapes=[
-            pltpu.VMEM((n_dp,) + value.shape, f32),
-            pltpu.VMEM((n_tensor,) + value.shape, f32),
-            pltpu.VMEM(value.shape, f32),
+    outs = pl.pallas_call(
+        functools.partial(
+            update_kernel,
+            count=count,
+            stacked=stacked,
+            sizes=(("dp", n_dp), ("tensor", n_tensor)),
+        ),
+        out_shape=[shape(w.shape, f32) for w in weights] + [shape((8, 128), f32)],
+        in_specs=[hbm] * (2 * count) + [vmem],
+        out_specs=[hbm] * count + [vmem],
+        scratch_shapes=[pltpu.VMEM(a.shape, f32) for a in (*weights, *directions, *weights)]
+        + [
+            dma((2 * count,)),
+            dma((count,)),
+            pltpu.VMEM((8, 128), f32),
+            pltpu.VMEM((n_dp, 8, 128), f32),
+            pltpu.VMEM((n_tensor, 8, 128), f32),
+            pltpu.VMEM((8, 128), f32),
             dma((2, most)),
             dma((2, most)),
             dma((2,)),
         ],
-        compiler_params=pltpu.CompilerParams(collective_id=call_id, has_side_effects=True),
-    )(value)
-
-
-def lamb_terms(weight, gradient, moments):
-    first_moment = 0.5 * moments[0] + 0.5 * gradient
-    root_moment = jnp.sqrt(0.5 * moments[1] * moments[1] + 0.5 * gradient * gradient)
-    direction = first_moment / (root_moment + moment_eps) + decay_rate * weight
-    return (jnp.stack([first_moment, root_moment]), direction)
-
-
-def piece_sums(tensor_val, stacked):
-    squares = tensor_val * tensor_val
-    if stacked:
-        return jnp.sum(squares.reshape(squares.shape[0], -1), axis=1)
-    return jnp.sum(squares).reshape(1)
+        compiler_params=pltpu.CompilerParams(
+            collective_id=call_id, has_side_effects=True, vmem_limit_bytes=40 * 2**20
+        ),
+        name="lamb_update",
+    )(*weights, *directions, sums)
+    return outs[:count], outs[count]
 
 
 def local(
@@ -1025,9 +1330,10 @@
 
     qkv = (dot(inputs_full, attn_own, 1, 0) + qkv_bias).astype(bf16)
     out_t, lse = attention_forward(parts, qkv)
-    sizes = {"dp": n_dp, "tensor": n_tensor}
+    sizes = {"dp": n_dp, "tensor": n_tensor, "all": n_dp * n_tensor}
     (attended,) = collect([("rows", "tensor")], [out_t.reshape(head_cols, length)], sizes, 2)
-    output, grad_one, grad_attended, vector_part, grad_glu, grad_rest = feed_forward(
+    paired = n_dp == 8 and rows % 16 == 0 and n_tensor % 2 == 0
+    output, grad_one, grad_attended, vector_part, grad_all = feed_forward(
         attended,
         inputs,
         cotangent,
@@ -1035,36 +1341,40 @@
         wall,
         head_cols,
         hidden_cols,
-    )
-    if rows % 16:
-        grad_glu, grad_rest = [
-            g.reshape(n_tensor, n_dp, rows, -1).transpose(1, 0, 2, 3) for g in (grad_glu, grad_rest)
-        ]
-    glu_part = lax.psum_scatter(grad_glu, "dp", scatter_dimension=0, tiled=False)
-    rest_part = lax.psum_scatter(grad_rest, "dp", scatter_dimension=0, tiled=False)
-    vector_all = sum_everywhere(vector_part, n_dp, n_tensor, 5)[:6]
+        paired,
+        8,
+    )
     slice_width = vector_mom.shape[2]
-    vector_sum = lax.dynamic_slice_in_dim(
-        vector_all, (lax.axis_index("dp") * n_tensor + tensor_pos) * slice_width, slice_width, 1
-    )
-    grad_tokens, attn_grad, qv_grad = attention_backward(
-        parts, qkv, grad_attended, out_t, lse, inputs_full, n_tensor, 6
-    )
+    grad_tokens, attn_grad, qv_grad, late_part, vector_part = attention_backward(
+        parts, qkv, grad_attended, out_t, lse, inputs_full, grad_all, vector_part, n_tensor, paired, 6
+    )
+    if not paired:
+        if rows % 16:
+            grad_all = grad_all.reshape(n_tensor, n_dp, rows, -1).transpose(1, 0, 2, 3)
+        late_part = lax.psum_scatter(grad_all, "dp", scatter_dimension=0, tiled=False)
     qv_grad = qv_grad.reshape(head_count, 3, HEAD)
     qv_grad = jnp.stack([qv_grad[:, 0], qv_grad[:, 2]]).reshape(2, n_dp, qv_cols)
     qv_grad = jnp.pad(
         qv_grad.transpose(1, 0, 2).reshape(n_dp, 1, 2 * qv_cols),
         ((0, 0), (0, 7), (0, -2 * qv_cols % 128)),
     )
-    qv_sum, attn_part, glu_sum = collect(
-        [("sum", "dp"), ("sum", "dp"), ("sum", "tensor")],
-        [qv_grad, attn_grad.reshape(n_dp, rows, -1), glu_part],
+    vector_blocks = jnp.pad(
+        vector_part.reshape(8, n_dp, rows).transpose(1, 0, 2), ((0, 0), (0, 0), (0, -rows % 128))
+    )
+    late_sum, attn_part, qv_sum, vector_sum, input_grad = collect(
+        [("sum", "tensor"), ("sum", "dp"), ("sum", "dp"), ("sum", "dp")],
+        [late_part, attn_grad.reshape(n_dp, rows, -1), qv_grad, vector_blocks],
         sizes,
         3,
-    )
-    (rest_sum,) = collect([("sum", "tensor")], [rest_part], sizes, 4)
+        (grad_tokens, grad_one, attn_all),
+    )
+    vector_sum = lax.dynamic_slice_in_dim(
+        vector_sum[:6], tensor_pos * slice_width, slice_width, 1
+    )
+    glu_sum = late_sum[:, : 2 * hidden_cols]
+    rest_sum = late_sum[:, 2 * hidden_cols :]
     glu_sum = glu_sum.reshape(rows, 2, hidden_cols).transpose(1, 0, 2)
-    down_sum = rest_sum[:, :hidden_cols].T
+    down_sum = rest_sum[:, :hidden_cols]
     out_sum = rest_sum[:, hidden_cols : hidden_cols + head_cols].T
     attn_sum = (
         attn_part.reshape(rows, head_count, 3, HEAD)
@@ -1073,36 +1383,21 @@
     )
     qv_sum = qv_sum[0, : 2 * qv_cols].reshape(2, qv_cols)
 
-    input_grad = input_gradient(grad_tokens, grad_one, attn_all)
-
     vector_own = lax.dynamic_slice_in_dim(vectors, tensor_pos * slice_width, slice_width, 1)
-    owned_parts = (attn_w, out_w, glu_w, down_w, qv_bias, vector_own)
+    owned_parts = (attn_w, out_w, glu_w, down_w.T, qv_bias, vector_own)
     gradients = (attn_sum, out_sum, glu_sum, down_sum, qv_sum, vector_sum)
-    moments = (attn_mom, out_mom, glu_mom, down_mom, qv_mom, vector_mom)
+    moments = (attn_mom, out_mom, glu_mom, down_mom.swapaxes(1, 2), qv_mom, vector_mom)
     stack_flags = (True, False, True, False, True, True)
-    new_moments = []
-    directions = []
-    for weight, gradient, moment in zip(owned_parts, gradients, moments):
-        pair, direction = lamb_terms(weight, gradient, moment)
-        new_moments.append(pair)
-        directions.append(direction)
-    weight_sums = jnp.concatenate([piece_sums(w, f) for w, f in zip(owned_parts, stack_flags)])
-    dir_sums = jnp.concatenate([piece_sums(r, f) for r, f in zip(directions, stack_flags)])
-    totals = jnp.pad(jnp.stack([weight_sums, dir_sums]), ((0, 6), (0, 113)))
-    totals = sum_everywhere(totals, n_dp, n_tensor, 9)[:2, :15]
-    norm_values = jnp.sqrt(totals + 1e-12)
-    ratios = norm_values[0] / norm_values[1]
-    new_weights = []
-    offset = 0
-    for weight, direction, stacked in zip(owned_parts, directions, stack_flags):
-        amount = weight.shape[0] if stacked else 1
-        factor = ratios[offset : offset + amount]
-        if stacked:
-            factor = factor.reshape((amount,) + (1,) * (weight.ndim - 1))
-        else:
-            factor = factor[0]
-        new_weights.append(weight - learn_rate * factor * direction)
-        offset = offset + amount
+    new_moments, directions, sums = lamb_directions(owned_parts, gradients, moments, stack_flags)
+    new_weights, norms = lamb_update(
+        owned_parts, directions, sums, stack_flags, n_dp, n_tensor, 9
+    )
+    gradients, new_moments, new_weights = [
+        (*group[:3], group[3].swapaxes(-1, -2), *group[4:])
+        for group in (gradients, new_moments, new_weights)
+    ]
+    norm_values = norms[:2, :15]
+    ratios = norms[2, :15]
     return (
         output,
         input_grad,

time: 443 us -> 419 us (0.946)
  other arithmetic: 32.7 us -> 5.9 us
  local copies, waits for them, and re-layouts: 26.3 us -> 41.4 us
  Pallas kernels: 356 us -> 344 us
    pallas_call x6 -> x4, Pallas kernels: 103 us -> 83 us  [the longest x2 58.2 us: collect(): pl.pallas_call(functools.partial(collect_kernel, ops=ops, sizes=sizes, be...]
    reduce_sum x11 -> x0, other arithmetic: 12 us -> none  [the longest x7 7.47 us: piece_sums(): return jnp.sum(squares.reshape(squares.shape[0], -1), axis=1)]
    unnamed x91 -> x69, local copies, waits for them, and re-layouts: 17.4 us -> 28.4 us
    pallas_call x1, Pallas kernels: 45.9 us -> 55.2 us  [feed_forward(): pl.pallas_call(functools.partial(ff_kernel, head_cols=head_cols, hid_cols...]
    sub x6 -> x0, other arithmetic: 6.93 us -> none  [local(): new_weights.append(weight - learn_rate * factor * direction)]
    another operation x10 -> x0, other arithmetic: 6.21 us -> none  [the longest x9 5.6 us: lamb_terms(): return (jnp.stack([first_moment, root_moment]), direction)]
  transfers between devices with their start and end apart: 4 -> 2, of which waited for: 0 -> 0; matrix products, arithmetic and copies ran while one was open for 4% -> 3% of each run, Pallas kernels for 62% -> 57%
where the time goes in v4:
time: 419 us; the launch traced here: 412 us
  Pallas kernels  344 us (82%)
  local copies, waits for them, and re-layouts  41.4 us (10%)
  between operations  14.7 us (4%)
  matrix products  5.96 us (1%)
  other arithmetic  5.9 us (1%)
    pallas_call x2, Pallas kernels, gather_blocks(): pl.pallas_call(functools.partial(gather_kernel, n_chain=len(on_chain), n_...  96.7 us
    pallas_call x1, Pallas kernels, attention_backward(): pl.pallas_call(functools.partial(bwd_kernel, heads=heads, length=length,...  83.6 us
    pallas_call x2, Pallas kernels, collect(): pl.pallas_call(functools.partial(collect_kernel, ops=ops, sizes=sizes, be...  58.2 us
    pallas_call x1, Pallas kernels, feed_forward(): pl.pallas_call(functools.partial(ff_kernel, head_cols=head_cols, hid_cols...  55.2 us
    unnamed x69, local copies, waits for them, and re-layouts  28.4 us
    pallas_call x1, Pallas kernels, attention_forward(): pl.pallas_call(functools.partial(fwd_kernel, heads=heads, length=length,...  25.6 us
    pallas_call x1, Pallas kernels, lamb_update(): pl.pallas_call(functools.partial(update_kernel, count=count, stacked=stac...  19.7 us
  transfers between devices with their start and end apart: 2, of which 0 were waited for; matrix products, arithmetic and copies ran while one was open for 3% of the time, Pallas kernels for 57%

profile of v4, /device:TPU:0, one launch (start us, length us, event | category | flops | bytes accessed | tf_op | source)
XLA Modules:
  0.0 412.1 jit_solution(17213240936838761523)
XLA Ops:
  7.3 1.2 copy.95
  8.6 0.7 convert_element_type.49
  9.4 0.7 convert_element_type.50
  10.3 1.1 convert_bitcast_fusion
  11.7 0.8 fusion.2.refs_0_
  12.5 0.7 maximum_maximum_fusion.refs_1_
  13.2 43.6 %shard_map.318 = (bf16[4,96,2560]{2,1,0:T(8,128)(2,1)}, bf16[8,96,640]{2,1,0:T(8,128)(2,1)}) custom-call(bf16[96,2560]{1,0:T(8,128)(2,1)} %fusion.2.refs_0_, bf16[96,640]{1,0:T(8,128)(2,1)} %maximum_maximum_fusion.refs_1_), custom_call_target="tpu_custom_call" | custom-call | tf_op jit(solution)/shard_map/pallas_call | solution.py:919
  57.0 0.8 copy.107
  57.8 1.2 slice_reduce_fusion
  58.9 0.6 copy.102
  60.3 53.0 %shard_map.319 = bf16[4,512,768]{2,1,0:T(8,128)(2,1)} custom-call(bf16[512,768]{1,0:T(8,128)(2,1)} %x_ref.1), custom_call_target="tpu_custom_call" | custom-call | tf_op jit(solution)/shard_map/pallas_call | solution.py:919
  113.3 6.0 %add_convert_fusion.qkv_ref = bf16[2048,576]{1,0:T(8,128)(2,1)} fusion(bf16[2048,768]{1,0:T(8,128)(2,1)} %bitcast.65, f32[576]{0:T(1024)S(1)} %add.30, bf16[768,640]{1,0:T(8,128)(2,1)S(1)} %bitcast.72), kind=kOutput, calls=%fused_computation | convolution fusion | flops 1814298624 | bytes 6490368 | tf_op jit(solution)/shard_map/dot_general | solution.py:28
  119.3 0.7 constant_dynamic-slice_fusion.2.parts_ref
  120.0 1.7 copy-done.23
  121.7 25.6 %attention_forward.1 = (bf16[3,64,2048]{2,1,0:T(8,128)(2,1)S(1)}, f32[3,1,2048]{2,1,0:T(1,128)S(1)}) custom-call(f32[3,3]{1,0:T(4,128)S(1)} %constant_dynamic-slice_fusion.2.parts_ref, bf16[2048,576]{1,0:T(8,128)(2,1)S(1)} %copy-done.23), custom_call_target="tpu_custom_call" | custom-call | flops 12884901888 | bytes 4718592 | tf_op jit(solution)/shard_map/attention_forward/pallas_call | solution.py:121
  148.0 17.5 %shard_map.320.att_ref = bf16[768,512]{1,0:T(8,128)(2,1)S(1)} custom-call(bf16[192,2048]{1,0:T(8,128)(2,1)S(1)} %bitcast.62), custom_call_target="tpu_custom_call" | custom-call | tf_op jit(solution)/shard_map/pallas_call | solution.py:1056
  165.5 0.9 copy-done.12
  167.6 55.2 %feed_forward.1 = (bf16[512,768]{1,0:T(8,128)(2,1)}, f32[512,768]{1,0:T(8,128)}, bf16[768,512]{1,0:T(8,128)(2,1)}, f32[8,768]{1,0:T(8,128)}, bf16[4,4,96,2560]{3,2,1,0:T(8,128)(2,1)}) custom-call(bf16[768,512]{1,0:T(8,128)(2,1)} %copy-done.12, bf16[512,768]{1,0:T(8,128)(2,1)} %x_ref.1, bf16[512,768]{1,0:T(8,128)(2,1)} %cot_ref.1, ...), custom_call_target="tpu_custom_call" | custom-call | flops 23555211264 | bytes 31457280 | tf_op jit(solution)/shard_map/feed_forward/pallas_call | solution.py:748
  222.8 83.6 %attention_backward.1 = (bf16[2304,512]{1,0:T(8,128)(2,1)}, bf16[768,576]{1,0:T(8,128)(2,1)}, f32[3,192,1]{2,1,0:T(8,128)}, bf16[4,96,2560]{2,1,0:T(8,128)(2,1)}, f32[8,768]{1,0:T(8,128)}) custom-call(f32[3,3]{1,0:T(4,128)} %copy-done.21, bf16[2048,576]{1,0:T(8,128)(2,1)} %add_convert_fusion.qkv_ref, bf16[768,512]{1,0:T(8,128)(2,1)} %get-tuple-element.69.own_ref, ...), custom_call_target="tpu_custom_call" | custom-call | flops 32212254720 | bytes 9437184 | tf_op jit(solution)/shard_map/attention_backward/pallas_call | solution.py:451
  306.4 0.8 reshape.120
  307.2 1.1 reduce.3
  308.8 2.1 copy-done.1
  310.9 1.7 copy-done.5
  312.6 1.5 copy-done.6
  314.1 1.4 copy-done.7
  315.6 1.2 copy-done.8
  316.8 40.7 %shard_map.321 = (f32[96,2560]{1,0:T(8,128)S(1)}, f32[96,576]{1,0:T(8,128)S(1)}, f32[8,128]{1,0:T(8,128)S(1)}, f32[8,128]{1,0:T(8,128)S(1)}, f32[512,768]{1,0:T(8,128)S(1)}) custom-call(bf16[4,96,2560]{2,1,0:T(8,128)(2,1)S(1)} %copy-done.6, bf16[8,96,576]{2,1,0:T(8,128)(2,1)S(1)} %bitcast.61, f32[8,8,128]{2,1,0:T(8,128)S(1)} %pad.26.refs_2_, ...), custom_call_target="tpu_custom_call" | custom-call | tf_op jit(solution)/shard_map/pallas_call | solution.py:1056
  357.5 1.5 copy.110
  359.0 0.9 fusion.3
  359.8 1.5 slice_bitcast_fusion.refs_7_
  361.4 0.9 copy.121
  362.4 0.9 copy.114.refs_6_
  364.0 0.7 constant_dynamic-slice_fusion
  364.6 5.2 %lamb_directions.1 = (f32[2,3,96,192]{3,2,1,0:T(8,128)}, f32[2,192,96]{2,1,0:T(8,128)}, f32[2,2,96,768]{3,2,1,0:T(8,128)}, f32[2,96,768]{2,1,0:T(8,128)}, f32[2,...) custom-call(f32[3,96,192]{2,1,0:T(8,128)} %refs_0_.4, ...), custom_call_target="tpu_custom_call" | custom-call | tf_op jit(solution)/shard_map/lamb_directions/pallas_call | solution.py:1168
  369.9 1.1 copy-done.13
  370.9 1.0 copy-done.14
  371.9 1.0 copy-done.15
  372.8 0.9 copy-done.16
  373.7 0.7 copy-done.18
  374.4 0.7 copy-done.19
  375.1 0.7 copy-done.22
  375.8 19.7 %lamb_update.1 = (f32[3,96,192]{2,1,0:T(8,128)S(1)}, f32[192,96]{1,0:T(8,128)S(1)}, f32[2,96,768]{2,1,0:T(8,128)S(1)}, f32[96,768]{1,0:T(8,128)S(1)}, f32[2,24]{...) custom-call(f32[3,96,192]{2,1,0:T(8,128)S(1)} %copy-done.4, f32[192,96]{1,0:T(8,128)S(1)} %copy-done.10, ...), custom_call_target="tpu_custom_call" | custom-call | tf_op jit(solution)/shard_map/lamb_update/pallas_call | solution.py:1215
  396.5 1.3 copy.115
  397.8 2.1 copy.131
  399.9 1.1 copy.132
  401.0 0.7 copy.133
  402.4 0.8 copy.135
  403.2 0.7 copy.136
  (92 shorter events, 7.6 us)
Async XLA Ops:
  7.2 4.3 %copy-start.2 = (f32[768,96]{0,1:T(8,128)S(1)}, f32[768,96]{0,1:T(8,128)}, u32[]{:S(2)}) copy-start(f32[768,96]{0,1:T(8,128)} %param.20) | copy-start | bytes 884740
  7.2 4.3 %copy-start.9 = (f32[192,96]{1,0:T(8,128)S(1)}, f32[192,96]{1,0:T(8,128)}, u32[]{:S(2)}) copy-start(f32[192,96]{1,0:T(8,128)} %refs_1_.3) | copy-start | bytes 221188
  7.2 160.4 %all-gather.6.cloned.1.call-start = ((), (), s32[]{:S(2)}) async-start(), calls=%async_computation.1 | async-start | bytes 17694720 | tf_op jit(solution)/shard_map/all_gather | solution.py:1305
  56.9 2.1 copy-start.25
  56.9 251.9 %all-gather.4.cloned.1.call-start = ((), (), s32[]{:S(2)}) async-start(), calls=%async_computation | async-start | bytes 4055040 | tf_op jit(solution)/shard_map/all_gather | solution.py:1306
  120.0 1.7 copy-start.23
  121.7 25.6 %copy-start.21 = (f32[3,3]{1,0:T(4,128)}, f32[3,3]{1,0:T(4,128)S(1)}, u32[]{:S(2)}) copy-start(f32[3,3]{1,0:T(4,128)S(1)} %constant_dynamic-slice_fusion.2.parts_ref) | copy-start | bytes 112
  121.7 44.7 %copy-start.27 = (f32[2,6,24]{2,0,1:T(2,128)S(1)}, f32[2,6,24]{2,0,1:T(2,128)}, u32[]{:S(2)}) copy-start(f32[2,6,24]{2,0,1:T(2,128)} %param.28) | copy-start | bytes 3460
  147.4 0.6 copy-start.24
  148.0 74.8 %copy-start.11 = (bf16[3,64,2048]{2,1,0:T(8,128)(2,1)}, bf16[3,64,2048]{2,1,0:T(8,128)(2,1)S(1)}, u32[]{:S(2)}) copy-start(bf16[3,64,2048]{2,1,0:T(8,128)(2,1)S(1)} %get-tuple-element.66.ot_ref) | copy-start | bytes 2359300
  165.5 0.9 copy-start.12
  308.8 2.1 copy-start.1
  310.9 1.7 copy-start.5
  312.6 1.5 copy-start.6
  314.1 1.4 copy-start.7
  315.6 1.2 copy-start.8
  358.9 5.0 %copy-start.26 = (f32[6,96]{1,0:T(8,128)S(1)}, f32[6,96]{1,0:T(8,128)}, u32[]{:S(2)}) copy-start(f32[6,96]{1,0:T(8,128)} %param.22) | copy-start | bytes 6916
  363.3 6.5 %copy-start = (f32[2,96,768]{2,1,0:T(8,128)S(1)}, f32[2,96,768]{2,1,0:T(8,128)}, u32[]{:S(2)}) copy-start(f32[2,96,768]{2,1,0:T(8,128)} %refs_2_.3) | copy-start | bytes 1769476
  363.3 6.5 %copy-start.3 = (f32[768,96]{0,1:T(8,128)S(1)}, f32[768,96]{0,1:T(8,128)}, u32[]{:S(2)}) copy-start(f32[768,96]{0,1:T(8,128)} %param.20) | copy-start | bytes 884740
  363.3 6.5 %copy-start.4 = (f32[3,96,192]{2,1,0:T(8,128)S(1)}, f32[3,96,192]{2,1,0:T(8,128)}, u32[]{:S(2)}) copy-start(f32[3,96,192]{2,1,0:T(8,128)} %refs_0_.4) | copy-start | bytes 663556
  363.3 6.5 %copy-start.10 = (f32[192,96]{1,0:T(8,128)S(1)}, f32[192,96]{1,0:T(8,128)}, u32[]{:S(2)}) copy-start(f32[192,96]{1,0:T(8,128)} %refs_1_.3) | copy-start | bytes 221188
  363.3 6.6 %copy-start.20 = (f32[2,24]{1,0:T(2,128)S(1)}, f32[2,24]{1,0:T(2,128)}, u32[]{:S(2)}) copy-start(f32[2,24]{1,0:T(2,128)} %refs_4_.3) | copy-start | bytes 580
  364.6 5.2 %copy-start.17 = (f32[6,24]{1,0:T(8,128)S(1)}, f32[6,24]{1,0:T(8,128)}, u32[]{:S(2)}) copy-start(f32[6,24]{1,0:T(8,128)} %get-tuple-element.198.refs_5_) | copy-start | bytes 1732
  369.8 1.1 copy-start.13
  370.9 1.0 copy-start.14
  371.9 1.0 copy-start.15
  372.8 0.9 copy-start.16
  373.7 0.7 copy-start.18
  374.4 0.7 copy-start.19
  375.1 0.7 copy-start.22
Sparse Core Ops, SparseCore 0:
  57.0 81.6 all-gather.5
  142.1 64.6 all-gather.3

commit v5 on v4

--- a/solution.py
+++ b/solution.py
@@ -115,7 +115,7 @@
 def attention_forward(parts, qkv):
     length = qkv.shape[0]
     heads = qkv.shape[1] // (3 * HEAD)
-    unroll = 2
+    unroll = 4
     vmem = pl.BlockSpec(memory_space=pltpu.VMEM)
     work = heads * length * length
     return pl.pallas_call(
@@ -1303,13 +1303,8 @@
     (inputs_full,) = gather_blocks([first_inputs], [], n_tensor, n_dp, 1)
     inputs_full = inputs_full.reshape(length, width)
     wall = lax.all_gather(wall_chain, "dp")
-    attn_all = lax.all_gather(attn_rows, ("dp", "tensor")).reshape(
-        n_dp, n_tensor, rows, -1
-    )
     if rows % 16:
-        wall, attn_all = [
-            w.transpose(1, 0, 2, 3).reshape(1, n_tensor, width, -1) for w in (wall, attn_all)
-        ]
+        wall = wall.transpose(1, 0, 2, 3).reshape(1, n_tensor, width, -1)
 
     attn_own = own[:, : 3 * head_cols]
     vector_rows = own[:, 3 * head_cols : 3 * head_cols + 6].T.astype(f32)
@@ -1332,6 +1327,12 @@
     out_t, lse = attention_forward(parts, qkv)
     sizes = {"dp": n_dp, "tensor": n_tensor, "all": n_dp * n_tensor}
     (attended,) = collect([("rows", "tensor")], [out_t.reshape(head_cols, length)], sizes, 2)
+    attended, attn_rows = lax.optimization_barrier((attended, attn_rows))
+    attn_all = lax.all_gather(attn_rows, ("dp", "tensor")).reshape(
+        n_dp, n_tensor, rows, -1
+    )
+    if rows % 16:
+        attn_all = attn_all.transpose(1, 0, 2, 3).reshape(1, n_tensor, width, -1)
     paired = n_dp == 8 and rows % 16 == 0 and n_tensor % 2 == 0
     output, grad_one, grad_attended, vector_part, grad_all = feed_forward(
         attended,

time: 419 us -> 412 us (0.983)
  no operation moved by 1% of the time
where the time goes in v5:
time: 412 us; the launch traced here: 406 us
  Pallas kernels  341 us (83%)
  local copies, waits for them, and re-layouts  39.7 us (10%)
  between operations  14.7 us (4%)
  other arithmetic  5.91 us (1%)
  matrix products  4.51 us (1%)
    pallas_call x2, Pallas kernels, gather_blocks(): pl.pallas_call(functools.partial(gather_kernel, n_chain=len(on_chain), n_...  96.7 us
    pallas_call x1, Pallas kernels, attention_backward(): pl.pallas_call(functools.partial(bwd_kernel, heads=heads, length=length,...  82.9 us
    pallas_call x2, Pallas kernels, collect(): pl.pallas_call(functools.partial(collect_kernel, ops=ops, sizes=sizes, be...  56.7 us
    pallas_call x1, Pallas kernels, feed_forward(): pl.pallas_call(functools.partial(ff_kernel, head_cols=head_cols, hid_cols...  56.1 us
    unnamed x69, local copies, waits for them, and re-layouts  26.6 us
    pallas_call x1, Pallas kernels, attention_forward(): pl.pallas_call(functools.partial(fwd_kernel, heads=heads, length=length,...  23.8 us
    pallas_call x1, Pallas kernels, lamb_update(): pl.pallas_call(functools.partial(update_kernel, count=count, stacked=stac...  19.6 us
  transfers between devices with their start and end apart: 2, of which 0 were waited for; matrix products, arithmetic and copies ran while one was open for 3% of the time, Pallas kernels for 57%

profile of v5, /device:TPU:0, one launch (start us, length us, event | category | flops | bytes accessed | tf_op | source)
XLA Modules:
  0.0 405.8 jit_solution(14753972007443303141)
XLA Ops:
  7.3 1.2 copy.93
  8.6 0.7 convert_element_type.49
  9.4 0.7 convert_element_type.50
  10.3 1.1 convert_bitcast_fusion
  11.7 0.8 fusion.2.refs_0_
  12.5 0.7 maximum_maximum_fusion.refs_1_
  13.2 43.6 %shard_map.318 = (bf16[4,96,2560]{2,1,0:T(8,128)(2,1)}, bf16[8,96,640]{2,1,0:T(8,128)(2,1)}) custom-call(bf16[96,2560]{1,0:T(8,128)(2,1)} %fusion.2.refs_0_, bf16[96,640]{1,0:T(8,128)(2,1)} %maximum_maximum_fusion.refs_1_), custom_call_target="tpu_custom_call" | custom-call | tf_op jit(solution)/shard_map/pallas_call | solution.py:919
  57.0 1.2 slice_reduce_fusion
  58.9 53.0 %shard_map.319 = bf16[4,512,768]{2,1,0:T(8,128)(2,1)} custom-call(bf16[512,768]{1,0:T(8,128)(2,1)} %x_ref.1), custom_call_target="tpu_custom_call" | custom-call | tf_op jit(solution)/shard_map/pallas_call | solution.py:919
  111.9 0.7 constant_dynamic-slice_fusion.2.parts_ref
  112.7 4.5 %add_convert_fusion.qkv_ref = bf16[2048,576]{1,0:T(8,128)(2,1)S(1)} fusion(bf16[2048,768]{1,0:T(8,128)(2,1)} %bitcast.64, f32[576]{0:T(1024)S(1)} %add.30, bf16[768,640]{1,0:T(8,128)(2,1)S(1)} %bitcast.70), kind=kOutput, calls=%fused_computation | convolution fusion | flops 1814298624 | bytes 6490368 | tf_op jit(solution)/shard_map/dot_general | solution.py:28
  117.2 23.8 %attention_forward.1 = (bf16[3,64,2048]{2,1,0:T(8,128)(2,1)S(1)}, f32[3,1,2048]{2,1,0:T(1,128)S(1)}) custom-call(f32[3,3]{1,0:T(4,128)S(1)} %constant_dynamic-slice_fusion.2.parts_ref, bf16[2048,576]{1,0:T(8,128)(2,1)S(1)} %add_convert_fusion.qkv_ref), custom_call_target="tpu_custom_call" | custom-call | flops 12884901888 | bytes 4718592 | tf_op jit(solution)/shard_map/attention_forward/pallas_call | solution.py:121
  141.6 15.0 %shard_map.320.att_ref = bf16[768,512]{1,0:T(8,128)(2,1)S(1)} custom-call(bf16[192,2048]{1,0:T(8,128)(2,1)S(1)} %bitcast.61), custom_call_target="tpu_custom_call" | custom-call | tf_op jit(solution)/shard_map/pallas_call | solution.py:1056
  156.6 0.9 copy-done.12
  157.5 0.8 copy.104
  158.3 0.6 copy.100
  160.2 56.1 %feed_forward.1 = (bf16[512,768]{1,0:T(8,128)(2,1)}, f32[512,768]{1,0:T(8,128)}, bf16[768,512]{1,0:T(8,128)(2,1)}, f32[8,768]{1,0:T(8,128)}, bf16[4,4,96,2560]{3,2,1,0:T(8,128)(2,1)}) custom-call(bf16[768,512]{1,0:T(8,128)(2,1)} %copy-done.12, bf16[512,768]{1,0:T(8,128)(2,1)} %x_ref.1, bf16[512,768]{1,0:T(8,128)(2,1)} %cot_ref.1, ...), custom_call_target="tpu_custom_call" | custom-call | flops 23555211264 | bytes 31457280 | tf_op jit(solution)/shard_map/feed_forward/pallas_call | solution.py:748
  216.3 82.9 %attention_backward.1 = (bf16[2304,512]{1,0:T(8,128)(2,1)}, bf16[768,576]{1,0:T(8,128)(2,1)}, f32[3,192,1]{2,1,0:T(8,128)}, bf16[4,96,2560]{2,1,0:T(8,128)(2,1)}, f32[8,768]{1,0:T(8,128)}) custom-call(f32[3,3]{1,0:T(4,128)} %copy-done.21, bf16[2048,576]{1,0:T(8,128)(2,1)} %copy-done.23, bf16[768,512]{1,0:T(8,128)(2,1)} %get-tuple-element.72.own_ref, ...), custom_call_target="tpu_custom_call" | custom-call | flops 32212254720 | bytes 9437184 | tf_op jit(solution)/shard_map/attention_backward/pallas_call | solution.py:451
  299.2 0.8 reshape.120
  300.1 1.1 reduce.3
  301.7 2.1 copy-done.1
  303.8 1.7 copy-done.5
  305.4 1.5 copy-done.6
  307.0 1.4 copy-done.7
  308.4 1.2 copy-done.8
  309.6 41.7 %shard_map.321 = (f32[96,2560]{1,0:T(8,128)S(1)}, f32[96,576]{1,0:T(8,128)S(1)}, f32[8,128]{1,0:T(8,128)S(1)}, f32[8,128]{1,0:T(8,128)S(1)}, f32[512,768]{1,0:T(8,128)S(1)}) custom-call(bf16[4,96,2560]{2,1,0:T(8,128)(2,1)S(1)} %copy-done.6, bf16[8,96,576]{2,1,0:T(8,128)(2,1)S(1)} %bitcast.60, f32[8,8,128]{2,1,0:T(8,128)S(1)} %pad.26.refs_2_, ...), custom_call_target="tpu_custom_call" | custom-call | tf_op jit(solution)/shard_map/pallas_call | solution.py:1056
  351.3 1.5 copy.107
  352.8 0.9 fusion.3
  353.6 1.5 slice_bitcast_fusion.refs_7_
  355.2 0.9 copy.118
  356.2 0.9 copy.111.refs_6_
  357.1 0.6 reshape_squeeze.7.refs_10_
  357.8 0.7 constant_dynamic-slice_fusion
  358.5 5.2 %lamb_directions.1 = (f32[2,3,96,192]{3,2,1,0:T(8,128)}, f32[2,192,96]{2,1,0:T(8,128)}, f32[2,2,96,768]{3,2,1,0:T(8,128)}, f32[2,96,768]{2,1,0:T(8,128)}, f32[2,...) custom-call(f32[3,96,192]{2,1,0:T(8,128)} %refs_0_.4, ...), custom_call_target="tpu_custom_call" | custom-call | tf_op jit(solution)/shard_map/lamb_directions/pallas_call | solution.py:1168
  363.7 1.1 copy-done.13
  364.7 1.0 copy-done.14
  365.7 1.0 copy-done.15
  366.7 0.9 copy-done.16
  367.6 0.7 copy-done.18
  368.3 0.7 copy-done.19
  368.9 0.7 copy-done.22
  369.6 19.6 %lamb_update.1 = (f32[3,96,192]{2,1,0:T(8,128)S(1)}, f32[192,96]{1,0:T(8,128)S(1)}, f32[2,96,768]{2,1,0:T(8,128)S(1)}, f32[96,768]{1,0:T(8,128)S(1)}, f32[2,24]{...) custom-call(f32[3,96,192]{2,1,0:T(8,128)S(1)} %copy-done.4, f32[192,96]{1,0:T(8,128)S(1)} %copy-done.10, ...), custom_call_target="tpu_custom_call" | custom-call | tf_op jit(solution)/shard_map/lamb_update/pallas_call | solution.py:1215
  390.2 1.3 copy.112
  391.5 2.1 copy.128
  393.6 1.1 copy.129
  394.7 0.7 copy.130
  396.1 0.8 copy.132
  396.9 0.7 copy.133
  (92 shorter events, 7.0 us)
Async XLA Ops:
  7.2 4.3 %copy-start.2 = (f32[768,96]{0,1:T(8,128)S(1)}, f32[768,96]{0,1:T(8,128)}, u32[]{:S(2)}) copy-start(f32[768,96]{0,1:T(8,128)} %param.20) | copy-start | bytes 884740
  7.2 4.3 %copy-start.9 = (f32[192,96]{1,0:T(8,128)S(1)}, f32[192,96]{1,0:T(8,128)}, u32[]{:S(2)}) copy-start(f32[192,96]{1,0:T(8,128)} %refs_1_.3) | copy-start | bytes 221188
  7.2 153.0 %all-gather.5.cloned.1.call-start = ((), (), s32[]{:S(2)}) async-start(), calls=%async_computation | async-start | bytes 17694720 | tf_op jit(solution)/shard_map/all_gather | solution.py:1305
  56.9 55.8 %copy-start.25 = (bf16[8,96,640]{2,1,0:T(8,128)(2,1)S(1)}, bf16[8,96,640]{2,1,0:T(8,128)(2,1)}, u32[]{:S(2)}) copy-start(bf16[8,96,640]{2,1,0:T(8,128)(2,1)} %get-tuple-element.65) | copy-start | bytes 2949124
  56.9 244.7 %all-gather.7.cloned.1.call-start = ((), (), s32[]{:S(2)}) async-start(), calls=%async_computation.1 | async-start | bytes 4055040 | tf_op jit(solution)/shard_map/all_gather | solution.py:1331
  112.6 4.5 %copy-start.21 = (f32[3,3]{1,0:T(4,128)}, f32[3,3]{1,0:T(4,128)S(1)}, u32[]{:S(2)}) copy-start(f32[3,3]{1,0:T(4,128)S(1)} %constant_dynamic-slice_fusion.2.parts_ref) | copy-start | bytes 112
  117.2 23.9 %copy-start.23 = (bf16[2048,576]{1,0:T(8,128)(2,1)}, bf16[2048,576]{1,0:T(8,128)(2,1)S(1)}, u32[]{:S(2)}) copy-start(bf16[2048,576]{1,0:T(8,128)(2,1)S(1)} %add_convert_fusion.qkv_ref) | copy-start | bytes 7077892
  141.0 0.6 copy-start.24
  141.6 74.6 %copy-start.11 = (bf16[3,64,2048]{2,1,0:T(8,128)(2,1)}, bf16[3,64,2048]{2,1,0:T(8,128)(2,1)S(1)}, u32[]{:S(2)}) copy-start(bf16[3,64,2048]{2,1,0:T(8,128)(2,1)S(1)} %get-tuple-element.68.ot_ref) | copy-start | bytes 2359300
  141.6 17.3 %copy-start.27 = (f32[2,6,24]{2,0,1:T(2,128)S(1)}, f32[2,6,24]{2,0,1:T(2,128)}, u32[]{:S(2)}) copy-start(f32[2,6,24]{2,0,1:T(2,128)} %param.28) | copy-start | bytes 3460
  156.6 0.9 copy-start.12
  301.6 2.1 copy-start.1
  303.8 1.7 copy-start.5
  305.4 1.5 copy-start.6
  307.0 1.4 copy-start.7
  308.4 1.2 copy-start.8
  352.8 5.0 %copy-start.26 = (f32[6,96]{1,0:T(8,128)S(1)}, f32[6,96]{1,0:T(8,128)}, u32[]{:S(2)}) copy-start(f32[6,96]{1,0:T(8,128)} %param.22) | copy-start | bytes 6916
  357.1 6.5 %copy-start = (f32[2,96,768]{2,1,0:T(8,128)S(1)}, f32[2,96,768]{2,1,0:T(8,128)}, u32[]{:S(2)}) copy-start(f32[2,96,768]{2,1,0:T(8,128)} %refs_2_.3) | copy-start | bytes 1769476
  357.1 6.5 %copy-start.3 = (f32[768,96]{0,1:T(8,128)S(1)}, f32[768,96]{0,1:T(8,128)}, u32[]{:S(2)}) copy-start(f32[768,96]{0,1:T(8,128)} %param.20) | copy-start | bytes 884740
  357.1 6.5 %copy-start.4 = (f32[3,96,192]{2,1,0:T(8,128)S(1)}, f32[3,96,192]{2,1,0:T(8,128)}, u32[]{:S(2)}) copy-start(f32[3,96,192]{2,1,0:T(8,128)} %refs_0_.4) | copy-start | bytes 663556
  357.1 6.5 %copy-start.10 = (f32[192,96]{1,0:T(8,128)S(1)}, f32[192,96]{1,0:T(8,128)}, u32[]{:S(2)}) copy-start(f32[192,96]{1,0:T(8,128)} %refs_1_.3) | copy-start | bytes 221188
  357.1 6.6 %copy-start.20 = (f32[2,24]{1,0:T(2,128)S(1)}, f32[2,24]{1,0:T(2,128)}, u32[]{:S(2)}) copy-start(f32[2,24]{1,0:T(2,128)} %refs_4_.3) | copy-start | bytes 580
  358.5 5.2 %copy-start.17 = (f32[6,24]{1,0:T(8,128)S(1)}, f32[6,24]{1,0:T(8,128)}, u32[]{:S(2)}) copy-start(f32[6,24]{1,0:T(8,128)} %get-tuple-element.202.refs_5_) | copy-start | bytes 1732
  363.7 1.1 copy-start.13
  364.7 1.0 copy-start.14
  365.7 1.0 copy-start.15
  366.7 0.9 copy-start.16
  367.6 0.7 copy-start.18
  368.2 0.7 copy-start.19
  368.9 0.7 copy-start.22
Sparse Core Ops, SparseCore 0:
  57.0 81.6 all-gather.4
  158.4 61.5 all-gather.6
